TPU v7x, 128 devices: a whole 4x4x4 slice. The times are simulated.
128 devices in a mesh: batch: 1, seq: 128 (over z, y, x, core).
Axes of the slice: x: 4, y: 4, z: 4, core: 2. Of those that a mesh axis runs over, the one named last changes fastest.
Arguments:
- tokens: bfloat16 [32768, 2048], P(('batch', 'seq'))
- w_query: bfloat16 [2048, 2048], replicated
- w_key: bfloat16 [2048, 2048], replicated
- w_value: bfloat16 [2048, 2048], replicated
- w_out: bfloat16 [2048, 2048], replicated
- rand_idx: int32 [512, 3], P(('batch', 'seq'))
Outputs:
- output: bfloat16 [32768, 2048], P(('batch', 'seq'))
All inputs are finite; a program needn't handle non-finite values.
Results may differ from a plain program's by a relative error of at most 0.00340356.
Values are sent between devices in bfloat16 or wider.
A program may use at most 1 GiB of HBM per device.

v0:
```python
import jax
import jax.numpy as jnp
from jax import lax
from jax.sharding import PartitionSpec as P

HEAD_DIM = 64
GLOBAL_BLOCKS = 2
HOT_PER_RAND = 4
NEG_BIG = -1e30


def block_attention(query_blk, key_rows, val_rows, key_mask):
    n_query, row_width = query_blk.shape
    n_heads = row_width // HEAD_DIM
    q_heads = query_blk.reshape(n_query, n_heads, HEAD_DIM)
    k_heads = key_rows.reshape(-1, n_heads, HEAD_DIM)
    v_heads = val_rows.reshape(-1, n_heads, HEAD_DIM)
    scores = jnp.einsum("qhd,khd->hqk", q_heads, k_heads, preferred_element_type=jnp.float32) * HEAD_DIM ** -0.5
    scores = jnp.where(key_mask[None, None, :], scores, NEG_BIG)
    attn_probs = jax.nn.softmax(scores, axis=-1).astype(jnp.bfloat16)
    attn_out = jnp.einsum("hqk,khd->qhd", attn_probs, v_heads, preferred_element_type=jnp.float32)
    return attn_out.astype(jnp.bfloat16).reshape(n_query, row_width)


def solution(mesh):
    n_seq = mesh.shape["seq"]
    row_spec = P(("batch", "seq"), None)
    rep_spec = P(None, None)

    def local_fn(tokens, w_query, w_key, w_value, w_out, rand_idx):
        blk_count, n_rand = rand_idx.shape
        tok_len = tokens.shape[0]
        blk_len = tok_len // blk_count
        row_width = w_query.shape[1]
        n_heads = row_width // HEAD_DIM
        n_hot = HOT_PER_RAND * n_rand
        pub_slots = GLOBAL_BLOCKS + n_hot
        total_blocks = n_seq * blk_count
        glob_rows = GLOBAL_BLOCKS * blk_len
        dev_index = lax.axis_index("seq")
        first_blk = dev_index * blk_count
        own_ids = first_blk + jnp.arange(blk_count)

        def project(weight):
            return jnp.dot(tokens, weight, preferred_element_type=jnp.float32).astype(jnp.bfloat16)

        q_loc = project(w_query)
        k_loc = project(w_key)
        v_loc = project(w_value)
        q_blocks = q_loc.reshape(blk_count, blk_len, row_width)
        k_blocks = k_loc.reshape(blk_count, blk_len, row_width)
        v_blocks = v_loc.reshape(blk_count, blk_len, row_width)

        to_right = [(src_dev, src_dev + 1) for src_dev in range(n_seq - 1)]
        to_left = [(src_dev + 1, src_dev) for src_dev in range(n_seq - 1)]
        left_k, left_v = lax.ppermute((k_blocks[-1], v_blocks[-1]), "seq", to_right)
        right_k, right_v = lax.ppermute((k_blocks[0], v_blocks[0]), "seq", to_left)
        k_ext = jnp.concatenate([left_k[None], k_blocks, right_k[None]])
        v_ext = jnp.concatenate([left_v[None], v_blocks, right_v[None]])

        idx_all = lax.all_gather(rand_idx, "seq", tiled=True)
        req_count = jax.ops.segment_sum(jnp.ones(idx_all.size, jnp.int32), idx_all.reshape(-1), num_segments=total_blocks)
        requested = req_count > 0
        blk_range = jnp.arange(total_blocks)
        hot_score = jnp.where(requested, req_count * total_blocks + (total_blocks - 1 - blk_range), -1)
        hot_order = lax.top_k(hot_score, n_hot)[1]
        hot_rank = jnp.sum(jnp.where(hot_order[None, :] == blk_range[:, None], jnp.arange(n_hot)[None, :], 0), axis=1)
        own_req = lax.dynamic_slice_in_dim(requested, first_blk, blk_count)
        own_rank = lax.dynamic_slice_in_dim(hot_rank, first_blk, blk_count)
        target = jnp.where(own_ids < GLOBAL_BLOCKS, own_ids, jnp.where(own_req, GLOBAL_BLOCKS + own_rank, -1))
        place = (jnp.arange(pub_slots)[:, None] == target[None, :]).astype(jnp.bfloat16)

        def publish(blocks, n_slots):
            return jnp.einsum("sl,lbe->sbe", place[:n_slots], blocks, preferred_element_type=jnp.float32).astype(jnp.bfloat16)

        pub_q, pub_k, pub_v = lax.psum((publish(q_blocks, GLOBAL_BLOCKS), publish(k_blocks, pub_slots), publish(v_blocks, pub_slots)), "seq")

        rand_slots = GLOBAL_BLOCKS + jnp.take(hot_rank, rand_idx)
        glob_slots = jnp.broadcast_to(jnp.arange(GLOBAL_BLOCKS), (blk_count, GLOBAL_BLOCKS))
        pub_rows = jnp.concatenate([glob_slots, rand_slots], axis=1)
        always_ok = jnp.zeros((blk_count, 1 + GLOBAL_BLOCKS + n_rand), jnp.int32) == 0
        mask_rows = jnp.concatenate([(own_ids - 1 >= GLOBAL_BLOCKS)[:, None], always_ok[:, :1], (own_ids + 1 < total_blocks)[:, None], always_ok[:, 1:]], axis=1)

        def one_block(blk_args):
            blk_pos, query_blk, pub_row, mask_row = blk_args
            key_rows = jnp.concatenate([lax.dynamic_slice_in_dim(k_ext, blk_pos, 3), jnp.take(pub_k, pub_row, axis=0)])
            val_rows = jnp.concatenate([lax.dynamic_slice_in_dim(v_ext, blk_pos, 3), jnp.take(pub_v, pub_row, axis=0)])
            return block_attention(query_blk, key_rows, val_rows, jnp.repeat(mask_row, blk_len))

        sparse_out = lax.map(one_block, (jnp.arange(blk_count), q_blocks, pub_rows, mask_rows))
        attn_loc = sparse_out.reshape(tok_len, row_width)

        glob_q = pub_q.reshape(glob_rows, n_heads, HEAD_DIM)
        k_heads = k_loc.reshape(tok_len, n_heads, HEAD_DIM)
        v_heads = v_loc.reshape(tok_len, n_heads, HEAD_DIM)
        glob_scores = jnp.einsum("qhd,khd->hqk", glob_q, k_heads, preferred_element_type=jnp.float32) * HEAD_DIM ** -0.5
        glob_exp = jnp.exp(glob_scores)
        part_num = jnp.einsum("hqk,khd->qhd", glob_exp.astype(jnp.bfloat16), v_heads, preferred_element_type=jnp.float32)
        glob_sum, glob_num = lax.psum((jnp.sum(glob_exp, axis=-1), part_num), "seq")
        glob_out = (glob_num / glob_sum.T[:, :, None]).astype(jnp.bfloat16).reshape(glob_rows, row_width)
        head_part = jnp.where(dev_index == 0, glob_out, attn_loc[:glob_rows])
        attn_loc = jnp.concatenate([head_part, attn_loc[glob_rows:]])
        out_f32 = lax.dot_general(attn_loc, w_out, (((1,), (1,)), ((), ())), preferred_element_type=jnp.float32)
        return out_f32.astype(jnp.bfloat16)

    return jax.shard_map(local_fn, mesh=mesh, in_specs=(row_spec, rep_spec, rep_spec, rep_spec, rep_spec, row_spec), out_specs=row_spec, check_vma=False)
```

profile of v0, /device:TPU:0, one launch (start us, length us, event | category | flops | bytes accessed | tf_op | source)
XLA Modules:
  0.0 553.7 jit_solution(11355289649303080462)
XLA Ops:
  6.5 37.8 %all-gather = s32[128,4,3]{2,1,0:T(4,128)S(1)} all-gather(s32[1,4,3]{2,1,0:T(4,128)} %bitcast.68), channel_id=1, replica_groups=mesh['batch'=1,'seq'=128] {'seq'}, dimensions={0}, use_global_device_ids=true | all-gather | bytes 6192 | tf_op jit(solution)/shard_map/all_gather | solution.py:61
  44.6 11.1 %scatter_custom_fusion = s32[512]{0:T(512)S(1)} fusion(s32[1536]{0:T(1024)S(1)} %reshape.114, s32[1536]{0:T(1024)S(1)} %broadcast.111, s32[]{:T(128)} %constant.38.clone.1), kind=kCustom, calls=%fused_computation.77 | custom fusion | flops 1536 | bytes 2052 | tf_op jit(solution)/shard_map/scatter-add | solution.py:62
  55.8 3.8 top_k.11
  59.8 5.9 %convolution_convert_fusion.3 = bf16[256,2048]{1,0:T(8,128)(2,1)S(1)} fusion(bf16[256,2048]{1,0:T(8,128)(2,1)S(1)} %copy-done, bf16[2048,2048]{1,0:T(8,128)(2,1)} %param.12), kind=kOutput, calls=%fused_computation.41 | convolution fusion | flops 2148007936 | bytes 10485760 | tf_op jit(solution)/shard_map/dot_general | solution.py:45
  65.7 3.1 convolution_convert_fusion
  71.3 3.1 convolution_convert_fusion.1
  79.7 2.6 copy.95
  88.9 4.2 collective-permute-start
  99.1 2.7 pad_maximum_fusion.2
  101.8 146.2 %all-reduce.6.cloned.1.call-done = (bf16[14,64,2048]{2,0,1:T(8,128)(2,1)}, bf16[14,64,2048]{2,0,1:T(8,128)(2,1)}, bf16[128,32,64]{0,2,1:T(8,128)(2,1)}) async-done(((bf16[14,64,2048]{2,0,1:T(8,128)(2,1)}, bf16[14,64,2048]{2,0,1:T(8,128)(2,1)}, bf16[128,32,64]{0,2,1:T(8,128)(2,1)}), (bf16[14,64,2048]{2,0,1:T(8,128)(2,1)}, bf16[14,64,2048]{2,0,1:T(8,128)(2,1)}, ...) | async-done | bytes 7864336 | tf_op jit(solution)/shard_map/psum | solution.py:76
  248.0 2.5 fusion.17
  252.5 6.2 %copy.88 = bf16[14,64,2048]{2,1,0:T(8,128)(2,1)} copy(bf16[14,64,2048]{2,0,1:T(8,128)(2,1)} %get-tuple-element.133) | data formatting | bytes 7340032 | tf_op jit(solution)/shard_map/while | solution.py:90
  258.7 3.8 copy.89
  262.5 209.9 %while.10 = (s32[]{:T(128)}, bf16[4,64,2048]{2,1,0:T(8,128)(2,1)}, s32[4]{0:T(128)S(1)}, bf16[6,64,2048]{2,1,0:T(8,128)(2,1)}, s32[4,5]{1,0:T(4,128)S(1)}, /*ind...) while((s32[]{:T(128)}, bf16[4,64,2048]{2,1,0:T(8,128)(2,1)}, ...), condition=%wide.region_12.14_spmd, body=%wide.region_9.13_spmd.sunk | while | flops 280364576 | bytes 71850904 | solution.py:90
  267.8 2.7 gather_fusion
  270.4 3.8 gather_fusion.1
  274.3 2.7 broadcast_select_fusion.3
  278.3 5.3 reshape.149
  285.1 8.7 %fusion.62 = f32[32,64,512]{2,1,0:T(8,128)} fusion(bf16[512,32,64]{2,1,0:T(8,128)(2,1)} %reshape.149, bf16[64,32,64]{2,1,0:T(8,128)(2,1)S(1)} %reshape.150), kind=kOutput, calls=%fused_computation.7.clone.1 | convolution fusion | flops 134217728 | bytes 6553600 | tf_op jit(solution)/shard_map/while/body/eval_jaxpr/qhd,khd->hqk/dot_general | solution.py:18
  294.0 6.6 %fusion.63 = (f32[32,64]{1,0:T(8,128)S(1)}, f32[32,64,512]{2,1,0:T(8,128)}) fusion(f32[32,64,512]{2,1,0:T(8,128)} %fusion.62, pred[512]{0:T(512)(128)(4,1)S(1)} %broadcast_in_dim.137), kind=kOutput, calls=%fused_computation.81.clone.1 | output fusion | flops 6291967 | bytes 8397312 | tf_op jit(solution)/shard_map/while/body/eval_jaxpr/sub | solution.py:20
  300.7 5.4 reshape.151
  306.1 8.0 %fusion.64 = bf16[32,64,64]{2,1,0:T(8,128)(2,1)S(1)} fusion(f32[32,64,512]{2,1,0:T(8,128)} %get-tuple-element.227, f32[32,64]{1,0:T(8,128)S(1)} %get-tuple-element.228, bf16[512,32,64]{2,1,0:T(8,128)(2,1)} %reshape.151), kind=kOutput, calls=%fused_computation.21.clone.1 | convolution fusion | flops 136445952 | bytes 6561792 | tf_op jit(solution)/shard_map/while/body/eval_jaxpr/hqk,khd->qhd/dot_general | solution.py:21
  320.1 2.7 gather_fusion
  322.8 3.8 gather_fusion.1
  326.6 2.7 broadcast_select_fusion.3
  330.6 5.3 reshape.149
  337.4 8.7 %fusion.62 = f32[32,64,512]{2,1,0:T(8,128)} fusion(bf16[512,32,64]{2,1,0:T(8,128)(2,1)} %reshape.149, bf16[64,32,64]{2,1,0:T(8,128)(2,1)S(1)} %reshape.150), kind=kOutput, calls=%fused_computation.7.clone.1 | convolution fusion | flops 134217728 | bytes 6553600 | tf_op jit(solution)/shard_map/while/body/eval_jaxpr/qhd,khd->hqk/dot_general | solution.py:18
  346.3 6.6 %fusion.63 = (f32[32,64]{1,0:T(8,128)S(1)}, f32[32,64,512]{2,1,0:T(8,128)}) fusion(f32[32,64,512]{2,1,0:T(8,128)} %fusion.62, pred[512]{0:T(512)(128)(4,1)S(1)} %broadcast_in_dim.137), kind=kOutput, calls=%fused_computation.81.clone.1 | output fusion | flops 6291967 | bytes 8397312 | tf_op jit(solution)/shard_map/while/body/eval_jaxpr/sub | solution.py:20
  353.1 5.4 reshape.151
  358.5 8.0 %fusion.64 = bf16[32,64,64]{2,1,0:T(8,128)(2,1)S(1)} fusion(f32[32,64,512]{2,1,0:T(8,128)} %get-tuple-element.227, f32[32,64]{1,0:T(8,128)S(1)} %get-tuple-element.228, bf16[512,32,64]{2,1,0:T(8,128)(2,1)} %reshape.151), kind=kOutput, calls=%fused_computation.21.clone.1 | convolution fusion | flops 136445952 | bytes 6561792 | tf_op jit(solution)/shard_map/while/body/eval_jaxpr/hqk,khd->qhd/dot_general | solution.py:21
  372.5 2.7 gather_fusion
  375.2 3.8 gather_fusion.1
  379.0 2.7 broadcast_select_fusion.3
  383.0 5.3 reshape.149
  389.8 8.7 %fusion.62 = f32[32,64,512]{2,1,0:T(8,128)} fusion(bf16[512,32,64]{2,1,0:T(8,128)(2,1)} %reshape.149, bf16[64,32,64]{2,1,0:T(8,128)(2,1)S(1)} %reshape.150), kind=kOutput, calls=%fused_computation.7.clone.1 | convolution fusion | flops 134217728 | bytes 6553600 | tf_op jit(solution)/shard_map/while/body/eval_jaxpr/qhd,khd->hqk/dot_general | solution.py:18
  398.7 6.6 %fusion.63 = (f32[32,64]{1,0:T(8,128)S(1)}, f32[32,64,512]{2,1,0:T(8,128)}) fusion(f32[32,64,512]{2,1,0:T(8,128)} %fusion.62, pred[512]{0:T(512)(128)(4,1)S(1)} %broadcast_in_dim.137), kind=kOutput, calls=%fused_computation.81.clone.1 | output fusion | flops 6291967 | bytes 8397312 | tf_op jit(solution)/shard_map/while/body/eval_jaxpr/sub | solution.py:20
  405.5 5.4 reshape.151
  410.8 8.0 %fusion.64 = bf16[32,64,64]{2,1,0:T(8,128)(2,1)S(1)} fusion(f32[32,64,512]{2,1,0:T(8,128)} %get-tuple-element.227, f32[32,64]{1,0:T(8,128)S(1)} %get-tuple-element.228, bf16[512,32,64]{2,1,0:T(8,128)(2,1)} %reshape.151), kind=kOutput, calls=%fused_computation.21.clone.1 | convolution fusion | flops 136445952 | bytes 6561792 | tf_op jit(solution)/shard_map/while/body/eval_jaxpr/hqk,khd->qhd/dot_general | solution.py:21
  424.8 2.7 gather_fusion
  427.5 3.8 gather_fusion.1
  431.3 2.7 broadcast_select_fusion.3
  435.3 5.3 reshape.149
  442.1 8.7 %fusion.62 = f32[32,64,512]{2,1,0:T(8,128)} fusion(bf16[512,32,64]{2,1,0:T(8,128)(2,1)} %reshape.149, bf16[64,32,64]{2,1,0:T(8,128)(2,1)S(1)} %reshape.150), kind=kOutput, calls=%fused_computation.7.clone.1 | convolution fusion | flops 134217728 | bytes 6553600 | tf_op jit(solution)/shard_map/while/body/eval_jaxpr/qhd,khd->hqk/dot_general | solution.py:18
  451.0 6.6 %fusion.63 = (f32[32,64]{1,0:T(8,128)S(1)}, f32[32,64,512]{2,1,0:T(8,128)}) fusion(f32[32,64,512]{2,1,0:T(8,128)} %fusion.62, pred[512]{0:T(512)(128)(4,1)S(1)} %broadcast_in_dim.137), kind=kOutput, calls=%fused_computation.81.clone.1 | output fusion | flops 6291967 | bytes 8397312 | tf_op jit(solution)/shard_map/while/body/eval_jaxpr/sub | solution.py:20
  457.8 5.4 reshape.151
  463.2 8.0 %fusion.64 = bf16[32,64,64]{2,1,0:T(8,128)(2,1)S(1)} fusion(f32[32,64,512]{2,1,0:T(8,128)} %get-tuple-element.227, f32[32,64]{1,0:T(8,128)S(1)} %get-tuple-element.228, bf16[512,32,64]{2,1,0:T(8,128)(2,1)} %reshape.151), kind=kOutput, calls=%fused_computation.21.clone.1 | convolution fusion | flops 136445952 | bytes 6561792 | tf_op jit(solution)/shard_map/while/body/eval_jaxpr/hqk,khd->qhd/dot_general | solution.py:21
  472.4 64.2 %psum.37 = f32[128,32]{0,1:T(8,128)S(1)} all-reduce(f32[128,32]{0,1:T(8,128)S(1)} %bitcast.67), channel_id=1, replica_groups=mesh['batch'=1,'seq'=128] {'seq'}, use_global_device_ids=true, to_apply=%region_6.7 | all-reduce | flops 4096 | bytes 32768 | tf_op jit(solution)/shard_map/psum | solution.py:99
  539.6 6.8 %convolution_convert_fusion.2 = bf16[256,2048]{1,0:T(8,128)(2,1)} fusion(bf16[2048,2048]{1,0:T(8,128)(2,1)} %param.14, bf16[128,2048]{1,0:T(8,128)(2,1)S(1)} %bitcast.65, bf16[128,2048]{1,0:T(8,128)(2,1)S(1)} %bitcast_select_fusion), kind=kOutput, calls=%fused_computation.40 | convolution fusion | flops 2150105088 | bytes 10485760 | tf_op jit(solution)/shard_map/dot_general | solution.py:103
  (147 shorter events, 53.8 us)
Async XLA Ops:
  6.5 53.3 %copy-start = (bf16[256,2048]{1,0:T(8,128)(2,1)S(1)}, bf16[256,2048]{1,0:T(8,128)(2,1)}, u32[]{:S(2)}) copy-start(bf16[256,2048]{1,0:T(8,128)(2,1)} %param.10) | copy-start | bytes 3145732
  6.5 241.5 %all-reduce.6.cloned.1.call-start = ((), (), s32[]{:S(2)}) async-start(), calls=%async_computation.1 | async-start | bytes 17825792 | tf_op jit(solution)/shard_map/psum | solution.py:76
  59.8 9.0 %copy-start.10 = (bf16[2048,2048]{1,0:T(8,128)(2,1)S(1)}, bf16[2048,2048]{1,0:T(8,128)(2,1)}, u32[]{:S(2)}) copy-start(bf16[2048,2048]{1,0:T(8,128)(2,1)} %param.13) | copy-start | bytes 25165828
  65.7 29.8 %copy-start.6 = (bf16[256,2048]{1,0:T(8,128)(2,1)}, bf16[256,2048]{1,0:T(8,128)(2,1)S(1)}, u32[]{:S(2)}) copy-start(bf16[256,2048]{1,0:T(8,128)(2,1)S(1)} %convolution_convert_fusion.3) | copy-start | bytes 3145732
  65.7 8.7 %slice-start = ((s8[8388608]{0:T(1024)(128)(4,1)}), s8[4194304]{0:T(1024)(128)(4,1)S(1)}, s32[]{:S(2)}) async-start(s8[8388608]{0:T(1024)(128)(4,1)} %bitcast.69), calls=%async_computation.2 | async-start | bytes 8388608
  68.8 5.5 %slice-start.1 = ((s8[8388608]{0:T(1024)(128)(4,1)}), s8[4194304]{0:T(1024)(128)(4,1)S(1)}, s32[]{:S(2)}) async-start(s8[8388608]{0:T(1024)(128)(4,1)} %bitcast.69), calls=%async_computation.3 | async-start | bytes 8388608
  71.2 25.6 %copy-start.5 = (bf16[256,2048]{1,0:T(8,128)(2,1)}, bf16[256,2048]{1,0:T(8,128)(2,1)S(1)}, u32[]{:S(2)}) copy-start(bf16[256,2048]{1,0:T(8,128)(2,1)S(1)} %convolution_convert_fusion.5) | copy-start | bytes 3145732
  76.8 1.0 copy-start.8
  83.6 10.9 %copy-start.9 = (s32[4,3]{1,0:T(4,128)S(1)}, s32[4,3]{1,0:T(4,128)}, u32[]{:S(2)}) copy-start(s32[4,3]{1,0:T(4,128)} %param.15) | copy-start | bytes 148
  83.6 454.3 %all-reduce.4.cloned.1.call-start = ((), (), s32[]{:S(2)}) async-start(), calls=%async_computation | async-start | bytes 2097152 | tf_op jit(solution)/shard_map/psum | solution.py:99
  84.5 13.1 %collective-permute-start.2 = (bf16[64,2048]{1,0:T(8,128)(2,1)}, bf16[64,2048]{1,0:T(8,128)(2,1)S(1)}, u32[]{:S(2)}, u32[]{:S(2)}) collective-permute-start(bf16[64,2048]{1,0:T(8,128)(2,1)} %get-tuple-element.146), channel_id=1, source_target_pairs={{0,1},{1,2},{2,3},{3,4},{4,5},{5,6},{6,7},{7,8},{8,9},{9,10},{10,1... | collective-permute-start | bytes 786440 | tf_op jit(solution)/shard_map/ppermute | solution.py:56
  86.8 10.8 %collective-permute-start.3 = (bf16[64,2048]{1,0:T(8,128)(2,1)}, bf16[64,2048]{1,0:T(8,128)(2,1)}, u32[]{:S(2)}, u32[]{:S(2)}) collective-permute-start(bf16[64,2048]{1,0:T(8,128)(2,1)} %get-tuple-element.147), channel_id=1, source_target_pairs={{1,0},{2,1},{3,2},{4,3},{5,4},{6,5},{7,6},{8,7},{9,8},{10,9},{11,1... | collective-permute-start | bytes 786440 | tf_op jit(solution)/shard_map/ppermute | solution.py:57
  88.9 10.2 %collective-permute-start = (bf16[64,2048]{1,0:T(8,128)(2,1)}, bf16[64,2048]{1,0:T(8,128)(2,1)}, u32[]{:S(2)}, u32[]{:S(2)}) collective-permute-start(bf16[64,2048]{1,0:T(8,128)(2,1)} %get-tuple-element.148), channel_id=1, source_target_pairs={{0,1},{1,2},{2,3},{3,4},{4,5},{5,6},{6,7},{7,8},{8,9},{9,10},{10,1... | collective-permute-start | bytes 786440 | tf_op jit(solution)/shard_map/ppermute | solution.py:56
  93.1 6.1 %collective-permute-start.1 = (bf16[64,2048]{1,0:T(8,128)(2,1)}, bf16[64,2048]{1,0:T(8,128)(2,1)}, u32[]{:S(2)}, u32[]{:S(2)}) collective-permute-start(bf16[64,2048]{1,0:T(8,128)(2,1)} %get-tuple-element.149), channel_id=1, source_target_pairs={{1,0},{2,1},{3,2},{4,3},{5,4},{6,5},{7,6},{8,7},{9,8},{10,9},{11,1... | collective-permute-start | bytes 786440 | tf_op jit(solution)/shard_map/ppermute | solution.py:57
  252.5 6.2 %copy-start.7 = (bf16[14,64,2048]{2,0,1:T(8,128)(2,1)S(1)}, bf16[14,64,2048]{2,0,1:T(8,128)(2,1)}, u32[]{:S(2)}) copy-start(bf16[14,64,2048]{2,0,1:T(8,128)(2,1)} %get-tuple-element.134) | copy-start | bytes 11010052
  262.7 5.0 copy-start.3
  294.0 6.6 %copy-start.2 = (bf16[5,64,2048]{2,1,0:T(8,128)(2,1)S(1)}, bf16[5,64,2048]{2,1,0:T(8,128)(2,1)}, u32[]{:S(2)}) copy-start(bf16[5,64,2048]{2,1,0:T(8,128)(2,1)} %get-tuple-element.229) | copy-start | bytes 3932164 | tf_op jit(solution)/shard_map/while
  306.1 9.0 %copy-start.4 = (bf16[6,64,2048]{2,1,0:T(8,128)(2,1)S(1)}, bf16[6,64,2048]{2,1,0:T(8,128)(2,1)}, u32[]{:S(2)}) copy-start(bf16[6,64,2048]{2,1,0:T(8,128)(2,1)} %copy-done.3) | copy-start | bytes 4718596 | tf_op jit(solution)/shard_map/while
  315.1 5.0 copy-start.3
  346.3 6.6 %copy-start.2 = (bf16[5,64,2048]{2,1,0:T(8,128)(2,1)S(1)}, bf16[5,64,2048]{2,1,0:T(8,128)(2,1)}, u32[]{:S(2)}) copy-start(bf16[5,64,2048]{2,1,0:T(8,128)(2,1)} %get-tuple-element.229) | copy-start | bytes 3932164 | tf_op jit(solution)/shard_map/while
  358.5 9.0 %copy-start.4 = (bf16[6,64,2048]{2,1,0:T(8,128)(2,1)S(1)}, bf16[6,64,2048]{2,1,0:T(8,128)(2,1)}, u32[]{:S(2)}) copy-start(bf16[6,64,2048]{2,1,0:T(8,128)(2,1)} %copy-done.3) | copy-start | bytes 4718596 | tf_op jit(solution)/shard_map/while
  367.4 5.0 copy-start.3
  398.7 6.6 %copy-start.2 = (bf16[5,64,2048]{2,1,0:T(8,128)(2,1)S(1)}, bf16[5,64,2048]{2,1,0:T(8,128)(2,1)}, u32[]{:S(2)}) copy-start(bf16[5,64,2048]{2,1,0:T(8,128)(2,1)} %get-tuple-element.229) | copy-start | bytes 3932164 | tf_op jit(solution)/shard_map/while
  410.8 9.0 %copy-start.4 = (bf16[6,64,2048]{2,1,0:T(8,128)(2,1)S(1)}, bf16[6,64,2048]{2,1,0:T(8,128)(2,1)}, u32[]{:S(2)}) copy-start(bf16[6,64,2048]{2,1,0:T(8,128)(2,1)} %copy-done.3) | copy-start | bytes 4718596 | tf_op jit(solution)/shard_map/while
  419.8 5.0 copy-start.3
  451.0 6.6 %copy-start.2 = (bf16[5,64,2048]{2,1,0:T(8,128)(2,1)S(1)}, bf16[5,64,2048]{2,1,0:T(8,128)(2,1)}, u32[]{:S(2)}) copy-start(bf16[5,64,2048]{2,1,0:T(8,128)(2,1)} %get-tuple-element.229) | copy-start | bytes 3932164 | tf_op jit(solution)/shard_map/while
  463.2 9.0 %copy-start.4 = (bf16[6,64,2048]{2,1,0:T(8,128)(2,1)S(1)}, bf16[6,64,2048]{2,1,0:T(8,128)(2,1)}, u32[]{:S(2)}) copy-start(bf16[6,64,2048]{2,1,0:T(8,128)(2,1)} %copy-done.3) | copy-start | bytes 4718596 | tf_op jit(solution)/shard_map/while
  539.6 6.8 %copy-start.1 = (bf16[256,2048]{1,0:T(8,128)(2,1)S(1)}, bf16[256,2048]{1,0:T(8,128)(2,1)}, u32[]{:S(2)}) copy-start(bf16[256,2048]{1,0:T(8,128)(2,1)} %param.10) | copy-start | bytes 3145732
Sparse Core Ops, SparseCore 0:
  83.7 164.2 all-reduce.5
  252.8 147.9 all-reduce.3
where the time goes:
time: 564 us; the launch traced here: 554 us
  waiting for transfers between devices  146 us (26%)
  local copies, waits for them, and re-layouts  112 us (20%)
  blocking collectives  102 us (18%)
  matrix products  97.1 us (17%)
  other arithmetic  64.1 us (11%)
  between operations  14.1 us (2%)
  starting transfers between devices  9.22 us (2%)
  loops' own time  9 us (2%)
    psum x1, waiting for transfers between devices, local_fn(): lax.psum((publish(q_blocks, GLOBAL_BLOCKS), publish(k_blocks, pub_slots),...  146 us
    psum x1, blocking collectives, local_fn(): glob_sum, glob_num = lax.psum((jnp.sum(glob_exp, axis=-1), part_num), 'seq')  64.2 us
    all_gather x1, blocking collectives, local_fn(): idx_all = lax.all_gather(rand_idx, 'seq', tiled=True)  37.8 us
    dot_general x4, matrix products, block_attention(): jnp.einsum('qhd,khd->hqk', q_heads, k_heads, preferred_element_type=jnp.f...  34.9 us
    dot_general x4, matrix products, block_attention(): jnp.einsum('hqk,khd->qhd', attn_probs, v_heads, preferred_element_type=jn...  32.1 us
    sub x4, other arithmetic, block_attention(): attn_probs = jax.nn.softmax(scores, axis=-1).astype(jnp.bfloat16)  26.3 us
    reshape x4, local copies, waits for them, and re-layouts, block_attention(): v_heads = val_rows.reshape(-1, n_heads, HEAD_DIM)  21.4 us
    reshape x4, local copies, waits for them, and re-layouts, block_attention(): k_heads = key_rows.reshape(-1, n_heads, HEAD_DIM)  21.3 us
  transfers between devices with their start and end apart: 6, of which 1 were waited for; matrix products, arithmetic and copies ran while one was open for 40% of the time, Pallas kernels for 0%

commit v1 on v0

v1 whole, which is shorter than its diff:
```python
import jax
import jax.numpy as jnp
from jax import lax
from jax.experimental import pallas as pl
from jax.experimental.pallas import tpu as pltpu
from jax.sharding import PartitionSpec as P

HEAD_DIM = 64
GLOBAL_BLOCKS = 2
HOT = 12
SLOTS = 16
BLK = 64
WIDTH = 2048
HALF = 1024
CHIPS = 64
NEG = -1e30
MESH = pl.DeviceIdType.MESH
VMEM = pltpu.VMEM
ANY = pl.ANY
PARTS = ((0, 768, (0, 1, 2)), (768, 640, (1, 2, 0)), (1408, 640, (2, 0, 1)))


def vspec():
    return pl.BlockSpec(memory_space=VMEM)


def params(effects=True, mib=60):
    return pltpu.CompilerParams(has_side_effects=effects, vmem_limit_bytes=mib * 1024 * 1024)


def where_am_i():
    dev = lax.axis_index("seq")
    return dev, dev // 2, dev % 2


def scatter_kernel(xs_ref, x_ref, idx_ref, recv_ref, xc_ref, idxall_ref, s_send, s_recv, i_send, i_recv, x_send, x_recv, h_send, h_recv, loc):
    dev, chip, core = where_am_i()

    def row_copy(dst_chip, slot):
        return pltpu.make_async_remote_copy(
            src_ref=xs_ref.at[dst_chip], dst_ref=recv_ref.at[slot], send_sem=s_send, recv_sem=s_recv.at[slot],
            device_id={"seq": 2 * dst_chip + core}, device_id_type=MESH)

    def idx_copy(dst, slot):
        return pltpu.make_async_remote_copy(
            src_ref=idx_ref, dst_ref=idxall_ref.at[slot], send_sem=i_send, recv_sem=i_recv.at[slot],
            device_id={"seq": dst}, device_id_type=MESH)

    own = pl.ds(1 + 4 * core, 4)
    part = pltpu.make_async_remote_copy(
        src_ref=x_ref, dst_ref=xc_ref.at[own], send_sem=x_send, recv_sem=x_recv,
        device_id={"seq": dev + 1 - 2 * core}, device_id_type=MESH)
    part.start()

    def start_idx(i, carry):
        idx_copy(dev ^ i, dev).start()
        return carry
    lax.fori_loop(1, 128, start_idx, 0)

    def start_row(i, carry):
        row_copy(chip ^ i, chip).start()
        return carry
    lax.fori_loop(1, CHIPS, start_row, 0)

    nbr = lax.rem(chip + 2 * core - 1 + CHIPS, CHIPS)
    halos = [pltpu.make_async_remote_copy(
        src_ref=x_ref.at[3 * core], dst_ref=xc_ref.at[9 * (1 - core)], send_sem=h_send.at[k], recv_sem=h_recv.at[1 - core],
        device_id={"seq": 2 * nbr + k}, device_id_type=MESH) for k in range(2)]
    for h in halos:
        h.start()
    locs = [pltpu.make_async_copy(xs_ref.at[chip], recv_ref.at[chip], loc.at[0]),
            pltpu.make_async_copy(x_ref, xc_ref.at[own], loc.at[1]),
            pltpu.make_async_copy(idx_ref, idxall_ref.at[dev], loc.at[2])]
    for l in locs:
        l.start()
    for l in locs:
        l.wait()
    part.wait_send()
    other = pl.ds(5 - 4 * core, 4)
    pltpu.make_async_remote_copy(
        src_ref=x_ref, dst_ref=xc_ref.at[other], send_sem=x_send, recv_sem=x_recv,
        device_id={"seq": dev + 1 - 2 * core}, device_id_type=MESH).wait_recv()
    for k in range(2):
        halos[k].wait_send()
        pltpu.make_async_remote_copy(
            src_ref=x_ref.at[0], dst_ref=xc_ref.at[9 * k], send_sem=h_send.at[0], recv_sem=h_recv.at[k],
            device_id={"seq": 2 * nbr + k}, device_id_type=MESH).wait_recv()

    def wait_idx(i, carry):
        idx_copy(dev ^ i, dev ^ i).wait()
        return carry
    lax.fori_loop(1, 128, wait_idx, 0)

    def wait_row(i, carry):
        row_copy(chip ^ i, chip ^ i).wait()
        return carry
    lax.fori_loop(1, CHIPS, wait_row, 0)


def scatter_rows(xs, x, idx):
    return pl.pallas_call(
        scatter_kernel,
        out_shape=(jax.ShapeDtypeStruct((CHIPS, BLK, 128), jnp.bfloat16),
                   jax.ShapeDtypeStruct((10, BLK, WIDTH), jnp.bfloat16),
                   jax.ShapeDtypeStruct((128, 1, 128), jnp.int32)),
        in_specs=[vspec()] * 3, out_specs=(vspec(),) * 3,
        scratch_shapes=[pltpu.SemaphoreType.DMA, pltpu.SemaphoreType.DMA((CHIPS,)),
                        pltpu.SemaphoreType.DMA, pltpu.SemaphoreType.DMA((128,)),
                        pltpu.SemaphoreType.DMA, pltpu.SemaphoreType.DMA,
                        pltpu.SemaphoreType.DMA((2,)), pltpu.SemaphoreType.DMA((2,)), pltpu.SemaphoreType.DMA((3,))],
        compiler_params=params(), name="scatter_rows",
    )(xs, x, idx)


def project_kernel(core_ref, x_ref, wq_ref, wk_ref, wv_ref, q_ref, k_ref, v_ref):
    q_ref[...] = (jnp.dot(x_ref[64:576, :], wq_ref[...], preferred_element_type=jnp.float32)).astype(jnp.bfloat16)
    k_ref[...] = jnp.dot(x_ref[...], wk_ref[...], preferred_element_type=jnp.float32).astype(jnp.bfloat16)
    v_ref[...] = jnp.dot(x_ref[...], wv_ref[...], preferred_element_type=jnp.float32).astype(jnp.bfloat16)


def project_rows(core, xc, wq, wk, wv):
    tile = 256
    steps = HALF // tile
    wspec = pl.BlockSpec((WIDTH, tile), lambda j, c: (0, c[0] * steps + j))
    return pl.pallas_call(
        project_kernel,
        grid_spec=pltpu.PrefetchScalarGridSpec(
            num_scalar_prefetch=1, grid=(steps,),
            in_specs=[pl.BlockSpec((640, WIDTH), lambda j, c: (0, 0)), wspec, wspec, wspec],
            out_specs=[pl.BlockSpec((512, tile), lambda j, c: (0, j)),
                       pl.BlockSpec((640, tile), lambda j, c: (0, j)),
                       pl.BlockSpec((640, tile), lambda j, c: (0, j))]),
        out_shape=(jax.ShapeDtypeStruct((512, HALF), jnp.bfloat16),
                   jax.ShapeDtypeStruct((640, HALF), jnp.bfloat16),
                   jax.ShapeDtypeStruct((640, HALF), jnp.bfloat16)),
        compiler_params=params(False), name="project_rows",
        cost_estimate=pl.CostEstimate(flops=2 * 1792 * WIDTH * HALF, bytes_accessed=20 << 20, transcendentals=0),
    )(core, xc, wq, wk, wv)


def gather_kernel(sel_ref, wq_ref, wk_ref, wv_ref, g_ref, w_buf, other, w_sem, p_sem, g_send, g_recv):
    dev, chip, core = where_am_i()
    cx, cy, cz = chip % 4, (chip // 4) % 4, chip // 16
    loads = [pltpu.make_async_copy(w.at[:, pl.ds(core * HALF, HALF)], w_buf.at[i], w_sem.at[i])
             for i, w in enumerate((wk_ref, wv_ref, wq_ref))]
    for l in loads:
        l.start()
    swap = pltpu.make_async_remote_copy(
        src_ref=sel_ref, dst_ref=other, send_sem=p_sem.at[0], recv_sem=p_sem.at[1],
        device_id={"seq": dev + 1 - 2 * core}, device_id_type=MESH)
    swap.start()
    swap.wait()
    rows = sel_ref[...] + other[...]
    out = []
    for i in range(3):
        loads[i].wait()
        out.append(jnp.dot(rows, w_buf[i], preferred_element_type=jnp.float32))
    kv = jnp.concatenate([out[0], out[1]], axis=1)
    glob_q = jnp.concatenate([out[2][0:1], out[2][1:2]], axis=1)
    row_id = lax.broadcasted_iota(jnp.int32, (SLOTS, WIDTH), 0)
    kv = jnp.where(row_id == 14, jnp.broadcast_to(glob_q, (SLOTS, WIDTH)), kv)
    g_ref[cz, cy, cx] = kv.astype(jnp.bfloat16)

    coord = (cx, cy, cz)
    scale = (1, 4, 16)

    def block(axes_done, at, cols):
        idx = []
        for axis in (2, 1, 0):
            idx.append(slice(None) if axis in axes_done else at[axis])
        return tuple(idx) + (slice(None), cols)

    def copies(part, stage, receive):
        start, size, order = PARTS[part]
        axis = order[stage]
        out = []
        for k in (1, 2, 3):
            to = lax.rem(coord[axis] + k, 4)
            frm = lax.rem(coord[axis] + 4 - k, 4)
            at = list(coord)
            if receive:
                at[axis] = frm
            ref = g_ref.at[block(order[:stage], at, slice(start, start + size))]
            out.append(pltpu.make_async_remote_copy(
                src_ref=ref, dst_ref=ref, send_sem=g_send.at[part, stage, k - 1], recv_sem=g_recv.at[part, stage, k - 1],
                device_id={"seq": dev + 2 * scale[axis] * (to - coord[axis])}, device_id_type=MESH))
        return out

    for stage in range(3):
        for part in range(3):
            if stage:
                for c in copies(part, stage - 1, True):
                    c.wait_recv()
            for c in copies(part, stage, False):
                c.start()
    for part in range(3):
        for c in copies(part, 2, True):
            c.wait_recv()
    for stage in range(3):
        for part in range(3):
            for c in copies(part, stage, False):
                c.wait_send()


def gather_rows(sel, wq, wk, wv):
    anyspec = pl.BlockSpec(memory_space=ANY)
    return pl.pallas_call(
        gather_kernel,
        out_shape=jax.ShapeDtypeStruct((4, 4, 4, SLOTS, WIDTH), jnp.bfloat16),
        in_specs=[vspec(), anyspec, anyspec, anyspec], out_specs=vspec(),
        scratch_shapes=[VMEM((3, WIDTH, HALF), jnp.bfloat16), VMEM((SLOTS, WIDTH), jnp.bfloat16),
                        pltpu.SemaphoreType.DMA((3,)), pltpu.SemaphoreType.DMA((2,)),
                        pltpu.SemaphoreType.DMA((3, 3, 3)), pltpu.SemaphoreType.DMA((3, 3, 3))],
        compiler_params=params(), name="gather_rows",
    )(sel, wq, wk, wv)


def split_heads(pair, rows):
    lane = lax.broadcasted_iota(jnp.int32, (rows, 128), 1)
    zero = jnp.zeros_like(pair)
    return jnp.concatenate([jnp.where(lane < HEAD_DIM, pair, zero), jnp.where(lane < HEAD_DIM, zero, pair)], axis=0)


def join_heads(out, rows):
    lane = lax.broadcasted_iota(jnp.int32, (rows, 128), 1)
    return jnp.where(lane < HEAD_DIM, out[:rows], out[rows:])


def attention_kernel(info_ref, q_ref, k_ref, v_ref, g_ref, o_ref, part_ref, hot):
    nt = (((1,), (1,)), ((), ()))
    row = lax.broadcasted_iota(jnp.int32, (256, 256), 0)
    col = lax.broadcasted_iota(jnp.int32, (256, 256), 1)
    perm = jnp.where(col == (row % 16) * 16 + row // 16, 1.0, 0.0).astype(jnp.bfloat16)

    def unpack(step, carry):
        z = step // 8
        cols = pl.ds(pl.multiple_of((step % 8) * 256, 256), 256)
        rows = g_ref[pl.ds(pl.multiple_of(z * 256, 256), 256), cols]
        moved = jnp.dot(perm, rows, preferred_element_type=jnp.float32).astype(jnp.bfloat16)
        for s in range(SLOTS):
            hot[pl.ds(pl.multiple_of(s * BLK + z * 16, 16), 16), cols] = moved[s * 16:s * 16 + 16]
        return carry
    lax.fori_loop(0, 32, unpack, 0)

    def one_block(b, carry):
        slots = [pl.multiple_of(info_ref[b * 3 + t] * BLK, BLK) for t in range(3)]
        left_bad = info_ref[32 + b]
        right_bad = info_ref[40 + b]
        key = lax.broadcasted_iota(jnp.int32, (1, 256), 1)
        bias = jnp.where((key < BLK) & (left_bad > 0), NEG, 0.0) + jnp.where((key >= 2 * BLK) & (key < 3 * BLK) & (right_bad > 0), NEG, 0.0)
        base = pl.multiple_of(b * BLK, BLK)
        for j in range(8):
            cols = slice(j * 128, j * 128 + 128)
            vcols = slice(HALF + j * 128, HALF + j * 128 + 128)
            queries = split_heads(q_ref[pl.ds(base, BLK), cols], BLK) * jnp.bfloat16(0.125)
            keys = jnp.concatenate([k_ref[pl.ds(base, 3 * BLK), cols], hot[0:2 * BLK, cols]] + [hot[pl.ds(s, BLK), cols] for s in slots], axis=0)
            vals = jnp.concatenate([v_ref[pl.ds(base, 3 * BLK), cols], hot[0:2 * BLK, vcols]] + [hot[pl.ds(s, BLK), vcols] for s in slots], axis=0)
            scores = lax.dot_general(queries, keys, nt, preferred_element_type=jnp.float32)
            scores = jnp.concatenate([scores[:, :256] + bias, scores[:, 256:]], axis=1)
            top = jnp.max(scores, axis=1, keepdims=True)
            probs = jnp.exp(scores - top)
            probs = probs * (1.0 / jnp.sum(probs, axis=1, keepdims=True))
            out = jnp.dot(probs.astype(jnp.bfloat16), vals, preferred_element_type=jnp.float32)
            o_ref[pl.ds(base, BLK), cols] = join_heads(out, BLK).astype(jnp.bfloat16)
        return carry
    lax.fori_loop(0, 8, one_block, 0)

    lane = lax.broadcasted_iota(jnp.int32, (128, 128), 1)
    stats = None
    for j in range(8):
        cols = slice(j * 128, j * 128 + 128)
        vcols = slice(HALF + j * 128, HALF + j * 128 + 128)
        glob = jnp.concatenate([hot[14 * BLK:15 * BLK, cols], hot[14 * BLK:15 * BLK, vcols]], axis=0)
        queries = split_heads(glob, 128) * jnp.bfloat16(0.125)
        scores = lax.dot_general(queries, k_ref[BLK:9 * BLK, cols], nt, preferred_element_type=jnp.float32)
        top = jnp.max(scores, axis=1, keepdims=True)
        probs = jnp.exp(scores - top)
        total = jnp.sum(probs, axis=1, keepdims=True)
        out = jnp.dot(probs.astype(jnp.bfloat16), v_ref[BLK:9 * BLK, cols], preferred_element_type=jnp.float32)
        g, t = j // 2, 2 * (j % 2)
        part_ref[:, 384 * g + 64 * t:384 * g + 64 * t + 128] = join_heads(out, 128)
        if t == 0:
            stats = jnp.zeros((128, 128), jnp.float32)
        for h in range(2):
            rows = slice(128 * h, 128 * h + 128)
            stats = jnp.where(lane == t + h, total[rows], stats)
            stats = jnp.where(lane == 4 + t + h, top[rows], stats)
        if t:
            part_ref[:, 384 * g + 256:384 * g + 384] = stats


def attention(info, q, k, v, g):
    return pl.pallas_call(
        attention_kernel,
        grid_spec=pltpu.PrefetchScalarGridSpec(
            num_scalar_prefetch=1, grid=(1,),
            in_specs=[vspec()] * 4, out_specs=[vspec()] * 2,
            scratch_shapes=[VMEM((SLOTS * BLK, WIDTH), jnp.bfloat16)]),
        out_shape=(jax.ShapeDtypeStruct((512, HALF), jnp.bfloat16), jax.ShapeDtypeStruct((128, 1536), jnp.float32)),
        compiler_params=params(False), name="attention",
        cost_estimate=pl.CostEstimate(flops=2 << 30, bytes_accessed=16 << 20, transcendentals=10 << 20),
    )(info, q, k, v, g)


def combine_kernel(part_ref, o_ref, full_ref, recv, glob, piece, c_send, c_recv, o_send, o_recv, g_send, g_recv, loc):
    dev, chip, core = where_am_i()

    def part_copy(dst_chip, slot):
        rows = pl.ds(pl.multiple_of((dst_chip % 16) * 8, 8), 8)
        cols = pl.ds(pl.multiple_of((dst_chip // 16) * 384, 128), 384)
        return pltpu.make_async_remote_copy(
            src_ref=part_ref.at[rows, cols], dst_ref=recv.at[slot], send_sem=c_send, recv_sem=c_recv.at[slot],
            device_id={"seq": 2 * dst_chip + core}, device_id_type=MESH)

    def start(i, carry):
        part_copy(chip ^ i, chip).start()
        return carry
    lax.fori_loop(1, CHIPS, start, 0)

    def o_copy(rows_of, cols_of):
        return pltpu.make_async_remote_copy(
            src_ref=o_ref.at[pl.ds(pl.multiple_of(rows_of * 256, 256), 256)],
            dst_ref=full_ref.at[:, pl.ds(pl.multiple_of(cols_of * HALF, HALF), HALF)],
            send_sem=o_send, recv_sem=o_recv, device_id={"seq": dev + 1 - 2 * core}, device_id_type=MESH)
    o_copy(1 - core, core).start()
    mine = [pltpu.make_async_copy(o_ref.at[pl.ds(pl.multiple_of(core * 256, 256), 256)],
                                  full_ref.at[:, pl.ds(pl.multiple_of(core * HALF, HALF), HALF)], loc.at[0]),
            pltpu.make_async_copy(part_ref.at[pl.ds(pl.multiple_of((chip % 16) * 8, 8), 8), pl.ds(pl.multiple_of((chip // 16) * 384, 128), 384)],
                                  recv.at[chip], loc.at[1])]
    for m in mine:
        m.start()
    for m in mine:
        m.wait()

    def wait(i, carry):
        part_copy(chip ^ i, chip ^ i).wait()
        return carry
    lax.fori_loop(1, CHIPS, wait, 0)

    top = lax.fori_loop(0, CHIPS, lambda i, t: jnp.maximum(t, recv[i, :, 256:384]), jnp.full((8, 128), NEG, jnp.float32), unroll=8)

    def add(i, carry):
        num, den = carry
        weight = pltpu.roll(jnp.exp(recv[i, :, 256:384] - top), 124, 1)
        wide = jnp.concatenate([jnp.broadcast_to(weight[:, t:t + 1], (8, HEAD_DIM)) for t in range(4)], axis=1)
        return num + wide * recv[i, :, 0:256], den + weight * recv[i, :, 256:384]
    num, den = lax.fori_loop(0, CHIPS, add, (jnp.zeros((8, 256), jnp.float32), jnp.zeros((8, 128), jnp.float32)), unroll=8)
    wide = jnp.concatenate([jnp.broadcast_to(den[:, t:t + 1], (8, HEAD_DIM)) for t in range(4)], axis=1)
    piece[...] = (num / wide).astype(jnp.bfloat16)

    def glob_slice(src_chip, src_core):
        return glob.at[pl.ds(pl.multiple_of((src_chip % 16) * 8, 8), 8),
                       pl.ds(pl.multiple_of(src_core * HALF + (src_chip // 16) * 256, 256), 256)]

    def glob_copy(src_chip, src_core):
        return pltpu.make_async_remote_copy(
            src_ref=piece, dst_ref=glob_slice(src_chip, src_core), send_sem=g_send,
            recv_sem=g_recv.at[2 * src_chip + src_core], device_id={"seq": 0}, device_id_type=MESH)

    o_copy(1 - core, core).wait_send()
    o_copy(core, 1 - core).wait_recv()

    @pl.when(dev != 0)
    def _():
        copy = glob_copy(chip, core)
        copy.start()
        copy.wait_send()

    @pl.when(dev == 0)
    def _():
        copy = pltpu.make_async_copy(piece, glob_slice(0, 0), loc.at[0])
        copy.start()
        copy.wait()

        def wait_glob(i, carry):
            glob_copy(i // 2, i % 2).wait_recv()
            return carry
        lax.fori_loop(1, 128, wait_glob, 0)
        full_ref[0:128, :] = glob[...]


def combine(part, o):
    return pl.pallas_call(
        combine_kernel,
        out_shape=jax.ShapeDtypeStruct((256, WIDTH), jnp.bfloat16),
        in_specs=[vspec()] * 2, out_specs=vspec(),
        scratch_shapes=[VMEM((CHIPS, 8, 384), jnp.float32), VMEM((128, WIDTH), jnp.bfloat16), VMEM((8, 256), jnp.bfloat16),
                        pltpu.SemaphoreType.DMA, pltpu.SemaphoreType.DMA((CHIPS,)),
                        pltpu.SemaphoreType.DMA, pltpu.SemaphoreType.DMA,
                        pltpu.SemaphoreType.DMA, pltpu.SemaphoreType.DMA((128,)), pltpu.SemaphoreType.DMA((2,))],
        compiler_params=params(), name="combine",
    )(part, o)


def solution(mesh):
    row_spec = P(("batch", "seq"), None)
    rep_spec = P(None, None)

    def local_fn(tokens, w_query, w_key, w_value, w_out, rand_idx):
        dev = lax.axis_index("seq")
        chip, core = dev // 2, dev % 2
        xs = tokens.reshape(4, BLK, 16, 128).transpose(1, 0, 2, 3).reshape(BLK, 64, 128)
        idx = jnp.pad(rand_idx.reshape(1, 12), ((0, 0), (0, 116)))
        recv, xc, idx_all = scatter_rows(xs, tokens.reshape(4, BLK, WIDTH), idx)

        ids = idx_all[:, 0, :12]
        blocks = jnp.arange(512, dtype=jnp.int32)
        present = jnp.any(ids.reshape(-1, 1) == blocks[None, :], axis=0)
        rank = jnp.sum(jnp.where((blocks[None, :] < blocks[:, None]) & present[None, :], 1, 0), axis=1)
        hot_ids = jnp.sum(jnp.where((rank[None, :] == jnp.arange(HOT)[:, None]) & present[None, :], blocks[None, :], 0), axis=1)
        pub = jnp.concatenate([jnp.arange(GLOBAL_BLOCKS), hot_ids, jnp.zeros((2,), jnp.int32)]).astype(jnp.int32)
        sel = jnp.take(recv.reshape(256, WIDTH), (pub // 8) * 4 + pub % 4, axis=0)
        sel = jnp.where((((pub // 4) % 2 == core) & (jnp.arange(SLOTS) < 14))[:, None], sel, jnp.zeros_like(sel))
        near = lax.dynamic_slice_in_dim(ids, 2 * chip, 2).reshape(8, 3)
        below = jnp.sum(jnp.where(hot_ids[None, None, :] < near[:, :, None], 1, 0), axis=2)
        own = chip * 8 + jnp.arange(8)
        info = jnp.concatenate([(GLOBAL_BLOCKS + below).reshape(24), jnp.zeros((8,), jnp.int32),
                                (own - 1 < GLOBAL_BLOCKS).astype(jnp.int32), (own + 1 >= 512).astype(jnp.int32)]).astype(jnp.int32)

        q, k, v = project_rows(core.reshape(1), xc.reshape(640, WIDTH), w_query, w_key, w_value)
        g = gather_rows(sel, w_query, w_key, w_value)
        o, part = attention(info, q, k, v, g.reshape(CHIPS * SLOTS, WIDTH))
        full = combine(part, o)
        out = lax.dot_general(full, w_out, (((1,), (1,)), ((), ())), preferred_element_type=jnp.float32)
        return out.astype(jnp.bfloat16)

    return jax.shard_map(local_fn, mesh=mesh, in_specs=(row_spec, rep_spec, rep_spec, rep_spec, rep_spec, row_spec), out_specs=row_spec, check_vma=False)
```

time: 564 us -> 189 us (0.34); the launches traced: 554 us -> 189 us
  Pallas kernels: 0 us -> 171 us
  waiting for transfers between devices: 146 us -> 0 us
  local copies, waits for them, and re-layouts: 112 us -> 7.72 us
  blocking collectives: 102 us -> 0 us
  matrix products: 97.1 us -> 7.05 us
  other arithmetic: 64.1 us -> 2.51 us
  between operations: 14.1 us -> 0.08 us
  starting transfers between devices: 9.22 us -> 0 us
  loops' own time: 9 us -> 0 us
    pallas_call x0 -> x5, Pallas kernels: none -> 171 us  [the longest x1 46.4 us: gather_rows(): pl.pallas_call(gather_kernel, out_shape=jax.ShapeDtypeStruct((4, 4, 4, SL...]
    psum x2 -> x0, waiting for transfers between devices: 146 us -> none  [the longest x1 146 us: local_fn(): lax.psum((publish(q_blocks, GLOBAL_BLOCKS), publish(k_blocks, pub_slots),...]
    dot_general x17 -> x1, matrix products: 97.1 us -> 7.05 us  [local_fn(): lax.dot_general(full, w_out, (((1,), (1,)), ((), ())), preferred_element_...]
    psum x1 -> x0, blocking collectives: 64.2 us -> none  [local_fn(): glob_sum, glob_num = lax.psum((jnp.sum(glob_exp, axis=-1), part_num), 'seq')]
    reshape x15 -> x3, local copies, waits for them, and re-layouts: 48.9 us -> 3.57 us  [the longest x1 1.51 us: local_fn(): sel = jnp.take(recv.reshape(256, WIDTH), pub // 8 * 4 + pub % 4, axis=0)]
    all_gather x1 -> x0, blocking collectives: 37.8 us -> none  [local_fn(): idx_all = lax.all_gather(rand_idx, 'seq', tiled=True)]
    sub x4 -> x0, other arithmetic: 26.3 us -> none  [block_attention(): attn_probs = jax.nn.softmax(scores, axis=-1).astype(jnp.bfloat16)]
    gather x10 -> x1, local copies, waits for them, and re-layouts: 26.7 us -> 0.6 us  [local_fn(): sel = jnp.take(recv.reshape(256, WIDTH), pub // 8 * 4 + pub % 4, axis=0)]
  transfers between devices with their start and end apart: 6 -> 0, of which waited for: 1 -> 0; matrix products, arithmetic and copies ran while one was open for 40% -> 0% of each run, Pallas kernels for 0% -> 0%
where the time goes in v1:
time: 189 us
  Pallas kernels  171 us (90%)
  local copies, waits for them, and re-layouts  7.72 us (4%)
  matrix products  7.05 us (4%)
  other arithmetic  2.51 us (1%)
    pallas_call x1, Pallas kernels, gather_rows(): pl.pallas_call(gather_kernel, out_shape=jax.ShapeDtypeStruct((4, 4, 4, SL...  46.4 us
    pallas_call x1, Pallas kernels, scatter_rows(): pl.pallas_call(scatter_kernel, out_shape=(jax.ShapeDtypeStruct((CHIPS, BL...  42.8 us
    pallas_call x1, Pallas kernels, attention(): pl.pallas_call(attention_kernel, grid_spec=pltpu.PrefetchScalarGridSpec(n...  37.2 us
    pallas_call x1, Pallas kernels, combine(): pl.pallas_call(combine_kernel, out_shape=jax.ShapeDtypeStruct((256, WIDTH...  32.7 us
    pallas_call x1, Pallas kernels, project_rows(): pl.pallas_call(project_kernel, grid_spec=pltpu.PrefetchScalarGridSpec(num...  12.3 us
    dot_general x1, matrix products, local_fn(): lax.dot_general(full, w_out, (((1,), (1,)), ((), ())), preferred_element_...  7.05 us

profile of v1, /device:TPU:0, one launch (start us, length us, event | category | flops | bytes accessed | tf_op | source)
XLA Modules:
  0.0 188.8 jit_solution(15760681497048513876)
XLA Ops:
  0.0 0.8 reshape.317
  0.8 0.6 pad.4.idx_ref
  1.4 1.5 copy.12
  2.8 1.3 copy.9
  4.1 42.8 %scatter_rows.1 = (bf16[64,64,128]{2,1,0:T(8,128)(2,1)}, bf16[10,64,2048]{2,1,0:T(8,128)(2,1)}, s32[128,1,128]{2,1,0:T(1,128)}) custom-call(bf16[64,64,128]{2,1,0:T(8,128)(2,1)} %bitcast.24, bf16[4,64,2048]{2,1,0:T(8,128)(2,1)} %bitcast.23, s32[1,128]{1,0:T(1,128)} %pad.4.idx_ref), custom_call_target="tpu_custom_call" | custom-call | tf_op jit(solution)/shard_map/scatter_rows/pallas_call | solution.py:101
  46.9 1.0 slice_reduce_fusion
  48.0 0.1 eq.43
  48.1 0.5 fusion
  48.6 0.1 select_reduce_fusion
  48.7 0.1 select_reduce_fusion.1
  48.9 0.1 fusion.7
  49.0 0.1 compare_and_fusion.1
  49.1 0.1 lt.79
  49.2 0.1 copy.10
  49.2 0.2 select_reduce_fusion.2
  49.5 0.1 copy.11
  49.5 0.1 add.98
  49.6 0.6 pad_add_fusion.1.info_ref
  50.3 1.5 reshape.320
  51.8 0.6 gather_fusion
  52.4 0.7 select_select_fusion.sel_ref
  53.1 12.3 %project_rows.1 = (bf16[512,1024]{1,0:T(8,128)(2,1)}, bf16[640,1024]{1,0:T(8,128)(2,1)}, bf16[640,1024]{1,0:T(8,128)(2,1)}) custom-call(s32[1]{0:T(128)} %bitcast.3.core_ref, bf16[640,2048]{1,0:T(8,128)(2,1)} %bitcast.27, bf16[2048,2048]{1,0:T(8,128)(2,1)} %wq_ref.3, bf16[2048,2048]{1,0:T(8,128)(2,1)} %wk_ref.3, bf16[2048,2048]{1,0:T(8,128)(2,1)} %wv_ref.3), custom_call_target="tpu_custom_call" | custom-call | flops 7516192768 | bytes 20971520 | tf_op jit(solution)/shard_map/project_rows/pallas_call | solution.py:125
  65.4 46.4 %gather_rows.1 = bf16[4,4,4,16,2048]{4,3,2,1,0:T(8,128)(2,1)} custom-call(bf16[16,2048]{1,0:T(8,128)(2,1)} %select_select_fusion.sel_ref, bf16[2048,2048]{1,0:T(8,128)(2,1)} %wq_ref.3, bf16[2048,2048]{1,0:T(8,128)(2,1)} %wk_ref.3, bf16[2048,2048]{1,0:T(8,128)(2,1)} %wv_ref.3), custom_call_target="tpu_custom_call" | custom-call | tf_op jit(solution)/shard_map/gather_rows/pallas_call | solution.py:207
  111.8 37.2 %attention.1 = (bf16[512,1024]{1,0:T(8,128)(2,1)}, f32[128,1536]{1,0:T(8,128)}) custom-call(s32[48]{0:T(128)} %pad_add_fusion.1.info_ref, bf16[512,1024]{1,0:T(8,128)(2,1)} %get-tuple-element.15.q_ref, bf16[640,1024]{1,0:T(8,128)(2,1)} %get-tuple-element.16.k_ref, bf16[640,1024]{1,0:T(8,128)(2,1)} %get-tuple-element.17.v_ref, bf16[1024,2048]{1,0:T(8,128)(2,1)} %bitcast.21), custom_call_target="tpu_custom_call" | custom-call | flops 2147483648 | bytes 16777216 | tf_op jit(solution)/shard_map/attention/pallas_call | solution.py:293
  149.0 32.7 %combine.1 = bf16[256,2048]{1,0:T(8,128)(2,1)} custom-call(f32[128,1536]{1,0:T(8,128)} %get-tuple-element.19.part_ref, bf16[512,1024]{1,0:T(8,128)(2,1)} %get-tuple-element.20.o_ref), custom_call_target="tpu_custom_call" | custom-call | tf_op jit(solution)/shard_map/combine/pallas_call | solution.py:383
  181.7 7.1 %convolution_convert_fusion = bf16[256,2048]{1,0:T(8,128)(2,1)} fusion(bf16[256,2048]{1,0:T(8,128)(2,1)} %combine.1, bf16[2048,2048]{1,0:T(8,128)(2,1)} %param.10), kind=kOutput, calls=%fused_computation.3 | convolution fusion | flops 2148007936 | bytes 10485760 | tf_op jit(solution)/shard_map/dot_general | solution.py:424
  (9 shorter events, 0.1 us)

commit v2 on v1

v2 whole, which is shorter than its diff:
```python
import jax
import jax.numpy as jnp
from jax import lax
from jax.experimental import pallas as pl
from jax.experimental.pallas import tpu as pltpu
from jax.sharding import PartitionSpec as P

HEAD_DIM = 64
GLOBAL_BLOCKS = 2
HOT = 12
SLOTS = 16
BLK = 64
WIDTH = 2048
HALF = 1024
CHIPS = 64
NEG = -1e30
MESH = pl.DeviceIdType.MESH
VMEM = pltpu.VMEM
ANY = pl.ANY
PARTS = ((0, 768, (0, 1, 2)), (768, 640, (1, 2, 0)), (1408, 640, (2, 0, 1)))


def permutation():
    row = lax.broadcasted_iota(jnp.int32, (256, 256), 0)
    col = lax.broadcasted_iota(jnp.int32, (256, 256), 1)
    return jnp.where(col == (row & 15) * 16 + (row >> 4), 1.0, 0.0).astype(jnp.bfloat16)


def vspec():
    return pl.BlockSpec(memory_space=VMEM)


def params(effects=True, mib=60):
    return pltpu.CompilerParams(has_side_effects=effects, vmem_limit_bytes=mib * 1024 * 1024)


def where_am_i():
    dev = lax.axis_index("seq")
    return dev, dev // 2, dev % 2


def front_kernel(xs_ref, x_ref, idx_ref, wq_ref, wk_ref, wv_ref,
                 q_ref, k_ref, v_ref, g_ref, hot_ref, idxall_ref,
                 xc, recv, w_buf, sel, other,
                 s_send, s_recv, i_send, i_recv, x_sem, h_send, h_recv, loc, w_sem, p_sem, g_send, g_recv):
    dev, chip, core = where_am_i()
    partner = dev + 1 - 2 * core
    cx, cy, cz = chip % 4, (chip // 4) % 4, chip // 16

    def rows64(i):
        return pl.ds(pl.multiple_of(i * BLK, BLK), BLK)

    def row_copy(dst_chip, slot):
        return pltpu.make_async_remote_copy(
            src_ref=xs_ref.at[dst_chip], dst_ref=recv.at[pl.ds(4 * slot, 4)], send_sem=s_send, recv_sem=s_recv.at[slot],
            device_id={"seq": 2 * dst_chip + core}, device_id_type=MESH)

    def idx_copy(dst_chip, slot):
        return pltpu.make_async_remote_copy(
            src_ref=idx_ref, dst_ref=idxall_ref.at[core, slot], send_sem=i_send.at[0], recv_sem=i_recv.at[slot],
            device_id={"seq": 2 * dst_chip + core}, device_id_type=MESH)

    def idx_swap(which):
        return pltpu.make_async_remote_copy(
            src_ref=idxall_ref.at[core], dst_ref=idxall_ref.at[which], send_sem=i_send.at[1], recv_sem=i_send.at[2],
            device_id={"seq": partner}, device_id_type=MESH)

    def x_swap(which):
        return pltpu.make_async_remote_copy(
            src_ref=x_ref, dst_ref=xc.at[pl.ds(pl.multiple_of(BLK + 256 * which, BLK), 256)],
            send_sem=x_sem.at[0], recv_sem=x_sem.at[1], device_id={"seq": partner}, device_id_type=MESH)

    x_swap(core).start()
    nbr = lax.rem(chip + 2 * core - 1 + CHIPS, CHIPS)

    def halo(dst_core, side):
        return pltpu.make_async_remote_copy(
            src_ref=x_ref.at[rows64(3 * core)], dst_ref=xc.at[rows64(9 * side)],
            send_sem=h_send.at[dst_core], recv_sem=h_recv.at[side],
            device_id={"seq": 2 * nbr + dst_core}, device_id_type=MESH)
    for t in range(2):
        halo(t, 1 - core).start()

    def start_idx(i, carry):
        idx_copy(chip ^ i, chip).start()
        return carry
    lax.fori_loop(1, CHIPS, start_idx, 0)

    def start_row(i, carry):
        row_copy(chip ^ i, chip).start()
        return carry
    lax.fori_loop(1, CHIPS, start_row, 0)

    def w_copy(i, t):
        w = (wq_ref, wk_ref, wv_ref)[i]
        return pltpu.make_async_copy(
            w.at[:, pl.ds(pl.multiple_of(core * HALF + t * 256, 256), 256)],
            w_buf.at[i, :, pl.ds(pl.multiple_of(t * 256, 256), 256)], w_sem.at[i, t])
    for t in range(4):
        for i in range(3):
            w_copy(i, t).start()

    locs = [pltpu.make_async_copy(xs_ref.at[chip], recv.at[pl.ds(4 * chip, 4)], loc.at[0]),
            pltpu.make_async_copy(x_ref, xc.at[pl.ds(pl.multiple_of(BLK + 256 * core, BLK), 256)], loc.at[1]),
            pltpu.make_async_copy(idx_ref, idxall_ref.at[core, chip], loc.at[2])]
    for l in locs:
        l.start()
    for l in locs:
        l.wait()
    x_swap(core).wait_send()
    x_swap(1 - core).wait_recv()
    for t in range(2):
        halo(t, 1 - core).wait_send()
        halo(t, t).wait_recv()

    def project(t, carry):
        cols = pl.ds(pl.multiple_of(t * 256, 256), 256)
        for i in range(3):
            w_copy(i, t).wait()
        q_ref[:, cols] = jnp.dot(xc[BLK:9 * BLK, :], w_buf[0, :, cols], preferred_element_type=jnp.float32).astype(jnp.bfloat16)
        k_ref[:, cols] = jnp.dot(xc[...], w_buf[1, :, cols], preferred_element_type=jnp.float32).astype(jnp.bfloat16)
        v_ref[:, cols] = jnp.dot(xc[...], w_buf[2, :, cols], preferred_element_type=jnp.float32).astype(jnp.bfloat16)
        return carry
    lax.fori_loop(0, 4, project, 0)

    def wait_idx(i, carry):
        idx_copy(chip ^ i, chip ^ i).wait()
        return carry
    lax.fori_loop(1, CHIPS, wait_idx, 0)
    idx_swap(core).start()
    idx_swap(core).wait_send()
    idx_swap(1 - core).wait_recv()
    ids = jnp.concatenate([idxall_ref[0, :, 0, :], idxall_ref[1, :, 0, :]], axis=0)
    ids = jnp.where(lax.broadcasted_iota(jnp.int32, (128, 128), 1) < 12, ids, 1 << 20)
    slot = lax.broadcasted_iota(jnp.int32, (SLOTS, 128), 0)
    names = slot
    published = [jnp.int32(0), jnp.int32(1)]
    for s in range(2, 14):
        h = jnp.min(jnp.where(ids > published[-1], ids, 1 << 20)) if s > 2 else jnp.min(ids)
        published.append(h)
        names = jnp.where(slot == s, h, names)
    hot_ref[...] = names

    def wait_row(i, carry):
        row_copy(chip ^ i, chip ^ i).wait()
        return carry
    lax.fori_loop(1, CHIPS, wait_row, 0)

    for s in range(SLOTS):
        if s < 14:
            h = published[s]
            rows = recv[jnp.minimum((h >> 3) * 4 + (h & 3), 4 * CHIPS - 1)]
            sel[16 * s:16 * s + 16, :] = jnp.where(((h >> 2) & 1) == core, rows, jnp.zeros_like(rows))
        else:
            sel[16 * s:16 * s + 16, :] = jnp.zeros((16, 128), jnp.bfloat16)
    swap = pltpu.make_async_remote_copy(
        src_ref=sel, dst_ref=other, send_sem=p_sem.at[0], recv_sem=p_sem.at[1],
        device_id={"seq": partner}, device_id_type=MESH)
    swap.start()
    swap.wait()
    moved = jnp.dot(permutation(), sel[...] + other[...], preferred_element_type=jnp.float32).astype(jnp.bfloat16)
    rows = jnp.concatenate([moved[16 * j:16 * j + 16] for j in range(16)], axis=1)
    out = [jnp.dot(rows, w_buf[i], preferred_element_type=jnp.float32) for i in range(3)]
    kv = jnp.concatenate([out[1], out[2]], axis=1)
    glob_q = jnp.concatenate([out[0][0:1], out[0][1:2]], axis=1)
    row_id = lax.broadcasted_iota(jnp.int32, (SLOTS, WIDTH), 0)
    kv = jnp.where(row_id == 14, jnp.broadcast_to(glob_q, (SLOTS, WIDTH)), kv)
    g_ref[cz, cy, cx] = kv.astype(jnp.bfloat16)

    coord = (cx, cy, cz)
    scale = (1, 4, 16)

    def block(axes_done, at, cols):
        idx = []
        for axis in (2, 1, 0):
            idx.append(slice(None) if axis in axes_done else at[axis])
        return tuple(idx) + (slice(None), cols)

    def copies(part, stage, receive):
        start, size, order = PARTS[part]
        axis = order[stage]
        out = []
        for k in (1, 2, 3):
            to = lax.rem(coord[axis] + k, 4)
            frm = lax.rem(coord[axis] + 4 - k, 4)
            at = list(coord)
            if receive:
                at[axis] = frm
            ref = g_ref.at[block(order[:stage], at, slice(start, start + size))]
            out.append(pltpu.make_async_remote_copy(
                src_ref=ref, dst_ref=ref, send_sem=g_send.at[part, stage, k - 1], recv_sem=g_recv.at[part, stage, k - 1],
                device_id={"seq": dev + 2 * scale[axis] * (to - coord[axis])}, device_id_type=MESH))
        return out

    for stage in range(3):
        for part in range(3):
            if stage:
                for c in copies(part, stage - 1, True):
                    c.wait_recv()
            for c in copies(part, stage, False):
                c.start()
    for part in range(3):
        for c in copies(part, 2, True):
            c.wait_recv()
    for stage in range(3):
        for part in range(3):
            for c in copies(part, stage, False):
                c.wait_send()


def front(xs, x, idx, wq, wk, wv):
    anyspec = pl.BlockSpec(memory_space=ANY)
    dma = pltpu.SemaphoreType.DMA
    return pl.pallas_call(
        front_kernel,
        out_shape=(jax.ShapeDtypeStruct((512, HALF), jnp.bfloat16),
                   jax.ShapeDtypeStruct((640, HALF), jnp.bfloat16),
                   jax.ShapeDtypeStruct((640, HALF), jnp.bfloat16),
                   jax.ShapeDtypeStruct((4, 4, 4, SLOTS, WIDTH), jnp.bfloat16),
                   jax.ShapeDtypeStruct((SLOTS, 128), jnp.int32),
                   jax.ShapeDtypeStruct((2, CHIPS, 1, 128), jnp.int32)),
        in_specs=[vspec()] * 3 + [anyspec] * 3, out_specs=(vspec(),) * 6,
        scratch_shapes=[VMEM((640, WIDTH), jnp.bfloat16), VMEM((4 * CHIPS, 16, 128), jnp.bfloat16),
                        VMEM((3, WIDTH, HALF), jnp.bfloat16), VMEM((256, 128), jnp.bfloat16), VMEM((256, 128), jnp.bfloat16),
                        dma, dma((CHIPS,)), dma((3,)), dma((CHIPS,)), dma((2,)), dma((2,)), dma((2,)), dma((3,)), dma((3, 4)),
                        dma((2,)), dma((3, 3, 3)), dma((3, 3, 3))],
        compiler_params=params(), name="front",
    )(xs, x, idx, wq, wk, wv)


def split_heads(pair, rows):
    lane = lax.broadcasted_iota(jnp.int32, (rows, 128), 1)
    zero = jnp.zeros_like(pair)
    return jnp.concatenate([jnp.where(lane < HEAD_DIM, pair, zero), jnp.where(lane < HEAD_DIM, zero, pair)], axis=0)


def join_heads(out, rows):
    lane = lax.broadcasted_iota(jnp.int32, (rows, 128), 1)
    return jnp.where(lane < HEAD_DIM, out[:rows], out[rows:])


def back_kernel(info_ref, q_ref, k_ref, v_ref, g_ref, full_ref, hot, o_ref, part_ref, recv, glob, piece,
                c_send, c_recv, o_send, o_recv, g_send, g_recv, loc):
    dev, chip, core = where_am_i()
    nt = (((1,), (1,)), ((), ()))
    perm = permutation()

    def unpack(step, carry):
        z = step // 8
        cols = pl.ds(pl.multiple_of((step % 8) * 256, 256), 256)
        rows = g_ref[pl.ds(pl.multiple_of(z * 256, 256), 256), cols]
        moved = jnp.dot(perm, rows, preferred_element_type=jnp.float32).astype(jnp.bfloat16)
        for s in range(SLOTS):
            hot[s, pl.ds(pl.multiple_of(z * 16, 16), 16), cols] = moved[s * 16:s * 16 + 16]
        return carry
    lax.fori_loop(0, 32, unpack, 0)

    lane = lax.broadcasted_iota(jnp.int32, (128, 128), 1)
    stats = None
    for j in range(8):
        cols = slice(j * 128, j * 128 + 128)
        vcols = slice(HALF + j * 128, HALF + j * 128 + 128)
        gq = jnp.concatenate([hot[14, :, cols], hot[14, :, vcols]], axis=0)
        queries = split_heads(gq, 128) * jnp.bfloat16(0.125)
        scores = lax.dot_general(queries, k_ref[BLK:9 * BLK, cols], nt, preferred_element_type=jnp.float32)
        top = jnp.max(scores, axis=1, keepdims=True)
        probs = jnp.exp(scores - top)
        total = jnp.sum(probs, axis=1, keepdims=True)
        out = jnp.dot(probs.astype(jnp.bfloat16), v_ref[BLK:9 * BLK, cols], preferred_element_type=jnp.float32)
        g, t = j // 2, 2 * (j % 2)
        part_ref[:, 384 * g + 64 * t:384 * g + 64 * t + 128] = join_heads(out, 128)
        if t == 0:
            stats = jnp.zeros((128, 128), jnp.float32)
        for h in range(2):
            rows = slice(128 * h, 128 * h + 128)
            stats = jnp.where(lane == t + h, total[rows], stats)
            stats = jnp.where(lane == 4 + t + h, top[rows], stats)
        if t:
            part_ref[:, 384 * g + 256:384 * g + 384] = stats

    def part_copy(dst_chip, slot):
        rows = pl.ds(pl.multiple_of((dst_chip % 16) * 8, 8), 8)
        cols = pl.ds(pl.multiple_of((dst_chip // 16) * 384, 128), 384)
        return pltpu.make_async_remote_copy(
            src_ref=part_ref.at[rows, cols], dst_ref=recv.at[slot], send_sem=c_send, recv_sem=c_recv.at[slot],
            device_id={"seq": 2 * dst_chip + core}, device_id_type=MESH)

    def start(i, carry):
        part_copy(chip ^ i, chip).start()
        return carry
    lax.fori_loop(1, CHIPS, start, 0)

    def o_copy(rows_of, cols_of):
        return pltpu.make_async_remote_copy(
            src_ref=o_ref.at[pl.ds(pl.multiple_of(rows_of * 256, 256), 256)],
            dst_ref=full_ref.at[:, pl.ds(pl.multiple_of(cols_of * HALF, HALF), HALF)],
            send_sem=o_send, recv_sem=o_recv, device_id={"seq": dev + 1 - 2 * core}, device_id_type=MESH)

    def one_block(step, carry):
        b = (step + 4 * (1 - core)) & 7
        slots = [0, 1] + [info_ref[b * 3 + t] for t in range(3)]
        left_bad = info_ref[32 + b]
        right_bad = info_ref[40 + b]
        key = lax.broadcasted_iota(jnp.int32, (1, 256), 1)
        bias = jnp.where((key < BLK) & (left_bad > 0), NEG, 0.0) + jnp.where((key >= 2 * BLK) & (key < 3 * BLK) & (right_bad > 0), NEG, 0.0)
        base = pl.multiple_of(b * BLK, BLK)
        for j in range(8):
            cols = slice(j * 128, j * 128 + 128)
            vcols = slice(HALF + j * 128, HALF + j * 128 + 128)
            queries = split_heads(q_ref[pl.ds(base, BLK), cols], BLK) * jnp.bfloat16(0.125)
            keys = jnp.concatenate([k_ref[pl.ds(base, 3 * BLK), cols]] + [hot[s, :, cols] for s in slots], axis=0)
            vals = jnp.concatenate([v_ref[pl.ds(base, 3 * BLK), cols]] + [hot[s, :, vcols] for s in slots], axis=0)
            scores = lax.dot_general(queries, keys, nt, preferred_element_type=jnp.float32)
            scores = jnp.concatenate([scores[:, :256] + bias, scores[:, 256:]], axis=1)
            top = jnp.max(scores, axis=1, keepdims=True)
            probs = jnp.exp(scores - top)
            probs = probs * (1.0 / jnp.sum(probs, axis=1, keepdims=True))
            out = jnp.dot(probs.astype(jnp.bfloat16), vals, preferred_element_type=jnp.float32)
            o_ref[pl.ds(base, BLK), cols] = join_heads(out, BLK).astype(jnp.bfloat16)
        return carry
    lax.fori_loop(0, 4, one_block, 0)
    o_copy(1 - core, core).start()
    lax.fori_loop(4, 8, one_block, 0)

    mine = [pltpu.make_async_copy(o_ref.at[pl.ds(pl.multiple_of(core * 256, 256), 256)],
                                  full_ref.at[:, pl.ds(pl.multiple_of(core * HALF, HALF), HALF)], loc.at[0]),
            pltpu.make_async_copy(part_ref.at[pl.ds(pl.multiple_of((chip % 16) * 8, 8), 8), pl.ds(pl.multiple_of((chip // 16) * 384, 128), 384)],
                                  recv.at[chip], loc.at[1])]
    for m in mine:
        m.start()
    for m in mine:
        m.wait()

    def wait(i, carry):
        part_copy(chip ^ i, chip ^ i).wait()
        return carry
    lax.fori_loop(1, CHIPS, wait, 0)

    top = lax.fori_loop(0, CHIPS, lambda i, t: jnp.maximum(t, recv[i, :, 256:384]), jnp.full((8, 128), NEG, jnp.float32), unroll=8)

    def add(i, carry):
        num, den = carry
        weight = pltpu.roll(jnp.exp(recv[i, :, 256:384] - top), 124, 1)
        wide = jnp.concatenate([jnp.broadcast_to(weight[:, t:t + 1], (8, HEAD_DIM)) for t in range(4)], axis=1)
        return num + wide * recv[i, :, 0:256], den + weight * recv[i, :, 256:384]
    num, den = lax.fori_loop(0, CHIPS, add, (jnp.zeros((8, 256), jnp.float32), jnp.zeros((8, 128), jnp.float32)), unroll=8)
    wide = jnp.concatenate([jnp.broadcast_to(den[:, t:t + 1], (8, HEAD_DIM)) for t in range(4)], axis=1)
    piece[...] = (num / wide).astype(jnp.bfloat16)

    def glob_slice(src_chip, src_core):
        return glob.at[pl.ds(pl.multiple_of((src_chip % 16) * 8, 8), 8),
                       pl.ds(pl.multiple_of(src_core * HALF + (src_chip // 16) * 256, 256), 256)]

    def glob_copy(src_chip, src_core):
        return pltpu.make_async_remote_copy(
            src_ref=piece, dst_ref=glob_slice(src_chip, src_core), send_sem=g_send,
            recv_sem=g_recv.at[2 * src_chip + src_core], device_id={"seq": 0}, device_id_type=MESH)

    o_copy(1 - core, core).wait_send()
    o_copy(core, 1 - core).wait_recv()

    @pl.when(dev != 0)
    def _():
        copy = glob_copy(chip, core)
        copy.start()
        copy.wait_send()

    @pl.when(dev == 0)
    def _():
        copy = pltpu.make_async_copy(piece, glob_slice(0, 0), loc.at[0])
        copy.start()
        copy.wait()

        def wait_glob(i, carry):
            glob_copy(i // 2, i % 2).wait_recv()
            return carry
        lax.fori_loop(1, 128, wait_glob, 0)
        full_ref[0:128, :] = glob[...]


def back(info, q, k, v, g):
    dma = pltpu.SemaphoreType.DMA
    return pl.pallas_call(
        back_kernel,
        out_shape=jax.ShapeDtypeStruct((256, WIDTH), jnp.bfloat16),
        in_specs=[pl.BlockSpec(memory_space=pltpu.SMEM)] + [vspec()] * 4, out_specs=vspec(),
        scratch_shapes=[VMEM((SLOTS, BLK, WIDTH), jnp.bfloat16), VMEM((512, HALF), jnp.bfloat16), VMEM((128, 1536), jnp.float32),
                        VMEM((CHIPS, 8, 384), jnp.float32), VMEM((128, WIDTH), jnp.bfloat16), VMEM((8, 256), jnp.bfloat16),
                        dma, dma((CHIPS,)), dma, dma, dma, dma((128,)), dma((2,))],
        compiler_params=params(), name="back",
    )(info, q, k, v, g)


def solution(mesh):
    row_spec = P(("batch", "seq"), None)
    rep_spec = P(None, None)

    def local_fn(tokens, w_query, w_key, w_value, w_out, rand_idx):
        dev = lax.axis_index("seq")
        chip, core = dev // 2, dev % 2
        xs = tokens.reshape(4, BLK, 16, 128).transpose(1, 0, 2, 3)
        idx = jnp.pad(rand_idx.reshape(1, 12), ((0, 0), (0, 116)))
        q, k, v, g, hot_rows, idx_all = front(xs, tokens, idx, w_query, w_key, w_value)
        near = lax.dynamic_slice_in_dim(idx_all[:, :, 0, :12], chip, 1, axis=1).reshape(8, 3)
        hot_ids = hot_rows[2:14, 0]
        below = jnp.sum(jnp.where(hot_ids[None, None, :] < near[:, :, None], 1, 0), axis=2)
        own = chip * 8 + jnp.arange(8)
        info = jnp.concatenate([(GLOBAL_BLOCKS + below).reshape(24), jnp.zeros((8,), jnp.int32),
                                (own - 1 < GLOBAL_BLOCKS).astype(jnp.int32), (own + 1 >= 512).astype(jnp.int32)]).astype(jnp.int32)
        full = back(info, q, k, v, g.reshape(CHIPS * SLOTS, WIDTH))
        out = lax.dot_general(full, w_out, (((1,), (1,)), ((), ())), preferred_element_type=jnp.float32)
        return out.astype(jnp.bfloat16)

    return jax.shard_map(local_fn, mesh=mesh, in_specs=(row_spec, rep_spec, rep_spec, rep_spec, rep_spec, row_spec), out_specs=row_spec, check_vma=False)
```

time: 189 us -> 161 us (0.85)
  Pallas kernels: 171 us -> 147 us
    pallas_call x5 -> x2, Pallas kernels: 171 us -> 147 us  [the longest x1 86.4 us: front(): pl.pallas_call(front_kernel, out_shape=(jax.ShapeDtypeStruct((512, HALF),...]
    reshape x2 -> x0, local copies, waits for them, and re-layouts: 2.81 us -> none  [the longest x1 1.51 us: local_fn(): sel = jnp.take(recv.reshape(256, WIDTH), pub // 8 * 4 + pub % 4, axis=0)]
where the time goes in v2:
time: 161 us
  Pallas kernels  147 us (91%)
  matrix products  7.05 us (4%)
  local copies, waits for them, and re-layouts  5.86 us (4%)
    pallas_call x1, Pallas kernels, front(): pl.pallas_call(front_kernel, out_shape=(jax.ShapeDtypeStruct((512, HALF),...  86.4 us
    pallas_call x1, Pallas kernels, back(): pl.pallas_call(back_kernel, out_shape=jax.ShapeDtypeStruct((256, WIDTH),...  60.4 us
    dot_general x1, matrix products, local_fn(): lax.dot_general(full, w_out, (((1,), (1,)), ((), ())), preferred_element_...  7.05 us

profile of v2, /device:TPU:0, one launch (start us, length us, event | category | flops | bytes accessed | tf_op | source)
XLA Modules:
  0.0 160.6 jit_solution(12426550925661727670)
XLA Ops:
  0.0 1.4 copy.11
  1.5 1.3 copy_bitcast_fusion.xs_ref
  2.8 0.8 reshape.18
  3.5 0.5 pad.4.idx_ref
  4.1 86.4 %front.1 = (bf16[512,1024]{1,0:T(8,128)(2,1)}, bf16[640,1024]{1,0:T(8,128)(2,1)}, bf16[640,1024]{1,0:T(8,128)(2,1)}, bf16[4,4,4,16,2048]{4,3,2,1,0:T(8,128)(2,1)...) custom-call(bf16[64,4,16,128]{3,2,1,0:T(8,128)(2,1)} %copy_bitcast_fusion.xs_ref, bf16[256,2048]{1,0:T(8,128)(2,1)} %x_ref.1, ...), custom_call_target="tpu_custom_call" | custom-call | tf_op jit(solution)/shard_map/front/pallas_call | solution.py:214
  90.5 0.7 dynamic-slice_reduce_fusion
  91.2 0.1 lt.26
  91.2 0.1 copy.9
  91.3 0.8 slice_reduce_fusion
  92.1 0.2 select_reduce_fusion
  92.4 0.1 copy.10
  92.5 0.1 add.25
  92.6 0.6 pad_add_fusion.info_ref
  93.1 60.4 %back.1 = bf16[256,2048]{1,0:T(8,128)(2,1)} custom-call(s32[48]{0:T(128)} %pad_add_fusion.info_ref, bf16[512,1024]{1,0:T(8,128)(2,1)} %get-tuple-element.13.q_ref, bf16[640,1024]{1,0:T(8,128)(2,1)} %get-tuple-element.14.k_ref, bf16[640,1024]{1,0:T(8,128)(2,1)} %get-tuple-element.15.v_ref, bf16[1024,2048]{1,0:T(8,128)(2,1)} %bitcast.14), custom_call_target="tpu_custom_call" | custom-call | tf_op jit(solution)/shard_map/back/pallas_call | solution.py:383
  153.5 7.1 %convolution_convert_fusion = bf16[256,2048]{1,0:T(8,128)(2,1)} fusion(bf16[256,2048]{1,0:T(8,128)(2,1)} %back.1, bf16[2048,2048]{1,0:T(8,128)(2,1)} %param.10), kind=kOutput, calls=%fused_computation | convolution fusion | flops 2148007936 | bytes 10485760 | tf_op jit(solution)/shard_map/dot_general | solution.py:411
  (3 shorter events, 0.0 us)

commit v3 on v0

v3 whole, which is shorter than its diff:
```python
import jax
import jax.numpy as jnp
from jax import lax
from jax.experimental import pallas as pl
from jax.experimental.pallas import tpu as pltpu
from jax.sharding import PartitionSpec as P

HEAD_DIM = 64
BLK = 64
SLOTS = 16
WIDTH = 2048
HALF = 1024
CHIPS = 64
PAIRS = 8
NEG = -1e30
FAR = 1 << 20
MESH = pl.DeviceIdType.MESH
VMEM = pltpu.VMEM
ORDERS = ((0, 1, 2), (1, 2, 0), (2, 0, 1))
NT = (((1,), (1,)), ((), ()))


def permutation():
    row = lax.broadcasted_iota(jnp.int32, (256, 256), 0)
    col = lax.broadcasted_iota(jnp.int32, (256, 256), 1)
    return jnp.where(col == (row & 15) * 16 + (row >> 4), 1.0, 0.0).astype(jnp.bfloat16)


def split_heads(pair, rows):
    lane = lax.broadcasted_iota(jnp.int32, (rows, 128), 1)
    zero = jnp.zeros_like(pair)
    return jnp.concatenate([jnp.where(lane < HEAD_DIM, pair, zero), jnp.where(lane < HEAD_DIM, zero, pair)], axis=0)


def join_heads(out, rows):
    lane = lax.broadcasted_iota(jnp.int32, (rows, 128), 1)
    return jnp.where(lane < HEAD_DIM, out[:rows], out[rows:])


def aligned(i, n):
    return pl.ds(pl.multiple_of(i * n, n), n)


def remote(src, dst, send, recv, dev):
    return pltpu.make_async_remote_copy(src_ref=src, dst_ref=dst, send_sem=send, recv_sem=recv,
                                        device_id={"seq": dev}, device_id_type=MESH)


def kernel(x_ref, idx_ref, wq_ref, wk_ref, wv_ref, full_ref,
           xs, xc, recv, w_buf, idx_all, sel, other, q_ref, k_ref, v_ref, gath, hot, o_ref, part, parts, glob, piece, near_s, slot_s,
           s_send, s_recv, i_send, i_recv, x_sem, h_send, h_recv, loc, w_sem, p_sem, g_send, g_recv,
           c_send, c_recv, o_send, o_recv, e_send, e_recv):
    dev = lax.axis_index("seq")
    chip, core = dev // 2, dev % 2
    partner = dev + 1 - 2 * core
    coord = (chip % 4, (chip // 4) % 4, chip // 16)
    scale = (1, 4, 16)
    perm = permutation()

    def w_copy(i, t):
        w = (wq_ref, wk_ref, wv_ref)[i]
        return pltpu.make_async_copy(w.at[:, aligned(core * 4 + t, 256)], w_buf.at[i, :, aligned(t, 256)], w_sem.at[i, t])

    def x_swap(which):
        return remote(x_ref, xc.at[pl.ds(pl.multiple_of(BLK + 256 * which, BLK), 256)], x_sem.at[0], x_sem.at[1], partner)

    def idx_copy(dst_chip, slot):
        return remote(idx_ref, idx_all.at[core, slot], i_send.at[0], i_recv.at[slot], 2 * dst_chip + core)

    def idx_swap(which):
        return remote(idx_all.at[core], idx_all.at[which], i_send.at[1], i_send.at[2], partner)

    def row_copy(dst_chip, slot):
        return remote(xs.at[dst_chip], recv.at[pl.ds(4 * slot, 4)], s_send, s_recv.at[slot], 2 * dst_chip + core)

    nbr = lax.rem(chip + 2 * core - 1 + CHIPS, CHIPS)

    def halo(dst_core, side):
        return remote(x_ref.at[aligned(3 * core, BLK)], xc.at[aligned(9 * side, BLK)], h_send.at[dst_core], h_recv.at[side],
                      2 * nbr + dst_core)

    with jax.named_scope("issue"):
        x_swap(core).start()
        for t in range(4):
            for i in range(3):
                w_copy(i, t).start()
        locs = [pltpu.make_async_copy(x_ref, xc.at[pl.ds(pl.multiple_of(BLK + 256 * core, BLK), 256)], loc.at[1]),
                pltpu.make_async_copy(idx_ref, idx_all.at[core, chip], loc.at[2])]
        for l in locs:
            l.start()

        def start_idx(i, carry):
            idx_copy(chip ^ i, chip).start()
            return carry
        lax.fori_loop(1, CHIPS, start_idx, 0, unroll=7)

    def relayout(step, carry):
        blk, group = step >> 2, step & 3
        rows = x_ref[aligned(step, 16), :]
        rows = jnp.concatenate([rows[:, 128 * c:128 * c + 128] for c in range(16)], axis=0)
        moved = jnp.dot(perm, rows, preferred_element_type=jnp.float32).astype(jnp.bfloat16)
        for a in range(16):
            xs[16 * group + a, blk] = moved[16 * a:16 * a + 16]
        return carry
    with jax.named_scope("relayout"):
        lax.fori_loop(0, 16, relayout, 0)

    def start_row(i, carry):
        row_copy(chip ^ i, chip).start()
        return carry
    with jax.named_scope("issue_rows"):
        lax.fori_loop(1, CHIPS, start_row, 0, unroll=7)
        own_row = pltpu.make_async_copy(xs.at[chip], recv.at[pl.ds(4 * chip, 4)], loc.at[0])
        own_row.start()
        for t in range(2):
            halo(t, 1 - core).start()

    with jax.named_scope("wait_x"):
        for l in locs:
            l.wait()
        x_swap(core).wait_send()
        x_swap(1 - core).wait_recv()

    def project(t, carry):
        cols = aligned(t, 256)
        for i in range(3):
            w_copy(i, t).wait()
        rows = xc[BLK:9 * BLK, :]
        q_ref[:, cols] = jnp.dot(rows, w_buf[0, :, cols], preferred_element_type=jnp.float32).astype(jnp.bfloat16)
        k_ref[BLK:9 * BLK, cols] = jnp.dot(rows, w_buf[1, :, cols], preferred_element_type=jnp.float32).astype(jnp.bfloat16)
        v_ref[BLK:9 * BLK, cols] = jnp.dot(rows, w_buf[2, :, cols], preferred_element_type=jnp.float32).astype(jnp.bfloat16)
        return carry
    with jax.named_scope("project"):
        lax.fori_loop(0, 4, project, 0)

    def wait_idx(i, carry):
        idx_copy(chip ^ i, chip ^ i).wait()
        return carry
    with jax.named_scope("wait_idx"):
        lax.fori_loop(1, CHIPS, wait_idx, 0)
        idx_swap(core).start()
        idx_swap(core).wait_send()
        idx_swap(1 - core).wait_recv()
    with jax.named_scope("names"):
        ids = jnp.concatenate([idx_all[0, :, 0, :], idx_all[1, :, 0, :]], axis=0)
        ids = jnp.where(lax.broadcasted_iota(jnp.int32, (128, 128), 1) < 12, ids, FAR)
        published = [jnp.int32(0), jnp.int32(1), jnp.min(ids)]
        for s in range(3, 14):
            published.append(jnp.min(jnp.where(ids > published[-1], ids, FAR)))

    def wait_row(i, carry):
        row_copy(chip ^ i, chip ^ i).wait()
        return carry
    with jax.named_scope("wait_rows"):
        lax.fori_loop(1, CHIPS, wait_row, 0)
        own_row.wait()

    with jax.named_scope("select"):
        for s in range(SLOTS):
            if s < 14:
                h = published[s]
                rows = recv[jnp.minimum((h >> 3) * 4 + (h & 3), 4 * CHIPS - 1)]
                sel[16 * s:16 * s + 16, :] = jnp.where(((h >> 2) & 1) == core, rows, jnp.zeros_like(rows))
            else:
                sel[16 * s:16 * s + 16, :] = jnp.zeros((16, 128), jnp.bfloat16)
        swap = remote(sel, other, p_sem.at[0], p_sem.at[1], partner)
        swap.start()
        swap.wait()
    with jax.named_scope("publish"):
        moved = jnp.dot(perm, sel[...] + other[...], preferred_element_type=jnp.float32).astype(jnp.bfloat16)
        rows = jnp.concatenate([moved[16 * j:16 * j + 16] for j in range(16)], axis=1)
        out = [jnp.dot(rows, w_buf[i], preferred_element_type=jnp.float32) for i in range(3)]
        row_id = lax.broadcasted_iota(jnp.int32, (SLOTS, 256), 0)
        for j in range(PAIRS):
            cols = slice(128 * j, 128 * j + 128)
            kv = jnp.concatenate([out[1][:, cols], out[2][:, cols]], axis=1)
            gq = jnp.concatenate([out[0][0:1, cols], out[0][1:2, cols]], axis=1)
            kv = jnp.where(row_id == 14, jnp.broadcast_to(gq, (SLOTS, 256)), kv)
            gath[j, coord[2], coord[1], coord[0]] = kv.astype(jnp.bfloat16)

    def copies(j, stage, receive):
        order = ORDERS[j % 3]
        axis = order[stage]
        out = []
        for k in (1, 2, 3):
            to = lax.rem(coord[axis] + k, 4)
            at = list(coord)
            if receive:
                at[axis] = lax.rem(coord[axis] + 4 - k, 4)
            ref = gath.at[(j,) + tuple(slice(None) if a in order[:stage] else at[a] for a in (2, 1, 0))]
            out.append(remote(ref, ref, g_send.at[j, stage, k - 1], g_recv.at[j, stage, k - 1],
                              dev + 2 * scale[axis] * (to - coord[axis])))
        return out

    def advance(j, stage):
        if stage:
            for c in copies(j, stage - 1, True):
                c.wait_recv()
        if stage < 3:
            for c in copies(j, stage, False):
                c.start()

    with jax.named_scope("gather0"):
        for j in range(PAIRS):
            advance(j, 0)
    with jax.named_scope("halo"):
        for t in range(2):
            halo(t, 1 - core).wait_send()
            halo(t, t).wait_recv()

        def project_halo(t, carry):
            cols = aligned(t, 256)
            rows = jnp.concatenate([xc[0:BLK, :], xc[9 * BLK:10 * BLK, :]], axis=0)
            for i, ref in ((1, k_ref), (2, v_ref)):
                out = jnp.dot(rows, w_buf[i, :, cols], preferred_element_type=jnp.float32).astype(jnp.bfloat16)
                ref[0:BLK, cols] = out[0:BLK]
                ref[9 * BLK:10 * BLK, cols] = out[BLK:]
            return carry
        lax.fori_loop(0, 4, project_halo, 0)
    with jax.named_scope("gather1"):
        for j in range(PAIRS):
            advance(j, 1)
    with jax.named_scope("gather2"):
        for j in range(PAIRS):
            advance(j, 2)

    with jax.named_scope("slots"):
        near = [pltpu.make_async_copy(idx_all.at[c, chip], near_s.at[c], loc.at[c]) for c in range(2)]
        for n in near:
            n.start()
        for n in near:
            n.wait()
        for b in range(8):
            for t in range(3):
                named = near_s[b // 4, 0, 3 * (b % 4) + t]
                at = jnp.int32(2)
                for h in published[2:]:
                    at = at + jnp.where(h < named, 1, 0)
                slot_s[3 * b + t] = at

    lane = lax.broadcasted_iota(jnp.int32, (128, 128), 1)
    key = lax.broadcasted_iota(jnp.int32, (1, 256), 1)

    def part_copy(wave, i, slot):
        dst_chip = 16 * wave + i
        return remote(part.at[wave, aligned(i, 8)], parts.at[slot], c_send, c_recv.at[slot], 2 * dst_chip + core)

    def o_copy(wave, rows_of, cols_of):
        return remote(o_ref.at[aligned(rows_of, 256), pl.ds(256 * wave, 256)],
                      full_ref.at[:, aligned(cols_of * 4 + wave, 256)], o_send.at[wave], o_recv.at[wave], partner)

    for wave in range(4):
        with jax.named_scope("wait_wave"):
            for j in (2 * wave, 2 * wave + 1):
                advance(j, 3)

        def unpack(z, carry):
            for j in (2 * wave, 2 * wave + 1):
                rows = gath[j, z].reshape(256, 256)
                moved = jnp.dot(perm, rows, preferred_element_type=jnp.float32).astype(jnp.bfloat16)
                for s in range(15):
                    hot[j, s, aligned(z, 16), :] = moved[s * 16:s * 16 + 16]
            return carry
        with jax.named_scope("unpack"):
            lax.fori_loop(0, 4, unpack, 0)

        with jax.named_scope("globpart"):
            stats = jnp.zeros((128, 128), jnp.float32)
            for t, j in enumerate((2 * wave, 2 * wave + 1)):
                cols = slice(128 * j, 128 * j + 128)
                gq = jnp.concatenate([hot[j, 14, :, 0:128], hot[j, 14, :, 128:256]], axis=0)
                queries = split_heads(gq, 128) * jnp.bfloat16(0.125)
                scores = lax.dot_general(queries, k_ref[BLK:9 * BLK, cols], NT, preferred_element_type=jnp.float32)
                top = jnp.max(scores, axis=1, keepdims=True)
                probs = jnp.exp(scores - top)
                total = jnp.sum(probs, axis=1, keepdims=True)
                out = jnp.dot(probs.astype(jnp.bfloat16), v_ref[BLK:9 * BLK, cols], preferred_element_type=jnp.float32)
                part[wave, :, 128 * t:128 * t + 128] = join_heads(out, 128)
                for h in range(2):
                    rows = slice(128 * h, 128 * h + 128)
                    stats = jnp.where(lane == 2 * t + h, total[rows], stats)
                    stats = jnp.where(lane == 4 + 2 * t + h, top[rows], stats)
            part[wave, :, 256:384] = stats

        def start_part(i, carry):
            j = i ^ (chip & 15)

            @pl.when(16 * wave + j != chip)
            def _():
                part_copy(wave, j, chip).start()
            return carry
        with jax.named_scope("issue_parts"):
            lax.fori_loop(0, 16, start_part, 0)

        def one_block(step, carry):
            b = (step + 4 * (1 - core)) & 7
            named = [0, 1] + [slot_s[3 * b + t] for t in range(3)]
            block_id = chip * 8 + b
            bias = (jnp.where((key < BLK) & (block_id - 1 < 2), NEG, 0.0)
                    + jnp.where((key >= 2 * BLK) & (key < 3 * BLK) & (block_id + 1 >= 8 * CHIPS), NEG, 0.0))
            base = pl.multiple_of(b * BLK, BLK)
            for j in (2 * wave, 2 * wave + 1):
                cols = slice(j * 128, j * 128 + 128)
                queries = split_heads(q_ref[pl.ds(base, BLK), cols], BLK) * jnp.bfloat16(0.125)
                keys = jnp.concatenate([k_ref[pl.ds(base, 3 * BLK), cols]] + [hot[j, s, :, 0:128] for s in named], axis=0)
                vals = jnp.concatenate([v_ref[pl.ds(base, 3 * BLK), cols]] + [hot[j, s, :, 128:256] for s in named], axis=0)
                scores = lax.dot_general(queries, keys, NT, preferred_element_type=jnp.float32)
                scores = jnp.concatenate([scores[:, :256] + bias, scores[:, 256:]], axis=1)
                top = jnp.max(scores, axis=1, keepdims=True)
                probs = jnp.exp(scores - top)
                probs = probs * (1.0 / jnp.sum(probs, axis=1, keepdims=True))
                out = jnp.dot(probs.astype(jnp.bfloat16), vals, preferred_element_type=jnp.float32)
                o_ref[pl.ds(base, BLK), cols] = join_heads(out, BLK).astype(jnp.bfloat16)
            return carry
        with jax.named_scope("blocks"):
            lax.fori_loop(0, 8, one_block, 0)
        o_copy(wave, 1 - core, core).start()

    with jax.named_scope("local"):
        mine = [pltpu.make_async_copy(o_ref.at[aligned(core, 256)], full_ref.at[:, aligned(core, HALF)], loc.at[0]),
                pltpu.make_async_copy(part.at[chip >> 4, aligned(chip & 15, 8)], parts.at[chip], loc.at[1])]
        for m in mine:
            m.start()
        for j in range(PAIRS):
            for stage in range(3):
                for c in copies(j, stage, False):
                    c.wait_send()

        for m in mine:
            m.wait()

    def wait_part(i, carry):
        part_copy(chip >> 4, chip & 15, chip ^ i).wait()
        return carry
    with jax.named_scope("wait_parts"):
        lax.fori_loop(1, CHIPS, wait_part, 0)

    with jax.named_scope("combine"):
        top = lax.fori_loop(0, CHIPS, lambda i, t: jnp.maximum(t, parts[i, :, 256:384]), jnp.full((8, 128), NEG, jnp.float32), unroll=8)

        def add(i, carry):
            num, den = carry
            weight = pltpu.roll(jnp.exp(parts[i, :, 256:384] - top), 124, 1)
            wide = jnp.concatenate([jnp.broadcast_to(weight[:, t:t + 1], (8, HEAD_DIM)) for t in range(4)], axis=1)
            return num + wide * parts[i, :, 0:256], den + weight * parts[i, :, 256:384]
        num, den = lax.fori_loop(0, CHIPS, add, (jnp.zeros((8, 256), jnp.float32), jnp.zeros((8, 128), jnp.float32)), unroll=8)
        wide = jnp.concatenate([jnp.broadcast_to(den[:, t:t + 1], (8, HEAD_DIM)) for t in range(4)], axis=1)
        piece[...] = (num / wide).astype(jnp.bfloat16)

    def glob_slice(src_chip, src_core):
        return glob.at[aligned(src_chip % 16, 8), aligned(src_core * 4 + src_chip // 16, 256)]

    def glob_copy(src_chip, src_core):
        return remote(piece, glob_slice(src_chip, src_core), e_send, e_recv.at[2 * src_chip + src_core], 0)

    with jax.named_scope("tail"):
        @pl.when(dev != 0)
        def _():
            copy = glob_copy(chip, core)
            copy.start()
            copy.wait_send()

        for wave in range(4):
            o_copy(wave, 1 - core, core).wait_send()
            o_copy(wave, core, 1 - core).wait_recv()

        @pl.when(dev == 0)
        def _():
            copy = pltpu.make_async_copy(piece, glob_slice(0, 0), loc.at[0])
            copy.start()
            copy.wait()

            def wait_glob(i, carry):
                glob_copy(i // 2, i % 2).wait_recv()
                return carry
            lax.fori_loop(1, 128, wait_glob, 0)
            full_ref[0:128, :] = glob[...]


def attend(x, idx, wq, wk, wv):
    vmem = pl.BlockSpec(memory_space=VMEM)
    hbm = pl.BlockSpec(memory_space=pl.ANY)
    dma = pltpu.SemaphoreType.DMA
    bf16, f32 = jnp.bfloat16, jnp.float32
    return pl.pallas_call(
        kernel,
        out_shape=jax.ShapeDtypeStruct((256, WIDTH), bf16),
        in_specs=[vmem, vmem, hbm, hbm, hbm], out_specs=vmem,
        scratch_shapes=[
            VMEM((CHIPS, 4, 16, 128), bf16), VMEM((640, WIDTH), bf16), VMEM((4 * CHIPS, 16, 128), bf16),
            VMEM((3, WIDTH, HALF), bf16), VMEM((2, CHIPS, 1, 128), jnp.int32), VMEM((256, 128), bf16), VMEM((256, 128), bf16),
            VMEM((512, HALF), bf16), VMEM((640, HALF), bf16), VMEM((640, HALF), bf16),
            VMEM((PAIRS, 4, 4, 4, SLOTS, 256), bf16), VMEM((PAIRS, SLOTS, BLK, 256), bf16), VMEM((512, HALF), bf16),
            VMEM((4, 128, 384), f32), VMEM((CHIPS, 8, 384), f32), VMEM((128, WIDTH), bf16), VMEM((8, 256), bf16),
            pltpu.SMEM((2, 1, 128), jnp.int32), pltpu.SMEM((24,), jnp.int32),
            dma, dma((CHIPS,)), dma((3,)), dma((CHIPS,)), dma((2,)), dma((2,)), dma((2,)), dma((3,)), dma((3, 4)), dma((2,)),
            dma((PAIRS, 3, 3)), dma((PAIRS, 3, 3)), dma, dma((CHIPS,)), dma((4,)), dma((4,)), dma, dma((128,))],
        compiler_params=pltpu.CompilerParams(has_side_effects=True, vmem_limit_bytes=62 * 1024 * 1024), name="attend",
    )(x, idx, wq, wk, wv)


def solution(mesh):
    row_spec = P(("batch", "seq"), None)
    rep_spec = P(None, None)

    def local_fn(tokens, w_query, w_key, w_value, w_out, rand_idx):
        idx = jnp.pad(rand_idx.reshape(1, 12), ((0, 0), (0, 116)))
        full = attend(tokens, idx, w_query, w_key, w_value)
        out = lax.dot_general(full, w_out, NT, preferred_element_type=jnp.float32)
        return out.astype(jnp.bfloat16)

    return jax.shard_map(local_fn, mesh=mesh, in_specs=(row_spec, rep_spec, rep_spec, rep_spec, rep_spec, row_spec), out_specs=row_spec, check_vma=False)
```

time: 564 us -> 118 us (0.21); the launches traced: 554 us -> 118 us
  waiting for transfers between devices: 146 us -> 0 us
  local copies, waits for them, and re-layouts: 112 us -> 1.28 us
  Pallas kernels: 0 us -> 110 us
  blocking collectives: 102 us -> 0 us
  matrix products: 97.1 us -> 7.05 us
  other arithmetic: 64.1 us -> 0 us
  between operations: 14.1 us -> 0.01 us
  starting transfers between devices: 9.22 us -> 0 us
  loops' own time: 9 us -> 0 us
    psum x2 -> x0, waiting for transfers between devices: 146 us -> none  [the longest x1 146 us: local_fn(): lax.psum((publish(q_blocks, GLOBAL_BLOCKS), publish(k_blocks, pub_slots),...]
    pallas_call x0 -> x1, Pallas kernels: none -> 110 us  [attend(): pl.pallas_call(kernel, out_shape=jax.ShapeDtypeStruct((256, WIDTH), bf16)...]
    dot_general x17 -> x1, matrix products: 97.1 us -> 7.05 us  [local_fn(): out = lax.dot_general(full, w_out, NT, preferred_element_type=jnp.float32)]
    psum x1 -> x0, blocking collectives: 64.2 us -> none  [local_fn(): glob_sum, glob_num = lax.psum((jnp.sum(glob_exp, axis=-1), part_num), 'seq')]
    reshape x15 -> x1, local copies, waits for them, and re-layouts: 48.9 us -> 0.76 us  [local_fn(): idx = jnp.pad(rand_idx.reshape(1, 12), ((0, 0), (0, 116)))]
    all_gather x1 -> x0, blocking collectives: 37.8 us -> none  [local_fn(): idx_all = lax.all_gather(rand_idx, 'seq', tiled=True)]
    gather x10 -> x0, local copies, waits for them, and re-layouts: 26.7 us -> none  [the longest x4 15.3 us: one_block(): jnp.take(pub_k, pub_row, axis=0)]
    sub x4 -> x0, other arithmetic: 26.3 us -> none  [block_attention(): attn_probs = jax.nn.softmax(scores, axis=-1).astype(jnp.bfloat16)]
  transfers between devices with their start and end apart: 6 -> 0, of which waited for: 1 -> 0; matrix products, arithmetic and copies ran while one was open for 40% -> 0% of each run, Pallas kernels for 0% -> 0%
where the time goes in v3:
time: 118 us
  Pallas kernels  110 us (93%)
  matrix products  7.05 us (6%)
  local copies, waits for them, and re-layouts  1.28 us (1%)
    pallas_call x1, Pallas kernels, attend(): pl.pallas_call(kernel, out_shape=jax.ShapeDtypeStruct((256, WIDTH), bf16)...  110 us
    dot_general x1, matrix products, local_fn(): out = lax.dot_general(full, w_out, NT, preferred_element_type=jnp.float32)  7.05 us

profile of v3, /device:TPU:0, one launch (start us, length us, event | category | flops | bytes accessed | tf_op | source)
XLA Modules:
  0.0 118.2 jit_solution(13947194735857536899)
XLA Ops:
  0.0 0.8 reshape.3
  0.8 0.5 pad.4.idx_ref
  1.3 109.8 %attend.1 = bf16[256,2048]{1,0:T(8,128)(2,1)} custom-call(bf16[256,2048]{1,0:T(8,128)(2,1)} %x_ref.1, s32[1,128]{1,0:T(1,128)} %pad.4.idx_ref, bf16[2048,2048]{1,0:T(8,128)(2,1)} %wq_ref.1, bf16[2048,2048]{1,0:T(8,128)(2,1)} %wk_ref.1, bf16[2048,2048]{1,0:T(8,128)(2,1)} %wv_ref.1), custom_call_target="tpu_custom_call" | custom-call | tf_op jit(solution)/shard_map/attend/pallas_call | solution.py:385
  111.1 7.1 %convolution_convert_fusion = bf16[256,2048]{1,0:T(8,128)(2,1)} fusion(bf16[256,2048]{1,0:T(8,128)(2,1)} %attend.1, bf16[2048,2048]{1,0:T(8,128)(2,1)} %param.10), kind=kOutput, calls=%fused_computation | convolution fusion | flops 2148007936 | bytes 10485760 | tf_op jit(solution)/shard_map/dot_general | solution.py:409

commit v4 on v3

--- a/solution.py
+++ b/solution.py
@@ -46,10 +46,10 @@
                                         device_id={"seq": dev}, device_id_type=MESH)
 
 
-def kernel(x_ref, idx_ref, wq_ref, wk_ref, wv_ref, full_ref,
-           xs, xc, recv, w_buf, idx_all, sel, other, q_ref, k_ref, v_ref, gath, hot, o_ref, part, parts, glob, piece, near_s, slot_s,
+def kernel(x_ref, rand_ref, wq_ref, wk_ref, wv_ref, wo_ref, y_ref,
+           idx_ref, full_ref, wo_buf, xs, xc, recv, w_buf, idx_all, sel, other, q_ref, k_ref, v_ref, gath, hot, o_ref, part, parts, glob, piece, near_s, slot_s,
            s_send, s_recv, i_send, i_recv, x_sem, h_send, h_recv, loc, w_sem, p_sem, g_send, g_recv,
-           c_send, c_recv, o_send, o_recv, e_send, e_recv):
+           c_send, c_recv, o_send, o_recv, e_send, e_recv, wo_sem):
     dev = lax.axis_index("seq")
     chip, core = dev // 2, dev % 2
     partner = dev + 1 - 2 * core
@@ -57,6 +57,14 @@
     scale = (1, 4, 16)
     perm = permutation()
 
+    barrier = pltpu.get_barrier_semaphore()
+
+    def greet(i, carry):
+        pl.semaphore_signal(barrier, inc=1, device_id={"seq": dev ^ i}, device_id_type=MESH)
+        return carry
+    with jax.named_scope("greet"):
+        lax.fori_loop(1, 128, greet, 0, unroll=8)
+
     def w_copy(i, t):
         w = (wq_ref, wk_ref, wv_ref)[i]
         return pltpu.make_async_copy(w.at[:, aligned(core * 4 + t, 256)], w_buf.at[i, :, aligned(t, 256)], w_sem.at[i, t])
@@ -79,20 +87,20 @@
         return remote(x_ref.at[aligned(3 * core, BLK)], xc.at[aligned(9 * side, BLK)], h_send.at[dst_core], h_recv.at[side],
                       2 * nbr + dst_core)
 
+    wo_copy = pltpu.make_async_copy(wo_ref, wo_buf, wo_sem)
+
     with jax.named_scope("issue"):
-        x_swap(core).start()
         for t in range(4):
             for i in range(3):
                 w_copy(i, t).start()
-        locs = [pltpu.make_async_copy(x_ref, xc.at[pl.ds(pl.multiple_of(BLK + 256 * core, BLK), 256)], loc.at[1]),
-                pltpu.make_async_copy(idx_ref, idx_all.at[core, chip], loc.at[2])]
-        for l in locs:
-            l.start()
-
-        def start_idx(i, carry):
-            idx_copy(chip ^ i, chip).start()
-            return carry
-        lax.fori_loop(1, CHIPS, start_idx, 0, unroll=7)
+        own_x = pltpu.make_async_copy(x_ref, xc.at[pl.ds(pl.multiple_of(BLK + 256 * core, BLK), 256)], loc.at[1])
+        own_x.start()
+        named_lane = lax.broadcasted_iota(jnp.int32, (1, 128), 1)
+        line = jnp.full((1, 128), FAR, jnp.int32)
+        for e in range(12):
+            line = jnp.where(named_lane == e, rand_ref[e // 3, e % 3], line)
+        idx_ref[...] = line
+        idx_all[core, chip] = line
 
     def relayout(step, carry):
         blk, group = step >> 2, step & 3
@@ -105,10 +113,18 @@
     with jax.named_scope("relayout"):
         lax.fori_loop(0, 16, relayout, 0)
 
+    def start_idx(i, carry):
+        idx_copy(chip ^ i, chip).start()
+        return carry
+
     def start_row(i, carry):
         row_copy(chip ^ i, chip).start()
         return carry
+    with jax.named_scope("barrier"):
+        pl.semaphore_wait(barrier, 127)
     with jax.named_scope("issue_rows"):
+        x_swap(core).start()
+        lax.fori_loop(1, CHIPS, start_idx, 0, unroll=7)
         lax.fori_loop(1, CHIPS, start_row, 0, unroll=7)
         own_row = pltpu.make_async_copy(xs.at[chip], recv.at[pl.ds(4 * chip, 4)], loc.at[0])
         own_row.start()
@@ -116,8 +132,8 @@
             halo(t, 1 - core).start()
 
     with jax.named_scope("wait_x"):
-        for l in locs:
-            l.wait()
+        own_x.wait()
+        wo_copy.start()
         x_swap(core).wait_send()
         x_swap(1 - core).wait_recv()
 
@@ -143,7 +159,6 @@
         idx_swap(1 - core).wait_recv()
     with jax.named_scope("names"):
         ids = jnp.concatenate([idx_all[0, :, 0, :], idx_all[1, :, 0, :]], axis=0)
-        ids = jnp.where(lax.broadcasted_iota(jnp.int32, (128, 128), 1) < 12, ids, FAR)
         published = [jnp.int32(0), jnp.int32(1), jnp.min(ids)]
         for s in range(3, 14):
             published.append(jnp.min(jnp.where(ids > published[-1], ids, FAR)))
@@ -353,16 +368,32 @@
     def glob_copy(src_chip, src_core):
         return remote(piece, glob_slice(src_chip, src_core), e_send, e_recv.at[2 * src_chip + src_core], 0)
 
+    def project_out(t, carry):
+        cols = aligned(t, 256)
+        y_ref[:, cols] = lax.dot_general(full_ref[...], wo_buf[cols, :], NT, preferred_element_type=jnp.float32).astype(jnp.bfloat16)
+        return carry
+
+    def project_glob(t, carry):
+        cols = aligned(t, 256)
+        y_ref[0:128, cols] = lax.dot_general(glob[...], wo_buf[cols, :], NT, preferred_element_type=jnp.float32).astype(jnp.bfloat16)
+        return carry
+
+    with jax.named_scope("wait_o"):
+        @pl.when(dev != 0)
+        def _():
+            glob_copy(chip, core).start()
+
+        for wave in range(4):
+            o_copy(wave, 1 - core, core).wait_send()
+            o_copy(wave, core, 1 - core).wait_recv()
+        wo_copy.wait()
+    with jax.named_scope("out"):
+        lax.fori_loop(0, 8, project_out, 0)
+
     with jax.named_scope("tail"):
         @pl.when(dev != 0)
         def _():
-            copy = glob_copy(chip, core)
-            copy.start()
-            copy.wait_send()
-
-        for wave in range(4):
-            o_copy(wave, 1 - core, core).wait_send()
-            o_copy(wave, core, 1 - core).wait_recv()
+            glob_copy(chip, core).wait_send()
 
         @pl.when(dev == 0)
         def _():
@@ -374,10 +405,10 @@
                 glob_copy(i // 2, i % 2).wait_recv()
                 return carry
             lax.fori_loop(1, 128, wait_glob, 0)
-            full_ref[0:128, :] = glob[...]
-
-
-def attend(x, idx, wq, wk, wv):
+            lax.fori_loop(0, 8, project_glob, 0)
+
+
+def attend(x, rand_idx, wq, wk, wv, wo):
     vmem = pl.BlockSpec(memory_space=VMEM)
     hbm = pl.BlockSpec(memory_space=pl.ANY)
     dma = pltpu.SemaphoreType.DMA
@@ -385,8 +416,9 @@
     return pl.pallas_call(
         kernel,
         out_shape=jax.ShapeDtypeStruct((256, WIDTH), bf16),
-        in_specs=[vmem, vmem, hbm, hbm, hbm], out_specs=vmem,
+        in_specs=[vmem, pl.BlockSpec(memory_space=pltpu.SMEM), hbm, hbm, hbm, hbm], out_specs=vmem,
         scratch_shapes=[
+            VMEM((1, 128), jnp.int32), VMEM((256, WIDTH), bf16), VMEM((WIDTH, WIDTH), bf16),
             VMEM((CHIPS, 4, 16, 128), bf16), VMEM((640, WIDTH), bf16), VMEM((4 * CHIPS, 16, 128), bf16),
             VMEM((3, WIDTH, HALF), bf16), VMEM((2, CHIPS, 1, 128), jnp.int32), VMEM((256, 128), bf16), VMEM((256, 128), bf16),
             VMEM((512, HALF), bf16), VMEM((640, HALF), bf16), VMEM((640, HALF), bf16),
@@ -394,9 +426,9 @@
             VMEM((4, 128, 384), f32), VMEM((CHIPS, 8, 384), f32), VMEM((128, WIDTH), bf16), VMEM((8, 256), bf16),
             pltpu.SMEM((2, 1, 128), jnp.int32), pltpu.SMEM((24,), jnp.int32),
             dma, dma((CHIPS,)), dma((3,)), dma((CHIPS,)), dma((2,)), dma((2,)), dma((2,)), dma((3,)), dma((3, 4)), dma((2,)),
-            dma((PAIRS, 3, 3)), dma((PAIRS, 3, 3)), dma, dma((CHIPS,)), dma((4,)), dma((4,)), dma, dma((128,))],
-        compiler_params=pltpu.CompilerParams(has_side_effects=True, vmem_limit_bytes=62 * 1024 * 1024), name="attend",
-    )(x, idx, wq, wk, wv)
+            dma((PAIRS, 3, 3)), dma((PAIRS, 3, 3)), dma, dma((CHIPS,)), dma((4,)), dma((4,)), dma, dma((128,)), dma],
+        compiler_params=pltpu.CompilerParams(has_side_effects=True, collective_id=0, vmem_limit_bytes=62 * 1024 * 1024), name="attend",
+    )(x, rand_idx, wq, wk, wv, wo)
 
 
 def solution(mesh):
@@ -404,9 +436,6 @@
     rep_spec = P(None, None)
 
     def local_fn(tokens, w_query, w_key, w_value, w_out, rand_idx):
-        idx = jnp.pad(rand_idx.reshape(1, 12), ((0, 0), (0, 116)))
-        full = attend(tokens, idx, w_query, w_key, w_value)
-        out = lax.dot_general(full, w_out, NT, preferred_element_type=jnp.float32)
-        return out.astype(jnp.bfloat16)
+        return attend(tokens, rand_idx, w_query, w_key, w_value, w_out)
 
     return jax.shard_map(local_fn, mesh=mesh, in_specs=(row_spec, rep_spec, rep_spec, rep_spec, rep_spec, row_spec), out_specs=row_spec, check_vma=False)

time: 118 us -> 112 us (0.949)
  matrix products: 7.05 us -> 0 us
    dot_general x1 -> x0, matrix products: 7.05 us -> none  [local_fn(): out = lax.dot_general(full, w_out, NT, preferred_element_type=jnp.float32)]
    unnamed x0 -> x1, local copies, waits for them, and re-layouts: none -> 2.3 us
where the time goes in v4:
time: 112 us; the launch traced here: 111 us
  Pallas kernels  109 us (97%)
  local copies, waits for them, and re-layouts  2.3 us (2%)
    pallas_call x1, Pallas kernels, attend(): pl.pallas_call(kernel, out_shape=jax.ShapeDtypeStruct((256, WIDTH), bf16)...  109 us
    unnamed x1, local copies, waits for them, and re-layouts  2.3 us

profile of v4, /device:TPU:0, one launch (start us, length us, event | category | flops | bytes accessed | tf_op | source)
XLA Modules:
  0.0 111.5 jit_solution(3912780129690454228)
XLA Ops:
  0.0 109.2 %attend.1 = bf16[256,2048]{1,0:T(8,128)(2,1)} custom-call(bf16[256,2048]{1,0:T(8,128)(2,1)} %x_ref.1, s32[4,3]{1,0:T(4,128)} %rand_ref.1, bf16[2048,2048]{1,0:T(8,128)(2,1)} %wq_ref.1, bf16[2048,2048]{1,0:T(8,128)(2,1)} %wk_ref.1, bf16[2048,2048]{1,0:T(8,128)(2,1)} %wv_ref.1, bf16[2048,2048]{1,0:T(8,128)(2,1)} %wo_ref.1), custom_call_target="tpu_custom_call" | custom-call | tf_op jit(solution)/shard_map/attend/pallas_call | solution.py:416
  109.2 2.3 %copy.8 = bf16[256,2048]{1,0:T(8,128)(2,1)} copy(bf16[256,2048]{1,0:T(8,128)(2,1)} %attend.1) | data formatting | bytes 2097152

commit v5 on v4

--- a/solution.py
+++ b/solution.py
@@ -18,6 +18,7 @@
 VMEM = pltpu.VMEM
 ORDERS = ((0, 1, 2), (1, 2, 0), (2, 0, 1))
 NT = (((1,), (1,)), ((), ()))
+TN = (((0,), (0,)), ((), ()))
 
 
 def permutation():
@@ -70,7 +71,7 @@
         return pltpu.make_async_copy(w.at[:, aligned(core * 4 + t, 256)], w_buf.at[i, :, aligned(t, 256)], w_sem.at[i, t])
 
     def x_swap(which):
-        return remote(x_ref, xc.at[pl.ds(pl.multiple_of(BLK + 256 * which, BLK), 256)], x_sem.at[0], x_sem.at[1], partner)
+        return remote(x_ref, xc.at[aligned(which, 256)], x_sem.at[0], x_sem.at[1], partner)
 
     def idx_copy(dst_chip, slot):
         return remote(idx_ref, idx_all.at[core, slot], i_send.at[0], i_recv.at[slot], 2 * dst_chip + core)
@@ -81,11 +82,11 @@
     def row_copy(dst_chip, slot):
         return remote(xs.at[dst_chip], recv.at[pl.ds(4 * slot, 4)], s_send, s_recv.at[slot], 2 * dst_chip + core)
 
-    nbr = lax.rem(chip + 2 * core - 1 + CHIPS, CHIPS)
-
-    def halo(dst_core, side):
-        return remote(x_ref.at[aligned(3 * core, BLK)], xc.at[aligned(9 * side, BLK)], h_send.at[dst_core], h_recv.at[side],
-                      2 * nbr + dst_core)
+    def halo(kv, side):
+        ref = (k_ref, v_ref)[kv]
+        to = lax.rem(chip + 1 + side * (CHIPS - 2), CHIPS)
+        return remote(ref.at[pl.ds((8 - 7 * side) * BLK, BLK)], ref.at[pl.ds(9 * side * BLK, BLK)],
+                      h_send.at[kv, side], h_recv.at[kv, side], 2 * to + core)
 
     wo_copy = pltpu.make_async_copy(wo_ref, wo_buf, wo_sem)
 
@@ -93,7 +94,7 @@
         for t in range(4):
             for i in range(3):
                 w_copy(i, t).start()
-        own_x = pltpu.make_async_copy(x_ref, xc.at[pl.ds(pl.multiple_of(BLK + 256 * core, BLK), 256)], loc.at[1])
+        own_x = pltpu.make_async_copy(x_ref, xc.at[aligned(core, 256)], loc.at[1])
         own_x.start()
         named_lane = lax.broadcasted_iota(jnp.int32, (1, 128), 1)
         line = jnp.full((1, 128), FAR, jnp.int32)
@@ -128,8 +129,6 @@
         lax.fori_loop(1, CHIPS, start_row, 0, unroll=7)
         own_row = pltpu.make_async_copy(xs.at[chip], recv.at[pl.ds(4 * chip, 4)], loc.at[0])
         own_row.start()
-        for t in range(2):
-            halo(t, 1 - core).start()
 
     with jax.named_scope("wait_x"):
         own_x.wait()
@@ -141,7 +140,7 @@
         cols = aligned(t, 256)
         for i in range(3):
             w_copy(i, t).wait()
-        rows = xc[BLK:9 * BLK, :]
+        rows = xc[...]
         q_ref[:, cols] = jnp.dot(rows, w_buf[0, :, cols], preferred_element_type=jnp.float32).astype(jnp.bfloat16)
         k_ref[BLK:9 * BLK, cols] = jnp.dot(rows, w_buf[1, :, cols], preferred_element_type=jnp.float32).astype(jnp.bfloat16)
         v_ref[BLK:9 * BLK, cols] = jnp.dot(rows, w_buf[2, :, cols], preferred_element_type=jnp.float32).astype(jnp.bfloat16)
@@ -169,6 +168,9 @@
     with jax.named_scope("wait_rows"):
         lax.fori_loop(1, CHIPS, wait_row, 0)
         own_row.wait()
+        for kv in range(2):
+            for side in range(2):
+                halo(kv, side).start()
 
     with jax.named_scope("select"):
         for s in range(SLOTS):
@@ -218,20 +220,6 @@
     with jax.named_scope("gather0"):
         for j in range(PAIRS):
             advance(j, 0)
-    with jax.named_scope("halo"):
-        for t in range(2):
-            halo(t, 1 - core).wait_send()
-            halo(t, t).wait_recv()
-
-        def project_halo(t, carry):
-            cols = aligned(t, 256)
-            rows = jnp.concatenate([xc[0:BLK, :], xc[9 * BLK:10 * BLK, :]], axis=0)
-            for i, ref in ((1, k_ref), (2, v_ref)):
-                out = jnp.dot(rows, w_buf[i, :, cols], preferred_element_type=jnp.float32).astype(jnp.bfloat16)
-                ref[0:BLK, cols] = out[0:BLK]
-                ref[9 * BLK:10 * BLK, cols] = out[BLK:]
-            return carry
-        lax.fori_loop(0, 4, project_halo, 0)
     with jax.named_scope("gather1"):
         for j in range(PAIRS):
             advance(j, 1)
@@ -253,49 +241,57 @@
                     at = at + jnp.where(h < named, 1, 0)
                 slot_s[3 * b + t] = at
 
-    lane = lax.broadcasted_iota(jnp.int32, (128, 128), 1)
-    key = lax.broadcasted_iota(jnp.int32, (1, 256), 1)
+    with jax.named_scope("halo"):
+        for kv in range(2):
+            for side in range(2):
+                halo(kv, side).wait()
+
+    key = lax.broadcasted_iota(jnp.int32, (3 * BLK, 1), 0)
 
     def part_copy(wave, i, slot):
         dst_chip = 16 * wave + i
         return remote(part.at[wave, aligned(i, 8)], parts.at[slot], c_send, c_recv.at[slot], 2 * dst_chip + core)
 
     def o_copy(wave, rows_of, cols_of):
-        return remote(o_ref.at[aligned(rows_of, 256), pl.ds(256 * wave, 256)],
+        return remote(o_ref.at[aligned(rows_of, 256), aligned(wave, 256)],
                       full_ref.at[:, aligned(cols_of * 4 + wave, 256)], o_send.at[wave], o_recv.at[wave], partner)
 
-    for wave in range(4):
+    def one_wave(wave, carry):
         with jax.named_scope("wait_wave"):
-            for j in (2 * wave, 2 * wave + 1):
-                advance(j, 3)
+            for w in range(4):
+                @pl.when(wave == w)
+                def _():
+                    for j in (2 * w, 2 * w + 1):
+                        advance(j, 3)
 
         def unpack(z, carry):
-            for j in (2 * wave, 2 * wave + 1):
-                rows = gath[j, z].reshape(256, 256)
+            for t in range(2):
+                rows = gath[2 * wave + t, z].reshape(256, 256)
                 moved = jnp.dot(perm, rows, preferred_element_type=jnp.float32).astype(jnp.bfloat16)
                 for s in range(15):
-                    hot[j, s, aligned(z, 16), :] = moved[s * 16:s * 16 + 16]
+                    hot[2 * wave + t, s, aligned(z, 16), :] = moved[s * 16:s * 16 + 16]
             return carry
         with jax.named_scope("unpack"):
             lax.fori_loop(0, 4, unpack, 0)
 
         with jax.named_scope("globpart"):
-            stats = jnp.zeros((128, 128), jnp.float32)
-            for t, j in enumerate((2 * wave, 2 * wave + 1)):
-                cols = slice(128 * j, 128 * j + 128)
+            sums, tops = [], []
+            for t in range(2):
+                j = 2 * wave + t
+                cols = aligned(j, 128)
                 gq = jnp.concatenate([hot[j, 14, :, 0:128], hot[j, 14, :, 128:256]], axis=0)
                 queries = split_heads(gq, 128) * jnp.bfloat16(0.125)
-                scores = lax.dot_general(queries, k_ref[BLK:9 * BLK, cols], NT, preferred_element_type=jnp.float32)
-                top = jnp.max(scores, axis=1, keepdims=True)
+                scores = lax.dot_general(k_ref[BLK:9 * BLK, cols], queries, NT, preferred_element_type=jnp.float32)
+                top = jnp.max(scores, axis=0, keepdims=True)
                 probs = jnp.exp(scores - top)
-                total = jnp.sum(probs, axis=1, keepdims=True)
-                out = jnp.dot(probs.astype(jnp.bfloat16), v_ref[BLK:9 * BLK, cols], preferred_element_type=jnp.float32)
+                total = jnp.sum(probs, axis=0, keepdims=True)
+                out = lax.dot_general(probs.astype(jnp.bfloat16), v_ref[BLK:9 * BLK, cols], TN, preferred_element_type=jnp.float32)
                 part[wave, :, 128 * t:128 * t + 128] = join_heads(out, 128)
                 for h in range(2):
-                    rows = slice(128 * h, 128 * h + 128)
-                    stats = jnp.where(lane == 2 * t + h, total[rows], stats)
-                    stats = jnp.where(lane == 4 + 2 * t + h, top[rows], stats)
-            part[wave, :, 256:384] = stats
+                    sums.append(total[:, 128 * h:128 * h + 128])
+                    tops.append(top[:, 128 * h:128 * h + 128])
+            stats = jnp.concatenate(sums + tops + [jnp.zeros((120, 128), jnp.float32)], axis=0)
+            part[wave, :, 256:384] = stats.T
 
         def start_part(i, carry):
             j = i ^ (chip & 15)
@@ -307,29 +303,32 @@
         with jax.named_scope("issue_parts"):
             lax.fori_loop(0, 16, start_part, 0)
 
-        def one_block(step, carry):
-            b = (step + 4 * (1 - core)) & 7
-            named = [0, 1] + [slot_s[3 * b + t] for t in range(3)]
-            block_id = chip * 8 + b
-            bias = (jnp.where((key < BLK) & (block_id - 1 < 2), NEG, 0.0)
-                    + jnp.where((key >= 2 * BLK) & (key < 3 * BLK) & (block_id + 1 >= 8 * CHIPS), NEG, 0.0))
-            base = pl.multiple_of(b * BLK, BLK)
-            for j in (2 * wave, 2 * wave + 1):
-                cols = slice(j * 128, j * 128 + 128)
-                queries = split_heads(q_ref[pl.ds(base, BLK), cols], BLK) * jnp.bfloat16(0.125)
-                keys = jnp.concatenate([k_ref[pl.ds(base, 3 * BLK), cols]] + [hot[j, s, :, 0:128] for s in named], axis=0)
-                vals = jnp.concatenate([v_ref[pl.ds(base, 3 * BLK), cols]] + [hot[j, s, :, 128:256] for s in named], axis=0)
-                scores = lax.dot_general(queries, keys, NT, preferred_element_type=jnp.float32)
-                scores = jnp.concatenate([scores[:, :256] + bias, scores[:, 256:]], axis=1)
-                top = jnp.max(scores, axis=1, keepdims=True)
-                probs = jnp.exp(scores - top)
-                probs = probs * (1.0 / jnp.sum(probs, axis=1, keepdims=True))
-                out = jnp.dot(probs.astype(jnp.bfloat16), vals, preferred_element_type=jnp.float32)
-                o_ref[pl.ds(base, BLK), cols] = join_heads(out, BLK).astype(jnp.bfloat16)
-            return carry
         with jax.named_scope("blocks"):
-            lax.fori_loop(0, 8, one_block, 0)
+            for b in range(8):
+                named = [0, 1] + [slot_s[3 * b + t] for t in range(3)]
+                rows = slice(b * BLK, b * BLK + BLK)
+                near = slice(b * BLK, b * BLK + 3 * BLK)
+                for t in range(2):
+                    j = 2 * wave + t
+                    cols = aligned(j, 128)
+                    queries = split_heads(q_ref[rows, cols], BLK) * jnp.bfloat16(0.125)
+                    keys = jnp.concatenate([k_ref[near, cols]] + [hot[j, s, :, 0:128] for s in named], axis=0)
+                    vals = jnp.concatenate([v_ref[near, cols]] + [hot[j, s, :, 128:256] for s in named], axis=0)
+                    scores = lax.dot_general(keys, queries, NT, preferred_element_type=jnp.float32)
+                    if b == 2:
+                        bias = jnp.where((key < BLK) & (chip == 0), NEG, 0.0)
+                    elif b == 7:
+                        bias = jnp.where((key >= 2 * BLK) & (chip == CHIPS - 1), NEG, 0.0)
+                    if b in (2, 7):
+                        scores = jnp.concatenate([scores[:3 * BLK] + bias, scores[3 * BLK:]], axis=0)
+                    top = jnp.max(scores, axis=0, keepdims=True)
+                    probs = jnp.exp(scores - top)
+                    probs = probs * (1.0 / jnp.sum(probs, axis=0, keepdims=True))
+                    out = lax.dot_general(probs.astype(jnp.bfloat16), vals, TN, preferred_element_type=jnp.float32)
+                    o_ref[rows, cols] = join_heads(out, BLK).astype(jnp.bfloat16)
         o_copy(wave, 1 - core, core).start()
+        return carry
+    lax.fori_loop(0, 4, one_wave, 0)
 
     with jax.named_scope("local"):
         mine = [pltpu.make_async_copy(o_ref.at[aligned(core, 256)], full_ref.at[:, aligned(core, HALF)], loc.at[0]),
@@ -419,13 +418,13 @@
         in_specs=[vmem, pl.BlockSpec(memory_space=pltpu.SMEM), hbm, hbm, hbm, hbm], out_specs=vmem,
         scratch_shapes=[
             VMEM((1, 128), jnp.int32), VMEM((256, WIDTH), bf16), VMEM((WIDTH, WIDTH), bf16),
-            VMEM((CHIPS, 4, 16, 128), bf16), VMEM((640, WIDTH), bf16), VMEM((4 * CHIPS, 16, 128), bf16),
+            VMEM((CHIPS, 4, 16, 128), bf16), VMEM((512, WIDTH), bf16), VMEM((4 * CHIPS, 16, 128), bf16),
             VMEM((3, WIDTH, HALF), bf16), VMEM((2, CHIPS, 1, 128), jnp.int32), VMEM((256, 128), bf16), VMEM((256, 128), bf16),
             VMEM((512, HALF), bf16), VMEM((640, HALF), bf16), VMEM((640, HALF), bf16),
             VMEM((PAIRS, 4, 4, 4, SLOTS, 256), bf16), VMEM((PAIRS, SLOTS, BLK, 256), bf16), VMEM((512, HALF), bf16),
             VMEM((4, 128, 384), f32), VMEM((CHIPS, 8, 384), f32), VMEM((128, WIDTH), bf16), VMEM((8, 256), bf16),
             pltpu.SMEM((2, 1, 128), jnp.int32), pltpu.SMEM((24,), jnp.int32),
-            dma, dma((CHIPS,)), dma((3,)), dma((CHIPS,)), dma((2,)), dma((2,)), dma((2,)), dma((3,)), dma((3, 4)), dma((2,)),
+            dma, dma((CHIPS,)), dma((3,)), dma((CHIPS,)), dma((2,)), dma((2, 2)), dma((2, 2)), dma((3,)), dma((3, 4)), dma((2,)),
             dma((PAIRS, 3, 3)), dma((PAIRS, 3, 3)), dma, dma((CHIPS,)), dma((4,)), dma((4,)), dma, dma((128,)), dma],
         compiler_params=pltpu.CompilerParams(has_side_effects=True, collective_id=0, vmem_limit_bytes=62 * 1024 * 1024), name="attend",
     )(x, rand_idx, wq, wk, wv, wo)

time: 112 us -> 97.9 us (0.87)
  Pallas kernels: 109 us -> 95.4 us
    pallas_call x1, Pallas kernels: 109 us -> 95.4 us  [attend(): pl.pallas_call(kernel, out_shape=jax.ShapeDtypeStruct((256, WIDTH), bf16)...]
where the time goes in v5:
time: 97.9 us; the launch traced here: 97.8 us
  Pallas kernels  95.4 us (97%)
  local copies, waits for them, and re-layouts  2.3 us (2%)
    pallas_call x1, Pallas kernels, attend(): pl.pallas_call(kernel, out_shape=jax.ShapeDtypeStruct((256, WIDTH), bf16)...  95.4 us
    unnamed x1, local copies, waits for them, and re-layouts  2.3 us

profile of v5, /device:TPU:0, one launch (start us, length us, event | category | flops | bytes accessed | tf_op | source)
XLA Modules:
  0.0 97.8 jit_solution(10013320286576556795)
XLA Ops:
  0.0 95.4 %attend.1 = bf16[256,2048]{1,0:T(8,128)(2,1)} custom-call(bf16[256,2048]{1,0:T(8,128)(2,1)} %x_ref.1, s32[4,3]{1,0:T(4,128)} %rand_ref.1, bf16[2048,2048]{1,0:T(8,128)(2,1)} %wq_ref.1, bf16[2048,2048]{1,0:T(8,128)(2,1)} %wk_ref.1, bf16[2048,2048]{1,0:T(8,128)(2,1)} %wv_ref.1, bf16[2048,2048]{1,0:T(8,128)(2,1)} %wo_ref.1), custom_call_target="tpu_custom_call" | custom-call | tf_op jit(solution)/shard_map/attend/pallas_call | solution.py:415
  95.4 2.3 %copy.8 = bf16[256,2048]{1,0:T(8,128)(2,1)} copy(bf16[256,2048]{1,0:T(8,128)(2,1)} %attend.1) | data formatting | bytes 2097152

commit v6 on v5

--- a/solution.py
+++ b/solution.py
@@ -48,9 +48,9 @@
 
 
 def kernel(x_ref, rand_ref, wq_ref, wk_ref, wv_ref, wo_ref, y_ref,
-           idx_ref, full_ref, wo_buf, xs, xc, recv, w_buf, idx_all, sel, other, q_ref, k_ref, v_ref, gath, hot, o_ref, part, parts, glob, piece, near_s, slot_s,
+           idx_ref, full_ref, wo_buf, xs, xc, recv, w_buf, idx_all, sel, other, q_ref, k_ref, v_ref, gath, hot, o_ref, part, parts, glob, piece, near_s, slot_s, queries_in, queries_g,
            s_send, s_recv, i_send, i_recv, x_sem, h_send, h_recv, loc, w_sem, p_sem, g_send, g_recv,
-           c_send, c_recv, o_send, o_recv, e_send, e_recv, wo_sem):
+           c_send, c_recv, o_send, o_recv, e_send, e_recv, wo_sem, b_send, b_recv):
     dev = lax.axis_index("seq")
     chip, core = dev // 2, dev % 2
     partner = dev + 1 - 2 * core
@@ -162,6 +162,20 @@
         for s in range(3, 14):
             published.append(jnp.min(jnp.where(ids > published[-1], ids, FAR)))
 
+    with jax.named_scope("slots"):
+        near = [pltpu.make_async_copy(idx_all.at[c, chip], near_s.at[c], loc.at[1 + c]) for c in range(2)]
+        for n in near:
+            n.start()
+        for n in near:
+            n.wait()
+        for b in range(8):
+            for t in range(3):
+                named = near_s[b // 4, 0, 3 * (b % 4) + t]
+                at = jnp.int32(2)
+                for h in published[2:]:
+                    at = at + jnp.where(h < named, 1, 0)
+                slot_s[3 * b + t] = at
+
     def wait_row(i, carry):
         row_copy(chip ^ i, chip ^ i).wait()
         return carry
@@ -171,6 +185,9 @@
         for kv in range(2):
             for side in range(2):
                 halo(kv, side).start()
+
+    def query_copy(dst_chip, src_chip):
+        return remote(queries_in.at[chip], queries_in.at[src_chip], b_send, b_recv.at[src_chip], 2 * dst_chip + core)
 
     with jax.named_scope("select"):
         for s in range(SLOTS):
@@ -186,13 +203,18 @@
     with jax.named_scope("publish"):
         moved = jnp.dot(perm, sel[...] + other[...], preferred_element_type=jnp.float32).astype(jnp.bfloat16)
         rows = jnp.concatenate([moved[16 * j:16 * j + 16] for j in range(16)], axis=1)
-        out = [jnp.dot(rows, w_buf[i], preferred_element_type=jnp.float32) for i in range(3)]
-        row_id = lax.broadcasted_iota(jnp.int32, (SLOTS, 256), 0)
+        gq = jnp.dot(rows, w_buf[0], preferred_element_type=jnp.float32)
+        gq = jnp.concatenate([gq[t:t + 1, 128 * j:128 * j + 128] for t in range(2) for j in range(PAIRS)], axis=0)
+        queries_in[chip] = gq.astype(jnp.bfloat16)
+
+        def start_query(i, carry):
+            query_copy(chip ^ i, chip).start()
+            return carry
+        lax.fori_loop(1, CHIPS, start_query, 0, unroll=7)
+        out = [jnp.dot(rows, w_buf[i], preferred_element_type=jnp.float32) for i in (1, 2)]
         for j in range(PAIRS):
             cols = slice(128 * j, 128 * j + 128)
-            kv = jnp.concatenate([out[1][:, cols], out[2][:, cols]], axis=1)
-            gq = jnp.concatenate([out[0][0:1, cols], out[0][1:2, cols]], axis=1)
-            kv = jnp.where(row_id == 14, jnp.broadcast_to(gq, (SLOTS, 256)), kv)
+            kv = jnp.concatenate([out[0][:, cols], out[1][:, cols]], axis=1)
             gath[j, coord[2], coord[1], coord[0]] = kv.astype(jnp.bfloat16)
 
     def copies(j, stage, receive):
@@ -223,23 +245,56 @@
     with jax.named_scope("gather1"):
         for j in range(PAIRS):
             advance(j, 1)
+    def wait_query(i, carry):
+        query_copy(chip ^ i, chip ^ i).wait()
+        return carry
+    with jax.named_scope("wait_queries"):
+        lax.fori_loop(1, CHIPS, wait_query, 0)
+
+    def unpack_queries(z, carry):
+        rows = queries_in[pl.ds(16 * z, 16)].reshape(256, 128)
+        moved = jnp.dot(perm, rows, preferred_element_type=jnp.float32).astype(jnp.bfloat16)
+        for s in range(16):
+            queries_g[s, aligned(z, 16), :] = moved[16 * s:16 * s + 16]
+        return carry
+
+    def glob_part(wave, carry):
+        sums, tops = [], []
+        for t in range(2):
+            j = 2 * wave + t
+            cols = aligned(j, 128)
+            gq = jnp.concatenate([queries_g[j], queries_g[PAIRS + j]], axis=0)
+            queries = split_heads(gq, 128) * jnp.bfloat16(0.125)
+            scores = lax.dot_general(k_ref[BLK:9 * BLK, cols], queries, NT, preferred_element_type=jnp.float32)
+            top = jnp.max(scores, axis=0, keepdims=True)
+            probs = jnp.exp(scores - top)
+            total = jnp.sum(probs, axis=0, keepdims=True)
+            out = lax.dot_general(probs.astype(jnp.bfloat16), v_ref[BLK:9 * BLK, cols], TN, preferred_element_type=jnp.float32)
+            part[wave, :, 128 * t:128 * t + 128] = join_heads(out, 128)
+            for h in range(2):
+                sums.append(total[:, 128 * h:128 * h + 128])
+                tops.append(top[:, 128 * h:128 * h + 128])
+        stats = jnp.concatenate(sums + tops + [jnp.zeros((120, 128), jnp.float32)], axis=0)
+        part[wave, :, 256:384] = stats.T
+        return carry
+    with jax.named_scope("globpart"):
+        lax.fori_loop(0, 4, unpack_queries, 0)
+        lax.fori_loop(0, 4, glob_part, 0)
+
+    def part_copy(dst_chip, slot):
+        return remote(part.at[dst_chip >> 4, aligned(dst_chip & 15, 8)], parts.at[slot], c_send, c_recv.at[slot], 2 * dst_chip + core)
+
+    def start_part(i, carry):
+        part_copy(chip ^ i, chip).start()
+        return carry
     with jax.named_scope("gather2"):
-        for j in range(PAIRS):
+        for j in range(4):
             advance(j, 2)
-
-    with jax.named_scope("slots"):
-        near = [pltpu.make_async_copy(idx_all.at[c, chip], near_s.at[c], loc.at[c]) for c in range(2)]
-        for n in near:
-            n.start()
-        for n in near:
-            n.wait()
-        for b in range(8):
-            for t in range(3):
-                named = near_s[b // 4, 0, 3 * (b % 4) + t]
-                at = jnp.int32(2)
-                for h in published[2:]:
-                    at = at + jnp.where(h < named, 1, 0)
-                slot_s[3 * b + t] = at
+        lax.fori_loop(1, CHIPS, start_part, 0, unroll=7)
+        own_part = pltpu.make_async_copy(part.at[chip >> 4, aligned(chip & 15, 8)], parts.at[chip], loc.at[1])
+        own_part.start()
+        for j in range(4, PAIRS):
+            advance(j, 2)
 
     with jax.named_scope("halo"):
         for kv in range(2):
@@ -248,15 +303,42 @@
 
     key = lax.broadcasted_iota(jnp.int32, (3 * BLK, 1), 0)
 
-    def part_copy(wave, i, slot):
-        dst_chip = 16 * wave + i
-        return remote(part.at[wave, aligned(i, 8)], parts.at[slot], c_send, c_recv.at[slot], 2 * dst_chip + core)
-
     def o_copy(wave, rows_of, cols_of):
         return remote(o_ref.at[aligned(rows_of, 256), aligned(wave, 256)],
                       full_ref.at[:, aligned(cols_of * 4 + wave, 256)], o_send.at[wave], o_recv.at[wave], partner)
 
+    def wait_part(i, carry):
+        part_copy(chip ^ i, chip ^ i).wait()
+        return carry
+
+    def glob_slice(src_chip, src_core):
+        return glob.at[aligned(src_chip % 16, 8), aligned(src_core * 4 + src_chip // 16, 256)]
+
+    def glob_copy(src_chip, src_core):
+        return remote(piece, glob_slice(src_chip, src_core), e_send, e_recv.at[2 * src_chip + src_core], 0)
+
+    def combine():
+        with jax.named_scope("wait_parts"):
+            lax.fori_loop(1, CHIPS, wait_part, 0)
+            own_part.wait()
+        with jax.named_scope("combine"):
+            top = lax.fori_loop(0, CHIPS, lambda i, t: jnp.maximum(t, parts[i, :, 256:384]), jnp.full((8, 128), NEG, jnp.float32), unroll=8)
+
+            def add(i, carry):
+                num, den = carry
+                weight = pltpu.roll(jnp.exp(parts[i, :, 256:384] - top), 124, 1)
+                wide = jnp.concatenate([jnp.broadcast_to(weight[:, t:t + 1], (8, HEAD_DIM)) for t in range(4)], axis=1)
+                return num + wide * parts[i, :, 0:256], den + weight * parts[i, :, 256:384]
+            num, den = lax.fori_loop(0, CHIPS, add, (jnp.zeros((8, 256), jnp.float32), jnp.zeros((8, 128), jnp.float32)), unroll=8)
+            wide = jnp.concatenate([jnp.broadcast_to(den[:, t:t + 1], (8, HEAD_DIM)) for t in range(4)], axis=1)
+            piece[...] = (num / wide).astype(jnp.bfloat16)
+
+            @pl.when(dev != 0)
+            def _():
+                glob_copy(chip, core).start()
+
     def one_wave(wave, carry):
+        pl.when(wave == 3)(combine)
         with jax.named_scope("wait_wave"):
             for w in range(4):
                 @pl.when(wave == w)
@@ -268,40 +350,11 @@
             for t in range(2):
                 rows = gath[2 * wave + t, z].reshape(256, 256)
                 moved = jnp.dot(perm, rows, preferred_element_type=jnp.float32).astype(jnp.bfloat16)
-                for s in range(15):
+                for s in range(14):
                     hot[2 * wave + t, s, aligned(z, 16), :] = moved[s * 16:s * 16 + 16]
             return carry
         with jax.named_scope("unpack"):
             lax.fori_loop(0, 4, unpack, 0)
-
-        with jax.named_scope("globpart"):
-            sums, tops = [], []
-            for t in range(2):
-                j = 2 * wave + t
-                cols = aligned(j, 128)
-                gq = jnp.concatenate([hot[j, 14, :, 0:128], hot[j, 14, :, 128:256]], axis=0)
-                queries = split_heads(gq, 128) * jnp.bfloat16(0.125)
-                scores = lax.dot_general(k_ref[BLK:9 * BLK, cols], queries, NT, preferred_element_type=jnp.float32)
-                top = jnp.max(scores, axis=0, keepdims=True)
-                probs = jnp.exp(scores - top)
-                total = jnp.sum(probs, axis=0, keepdims=True)
-                out = lax.dot_general(probs.astype(jnp.bfloat16), v_ref[BLK:9 * BLK, cols], TN, preferred_element_type=jnp.float32)
-                part[wave, :, 128 * t:128 * t + 128] = join_heads(out, 128)
-                for h in range(2):
-                    sums.append(total[:, 128 * h:128 * h + 128])
-                    tops.append(top[:, 128 * h:128 * h + 128])
-            stats = jnp.concatenate(sums + tops + [jnp.zeros((120, 128), jnp.float32)], axis=0)
-            part[wave, :, 256:384] = stats.T
-
-        def start_part(i, carry):
-            j = i ^ (chip & 15)
-
-            @pl.when(16 * wave + j != chip)
-            def _():
-                part_copy(wave, j, chip).start()
-            return carry
-        with jax.named_scope("issue_parts"):
-            lax.fori_loop(0, 16, start_part, 0)
 
         with jax.named_scope("blocks"):
             for b in range(8):
@@ -331,65 +384,20 @@
     lax.fori_loop(0, 4, one_wave, 0)
 
     with jax.named_scope("local"):
-        mine = [pltpu.make_async_copy(o_ref.at[aligned(core, 256)], full_ref.at[:, aligned(core, HALF)], loc.at[0]),
-                pltpu.make_async_copy(part.at[chip >> 4, aligned(chip & 15, 8)], parts.at[chip], loc.at[1])]
-        for m in mine:
-            m.start()
+        mine = pltpu.make_async_copy(o_ref.at[aligned(core, 256)], full_ref.at[:, aligned(core, HALF)], loc.at[0])
+        mine.start()
         for j in range(PAIRS):
             for stage in range(3):
                 for c in copies(j, stage, False):
                     c.wait_send()
-
-        for m in mine:
-            m.wait()
-
-    def wait_part(i, carry):
-        part_copy(chip >> 4, chip & 15, chip ^ i).wait()
-        return carry
-    with jax.named_scope("wait_parts"):
-        lax.fori_loop(1, CHIPS, wait_part, 0)
-
-    with jax.named_scope("combine"):
-        top = lax.fori_loop(0, CHIPS, lambda i, t: jnp.maximum(t, parts[i, :, 256:384]), jnp.full((8, 128), NEG, jnp.float32), unroll=8)
-
-        def add(i, carry):
-            num, den = carry
-            weight = pltpu.roll(jnp.exp(parts[i, :, 256:384] - top), 124, 1)
-            wide = jnp.concatenate([jnp.broadcast_to(weight[:, t:t + 1], (8, HEAD_DIM)) for t in range(4)], axis=1)
-            return num + wide * parts[i, :, 0:256], den + weight * parts[i, :, 256:384]
-        num, den = lax.fori_loop(0, CHIPS, add, (jnp.zeros((8, 256), jnp.float32), jnp.zeros((8, 128), jnp.float32)), unroll=8)
-        wide = jnp.concatenate([jnp.broadcast_to(den[:, t:t + 1], (8, HEAD_DIM)) for t in range(4)], axis=1)
-        piece[...] = (num / wide).astype(jnp.bfloat16)
-
-    def glob_slice(src_chip, src_core):
-        return glob.at[aligned(src_chip % 16, 8), aligned(src_core * 4 + src_chip // 16, 256)]
-
-    def glob_copy(src_chip, src_core):
-        return remote(piece, glob_slice(src_chip, src_core), e_send, e_recv.at[2 * src_chip + src_core], 0)
-
-    def project_out(t, carry):
-        cols = aligned(t, 256)
-        y_ref[:, cols] = lax.dot_general(full_ref[...], wo_buf[cols, :], NT, preferred_element_type=jnp.float32).astype(jnp.bfloat16)
-        return carry
-
-    def project_glob(t, carry):
-        cols = aligned(t, 256)
-        y_ref[0:128, cols] = lax.dot_general(glob[...], wo_buf[cols, :], NT, preferred_element_type=jnp.float32).astype(jnp.bfloat16)
-        return carry
+        mine.wait()
 
     with jax.named_scope("wait_o"):
-        @pl.when(dev != 0)
-        def _():
-            glob_copy(chip, core).start()
-
         for wave in range(4):
             o_copy(wave, 1 - core, core).wait_send()
             o_copy(wave, core, 1 - core).wait_recv()
         wo_copy.wait()
-    with jax.named_scope("out"):
-        lax.fori_loop(0, 8, project_out, 0)
-
-    with jax.named_scope("tail"):
+
         @pl.when(dev != 0)
         def _():
             glob_copy(chip, core).wait_send()
@@ -404,7 +412,14 @@
                 glob_copy(i // 2, i % 2).wait_recv()
                 return carry
             lax.fori_loop(1, 128, wait_glob, 0)
-            lax.fori_loop(0, 8, project_glob, 0)
+            full_ref[0:128, :] = glob[...]
+
+    def project_out(t, carry):
+        cols = aligned(t, 256)
+        y_ref[:, cols] = lax.dot_general(full_ref[...], wo_buf[cols, :], NT, preferred_element_type=jnp.float32)
+        return carry
+    with jax.named_scope("out"):
+        lax.fori_loop(0, 8, project_out, 0)
 
 
 def attend(x, rand_idx, wq, wk, wv, wo):
@@ -414,7 +429,7 @@
     bf16, f32 = jnp.bfloat16, jnp.float32
     return pl.pallas_call(
         kernel,
-        out_shape=jax.ShapeDtypeStruct((256, WIDTH), bf16),
+        out_shape=jax.ShapeDtypeStruct((256, WIDTH), f32),
         in_specs=[vmem, pl.BlockSpec(memory_space=pltpu.SMEM), hbm, hbm, hbm, hbm], out_specs=vmem,
         scratch_shapes=[
             VMEM((1, 128), jnp.int32), VMEM((256, WIDTH), bf16), VMEM((WIDTH, WIDTH), bf16),
@@ -424,8 +439,9 @@
             VMEM((PAIRS, 4, 4, 4, SLOTS, 256), bf16), VMEM((PAIRS, SLOTS, BLK, 256), bf16), VMEM((512, HALF), bf16),
             VMEM((4, 128, 384), f32), VMEM((CHIPS, 8, 384), f32), VMEM((128, WIDTH), bf16), VMEM((8, 256), bf16),
             pltpu.SMEM((2, 1, 128), jnp.int32), pltpu.SMEM((24,), jnp.int32),
+            VMEM((CHIPS, 16, 128), bf16), VMEM((16, BLK, 128), bf16),
             dma, dma((CHIPS,)), dma((3,)), dma((CHIPS,)), dma((2,)), dma((2, 2)), dma((2, 2)), dma((3,)), dma((3, 4)), dma((2,)),
-            dma((PAIRS, 3, 3)), dma((PAIRS, 3, 3)), dma, dma((CHIPS,)), dma((4,)), dma((4,)), dma, dma((128,)), dma],
+            dma((PAIRS, 3, 3)), dma((PAIRS, 3, 3)), dma, dma((CHIPS,)), dma((4,)), dma((4,)), dma, dma((128,)), dma, dma, dma((CHIPS,))],
         compiler_params=pltpu.CompilerParams(has_side_effects=True, collective_id=0, vmem_limit_bytes=62 * 1024 * 1024), name="attend",
     )(x, rand_idx, wq, wk, wv, wo)
 
@@ -435,6 +451,6 @@
     rep_spec = P(None, None)
 
     def local_fn(tokens, w_query, w_key, w_value, w_out, rand_idx):
-        return attend(tokens, rand_idx, w_query, w_key, w_value, w_out)
+        return attend(tokens, rand_idx, w_query, w_key, w_value, w_out).astype(jnp.bfloat16)
 
     return jax.shard_map(local_fn, mesh=mesh, in_specs=(row_spec, rep_spec, rep_spec, rep_spec, rep_spec, row_spec), out_specs=row_spec, check_vma=False)

time: 97.9 us -> 102 us (1.042)
  Pallas kernels: 95.4 us -> 99.2 us
  other arithmetic: 0 us -> 2.71 us
  local copies, waits for them, and re-layouts: 2.3 us -> 0 us
    pallas_call x1, Pallas kernels: 95.4 us -> 99.2 us  [attend(): pl.pallas_call(kernel, out_shape=jax.ShapeDtypeStruct((256, WIDTH), f32),...]
    convert_element_type x0 -> x1, other arithmetic: none -> 2.71 us  [local_fn(): attend(tokens, rand_idx, w_query, w_key, w_value, w_out)]
    unnamed x1 -> x0, local copies, waits for them, and re-layouts: 2.3 us -> none
where the time goes in v6:
time: 102 us
  Pallas kernels  99.2 us (97%)
  other arithmetic  2.71 us (3%)
    pallas_call x1, Pallas kernels, attend(): pl.pallas_call(kernel, out_shape=jax.ShapeDtypeStruct((256, WIDTH), f32),...  99.2 us
    convert_element_type x1, other arithmetic, local_fn(): attend(tokens, rand_idx, w_query, w_key, w_value, w_out)  2.71 us

profile of v6, /device:TPU:0, one launch (start us, length us, event | category | flops | bytes accessed | tf_op | source)
XLA Modules:
  0.0 101.9 jit_solution(3035345168436217879)
XLA Ops:
  0.0 99.2 %attend.1 = f32[256,2048]{1,0:T(8,128)} custom-call(bf16[256,2048]{1,0:T(8,128)(2,1)} %x_ref.1, s32[4,3]{1,0:T(4,128)} %rand_ref.1, bf16[2048,2048]{1,0:T(8,128)(2,1)} %wq_ref.1, bf16[2048,2048]{1,0:T(8,128)(2,1)} %wk_ref.1, bf16[2048,2048]{1,0:T(8,128)(2,1)} %wv_ref.1, bf16[2048,2048]{1,0:T(8,128)(2,1)} %wo_ref.1), custom_call_target="tpu_custom_call" | custom-call | tf_op jit(solution)/shard_map/attend/pallas_call | solution.py:430
  99.2 2.7 %convert_element_type.3 = bf16[256,2048]{1,0:T(8,128)(2,1)} convert(f32[256,2048]{1,0:T(8,128)} %attend.1) | non-fusion elementwise | flops 524288 | bytes 3145728 | tf_op jit(solution)/shard_map/convert_element_type | solution.py:454

commit v7 on v6

--- a/solution.py
+++ b/solution.py
@@ -48,9 +48,9 @@
 
 
 def kernel(x_ref, rand_ref, wq_ref, wk_ref, wv_ref, wo_ref, y_ref,
-           idx_ref, full_ref, wo_buf, xs, xc, recv, w_buf, idx_all, sel, other, q_ref, k_ref, v_ref, gath, hot, o_ref, part, parts, glob, piece, near_s, slot_s, queries_in, queries_g,
+           idx_ref, full_ref, wo_buf, xs, xc, recv, w_buf, idx_all, sel, other, q_ref, k_ref, v_ref, gath, hot, o_ref, part, parts, glob, piece, near_s, slot_s, queries_in, queries_g, queries_t,
            s_send, s_recv, i_send, i_recv, x_sem, h_send, h_recv, loc, w_sem, p_sem, g_send, g_recv,
-           c_send, c_recv, o_send, o_recv, e_send, e_recv, wo_sem, b_send, b_recv):
+           c_send, c_recv, o_send, o_recv, e_send, e_recv, wo_sem, b_send, b_recv, f_sem):
     dev = lax.axis_index("seq")
     chip, core = dev // 2, dev % 2
     partner = dev + 1 - 2 * core
@@ -147,6 +147,34 @@
         return carry
     with jax.named_scope("project"):
         lax.fori_loop(0, 4, project, 0)
+
+    def first_copy(dst_chip):
+        return remote(queries_g.at[dst_chip], queries_in.at[dst_chip], f_sem.at[0], f_sem.at[1], 2 * dst_chip + core)
+
+    def query_copy(dst_chip, src_chip):
+        return remote(queries_in.at[chip], queries_in.at[src_chip], b_send, b_recv.at[src_chip], 2 * dst_chip + core)
+
+    def relayout_queries(g, carry):
+        rows = [q_ref[pl.ds(pl.multiple_of(BLK * t + 16 * g, 16), 16), 128 * j:128 * j + 128] for t in range(2) for j in range(PAIRS)]
+        moved = jnp.dot(perm, jnp.concatenate(rows, axis=0), preferred_element_type=jnp.float32).astype(jnp.bfloat16)
+        for a in range(16):
+            queries_g[16 * g + a] = moved[16 * a:16 * a + 16]
+        return carry
+
+    def start_first(i, carry):
+        first_copy(i).start()
+        return carry
+
+    def sent_first(i, carry):
+        first_copy(i).wait_send()
+        return carry
+
+    with jax.named_scope("first"):
+        @pl.when(chip == 0)
+        def _():
+            lax.fori_loop(0, 4, relayout_queries, 0)
+            lax.fori_loop(1, CHIPS, start_first, 0, unroll=7)
+            queries_in[0] = queries_g[0]
 
     def wait_idx(i, carry):
         idx_copy(chip ^ i, chip ^ i).wait()
@@ -176,6 +204,19 @@
                     at = at + jnp.where(h < named, 1, 0)
                 slot_s[3 * b + t] = at
 
+    def start_query(i, carry):
+        query_copy(chip ^ i, chip).start()
+        return carry
+    with jax.named_scope("pass_on"):
+        @pl.when(chip == 0)
+        def _():
+            lax.fori_loop(1, CHIPS, sent_first, 0)
+
+        @pl.when(chip != 0)
+        def _():
+            first_copy(chip).wait_recv()
+        lax.fori_loop(1, CHIPS, start_query, 0, unroll=7)
+
     def wait_row(i, carry):
         row_copy(chip ^ i, chip ^ i).wait()
         return carry
@@ -185,9 +226,6 @@
         for kv in range(2):
             for side in range(2):
                 halo(kv, side).start()
-
-    def query_copy(dst_chip, src_chip):
-        return remote(queries_in.at[chip], queries_in.at[src_chip], b_send, b_recv.at[src_chip], 2 * dst_chip + core)
 
     with jax.named_scope("select"):
         for s in range(SLOTS):
@@ -203,14 +241,6 @@
     with jax.named_scope("publish"):
         moved = jnp.dot(perm, sel[...] + other[...], preferred_element_type=jnp.float32).astype(jnp.bfloat16)
         rows = jnp.concatenate([moved[16 * j:16 * j + 16] for j in range(16)], axis=1)
-        gq = jnp.dot(rows, w_buf[0], preferred_element_type=jnp.float32)
-        gq = jnp.concatenate([gq[t:t + 1, 128 * j:128 * j + 128] for t in range(2) for j in range(PAIRS)], axis=0)
-        queries_in[chip] = gq.astype(jnp.bfloat16)
-
-        def start_query(i, carry):
-            query_copy(chip ^ i, chip).start()
-            return carry
-        lax.fori_loop(1, CHIPS, start_query, 0, unroll=7)
         out = [jnp.dot(rows, w_buf[i], preferred_element_type=jnp.float32) for i in (1, 2)]
         for j in range(PAIRS):
             cols = slice(128 * j, 128 * j + 128)
@@ -242,9 +272,6 @@
     with jax.named_scope("gather0"):
         for j in range(PAIRS):
             advance(j, 0)
-    with jax.named_scope("gather1"):
-        for j in range(PAIRS):
-            advance(j, 1)
     def wait_query(i, carry):
         query_copy(chip ^ i, chip ^ i).wait()
         return carry
@@ -255,7 +282,7 @@
         rows = queries_in[pl.ds(16 * z, 16)].reshape(256, 128)
         moved = jnp.dot(perm, rows, preferred_element_type=jnp.float32).astype(jnp.bfloat16)
         for s in range(16):
-            queries_g[s, aligned(z, 16), :] = moved[16 * s:16 * s + 16]
+            queries_t[s, aligned(z, 16), :] = moved[16 * s:16 * s + 16]
         return carry
 
     def glob_part(wave, carry):
@@ -263,7 +290,7 @@
         for t in range(2):
             j = 2 * wave + t
             cols = aligned(j, 128)
-            gq = jnp.concatenate([queries_g[j], queries_g[PAIRS + j]], axis=0)
+            gq = jnp.concatenate([queries_t[j], queries_t[PAIRS + j]], axis=0)
             queries = split_heads(gq, 128) * jnp.bfloat16(0.125)
             scores = lax.dot_general(k_ref[BLK:9 * BLK, cols], queries, NT, preferred_element_type=jnp.float32)
             top = jnp.max(scores, axis=0, keepdims=True)
@@ -277,9 +304,19 @@
         stats = jnp.concatenate(sums + tops + [jnp.zeros((120, 128), jnp.float32)], axis=0)
         part[wave, :, 256:384] = stats.T
         return carry
-    with jax.named_scope("globpart"):
+    def glob_waves(half, carry):
+        with jax.named_scope("globpart"):
+            lax.fori_loop(2 * half, 2 * half + 2, glob_part, 0)
+
+        @pl.when(half == 0)
+        def _():
+            with jax.named_scope("gather1"):
+                for j in range(PAIRS):
+                    advance(j, 1)
+        return carry
+    with jax.named_scope("unpack_queries"):
         lax.fori_loop(0, 4, unpack_queries, 0)
-        lax.fori_loop(0, 4, glob_part, 0)
+    lax.fori_loop(0, 2, glob_waves, 0)
 
     def part_copy(dst_chip, slot):
         return remote(part.at[dst_chip >> 4, aligned(dst_chip & 15, 8)], parts.at[slot], c_send, c_recv.at[slot], 2 * dst_chip + core)
@@ -416,7 +453,7 @@
 
     def project_out(t, carry):
         cols = aligned(t, 256)
-        y_ref[:, cols] = lax.dot_general(full_ref[...], wo_buf[cols, :], NT, preferred_element_type=jnp.float32)
+        y_ref[:, cols] = lax.dot_general(full_ref[...], wo_buf[cols, :], NT, preferred_element_type=jnp.float32).astype(jnp.bfloat16)
         return carry
     with jax.named_scope("out"):
         lax.fori_loop(0, 8, project_out, 0)
@@ -429,7 +466,7 @@
     bf16, f32 = jnp.bfloat16, jnp.float32
     return pl.pallas_call(
         kernel,
-        out_shape=jax.ShapeDtypeStruct((256, WIDTH), f32),
+        out_shape=jax.ShapeDtypeStruct((256, WIDTH), bf16),
         in_specs=[vmem, pl.BlockSpec(memory_space=pltpu.SMEM), hbm, hbm, hbm, hbm], out_specs=vmem,
         scratch_shapes=[
             VMEM((1, 128), jnp.int32), VMEM((256, WIDTH), bf16), VMEM((WIDTH, WIDTH), bf16),
@@ -439,9 +476,9 @@
             VMEM((PAIRS, 4, 4, 4, SLOTS, 256), bf16), VMEM((PAIRS, SLOTS, BLK, 256), bf16), VMEM((512, HALF), bf16),
             VMEM((4, 128, 384), f32), VMEM((CHIPS, 8, 384), f32), VMEM((128, WIDTH), bf16), VMEM((8, 256), bf16),
             pltpu.SMEM((2, 1, 128), jnp.int32), pltpu.SMEM((24,), jnp.int32),
-            VMEM((CHIPS, 16, 128), bf16), VMEM((16, BLK, 128), bf16),
+            VMEM((CHIPS, 16, 128), bf16), VMEM((CHIPS, 16, 128), bf16), VMEM((16, BLK, 128), bf16),
             dma, dma((CHIPS,)), dma((3,)), dma((CHIPS,)), dma((2,)), dma((2, 2)), dma((2, 2)), dma((3,)), dma((3, 4)), dma((2,)),
-            dma((PAIRS, 3, 3)), dma((PAIRS, 3, 3)), dma, dma((CHIPS,)), dma((4,)), dma((4,)), dma, dma((128,)), dma, dma, dma((CHIPS,))],
+            dma((PAIRS, 3, 3)), dma((PAIRS, 3, 3)), dma, dma((CHIPS,)), dma((4,)), dma((4,)), dma, dma((128,)), dma, dma, dma((CHIPS,)), dma((2,))],
         compiler_params=pltpu.CompilerParams(has_side_effects=True, collective_id=0, vmem_limit_bytes=62 * 1024 * 1024), name="attend",
     )(x, rand_idx, wq, wk, wv, wo)
 
@@ -451,6 +488,6 @@
     rep_spec = P(None, None)
 
     def local_fn(tokens, w_query, w_key, w_value, w_out, rand_idx):
-        return attend(tokens, rand_idx, w_query, w_key, w_value, w_out).astype(jnp.bfloat16)
+        return attend(tokens, rand_idx, w_query, w_key, w_value, w_out)
 
     return jax.shard_map(local_fn, mesh=mesh, in_specs=(row_spec, rep_spec, rep_spec, rep_spec, rep_spec, row_spec), out_specs=row_spec, check_vma=False)

time: 102 us -> 98.2 us (0.963)
  Pallas kernels: 99.2 us -> 95.8 us
  other arithmetic: 2.71 us -> 0 us
  local copies, waits for them, and re-layouts: 0 us -> 2.3 us
    pallas_call x1, Pallas kernels: 99.2 us -> 95.8 us  [attend(): pl.pallas_call(kernel, out_shape=jax.ShapeDtypeStruct((256, WIDTH), bf16)...]
    convert_element_type x1 -> x0, other arithmetic: 2.71 us -> none  [local_fn(): attend(tokens, rand_idx, w_query, w_key, w_value, w_out)]
    unnamed x0 -> x1, local copies, waits for them, and re-layouts: none -> 2.3 us
where the time goes in v7:
time: 98.2 us; the launch traced here: 98.1 us
  Pallas kernels  95.8 us (98%)
  local copies, waits for them, and re-layouts  2.3 us (2%)
    pallas_call x1, Pallas kernels, attend(): pl.pallas_call(kernel, out_shape=jax.ShapeDtypeStruct((256, WIDTH), bf16)...  95.8 us
    unnamed x1, local copies, waits for them, and re-layouts  2.3 us

profile of v7, /device:TPU:0, one launch (start us, length us, event | category | flops | bytes accessed | tf_op | source)
XLA Modules:
  0.0 98.1 jit_solution(13028647540713021874)
XLA Ops:
  0.0 95.8 %attend.1 = bf16[256,2048]{1,0:T(8,128)(2,1)} custom-call(bf16[256,2048]{1,0:T(8,128)(2,1)} %x_ref.1, s32[4,3]{1,0:T(4,128)} %rand_ref.1, bf16[2048,2048]{1,0:T(8,128)(2,1)} %wq_ref.1, bf16[2048,2048]{1,0:T(8,128)(2,1)} %wk_ref.1, bf16[2048,2048]{1,0:T(8,128)(2,1)} %wv_ref.1, bf16[2048,2048]{1,0:T(8,128)(2,1)} %wo_ref.1), custom_call_target="tpu_custom_call" | custom-call | tf_op jit(solution)/shard_map/attend/pallas_call | solution.py:467
  95.8 2.3 %copy.8 = bf16[256,2048]{1,0:T(8,128)(2,1)} copy(bf16[256,2048]{1,0:T(8,128)(2,1)} %attend.1) | data formatting | bytes 2097152

commit v8 on v6

--- a/solution.py
+++ b/solution.py
@@ -12,6 +12,7 @@
 HALF = 1024
 CHIPS = 64
 PAIRS = 8
+ALL = (PAIRS,) + tuple(range(PAIRS))
 NEG = -1e30
 FAR = 1 << 20
 MESH = pl.DeviceIdType.MESH
@@ -48,9 +49,9 @@
 
 
 def kernel(x_ref, rand_ref, wq_ref, wk_ref, wv_ref, wo_ref, y_ref,
-           idx_ref, full_ref, wo_buf, xs, xc, recv, w_buf, idx_all, sel, other, q_ref, k_ref, v_ref, gath, hot, o_ref, part, parts, glob, piece, near_s, slot_s, queries_in, queries_g,
+           idx_ref, full_ref, wo_buf, xs, xc, recv, w_buf, idx_all, sel, other, q_ref, k_ref, v_ref, gath, hot, o_ref, part, parts, glob, piece, near_s, slot_s, gath_q, queries_t, acc,
            s_send, s_recv, i_send, i_recv, x_sem, h_send, h_recv, loc, w_sem, p_sem, g_send, g_recv,
-           c_send, c_recv, o_send, o_recv, e_send, e_recv, wo_sem, b_send, b_recv):
+           c_send, c_recv, o_send, o_recv, e_send, e_recv, wo_sem):
     dev = lax.axis_index("seq")
     chip, core = dev // 2, dev % 2
     partner = dev + 1 - 2 * core
@@ -185,9 +186,6 @@
         for kv in range(2):
             for side in range(2):
                 halo(kv, side).start()
-
-    def query_copy(dst_chip, src_chip):
-        return remote(queries_in.at[chip], queries_in.at[src_chip], b_send, b_recv.at[src_chip], 2 * dst_chip + core)
 
     with jax.named_scope("select"):
         for s in range(SLOTS):
@@ -205,12 +203,7 @@
         rows = jnp.concatenate([moved[16 * j:16 * j + 16] for j in range(16)], axis=1)
         gq = jnp.dot(rows, w_buf[0], preferred_element_type=jnp.float32)
         gq = jnp.concatenate([gq[t:t + 1, 128 * j:128 * j + 128] for t in range(2) for j in range(PAIRS)], axis=0)
-        queries_in[chip] = gq.astype(jnp.bfloat16)
-
-        def start_query(i, carry):
-            query_copy(chip ^ i, chip).start()
-            return carry
-        lax.fori_loop(1, CHIPS, start_query, 0, unroll=7)
+        gath_q[0, coord[2], coord[1], coord[0]] = gq.astype(jnp.bfloat16)
         out = [jnp.dot(rows, w_buf[i], preferred_element_type=jnp.float32) for i in (1, 2)]
         for j in range(PAIRS):
             cols = slice(128 * j, 128 * j + 128)
@@ -226,7 +219,8 @@
             at = list(coord)
             if receive:
                 at[axis] = lax.rem(coord[axis] + 4 - k, 4)
-            ref = gath.at[(j,) + tuple(slice(None) if a in order[:stage] else at[a] for a in (2, 1, 0))]
+            buf, at_j = (gath, j) if j < PAIRS else (gath_q, 0)
+            ref = buf.at[(at_j,) + tuple(slice(None) if a in order[:stage] else at[a] for a in (2, 1, 0))]
             out.append(remote(ref, ref, g_send.at[j, stage, k - 1], g_recv.at[j, stage, k - 1],
                               dev + 2 * scale[axis] * (to - coord[axis])))
         return out
@@ -240,22 +234,22 @@
                 c.start()
 
     with jax.named_scope("gather0"):
-        for j in range(PAIRS):
+        for j in ALL:
             advance(j, 0)
     with jax.named_scope("gather1"):
-        for j in range(PAIRS):
+        for j in ALL:
             advance(j, 1)
-    def wait_query(i, carry):
-        query_copy(chip ^ i, chip ^ i).wait()
-        return carry
+    with jax.named_scope("gather2"):
+        for j in ALL:
+            advance(j, 2)
+
     with jax.named_scope("wait_queries"):
-        lax.fori_loop(1, CHIPS, wait_query, 0)
+        advance(PAIRS, 3)
 
     def unpack_queries(z, carry):
-        rows = queries_in[pl.ds(16 * z, 16)].reshape(256, 128)
-        moved = jnp.dot(perm, rows, preferred_element_type=jnp.float32).astype(jnp.bfloat16)
-        for s in range(16):
-            queries_g[s, aligned(z, 16), :] = moved[16 * s:16 * s + 16]
+        moved = jnp.dot(perm, gath_q[0, z].reshape(256, 128), preferred_element_type=jnp.float32).astype(jnp.bfloat16)
+        for s in range(SLOTS):
+            queries_t[s, aligned(z, 16), :] = moved[16 * s:16 * s + 16]
         return carry
 
     def glob_part(wave, carry):
@@ -263,7 +257,7 @@
         for t in range(2):
             j = 2 * wave + t
             cols = aligned(j, 128)
-            gq = jnp.concatenate([queries_g[j], queries_g[PAIRS + j]], axis=0)
+            gq = jnp.concatenate([queries_t[j], queries_t[PAIRS + j]], axis=0)
             queries = split_heads(gq, 128) * jnp.bfloat16(0.125)
             scores = lax.dot_general(k_ref[BLK:9 * BLK, cols], queries, NT, preferred_element_type=jnp.float32)
             top = jnp.max(scores, axis=0, keepdims=True)
@@ -277,24 +271,19 @@
         stats = jnp.concatenate(sums + tops + [jnp.zeros((120, 128), jnp.float32)], axis=0)
         part[wave, :, 256:384] = stats.T
         return carry
+
+    def part_copy(dst_chip, slot):
+        return remote(part.at[dst_chip >> 4, aligned(dst_chip & 15, 8)], parts.at[slot], c_send, c_recv.at[slot], 2 * dst_chip + core)
+
+    def start_part(i, carry):
+        part_copy(chip ^ i, chip).start()
+        return carry
     with jax.named_scope("globpart"):
         lax.fori_loop(0, 4, unpack_queries, 0)
         lax.fori_loop(0, 4, glob_part, 0)
-
-    def part_copy(dst_chip, slot):
-        return remote(part.at[dst_chip >> 4, aligned(dst_chip & 15, 8)], parts.at[slot], c_send, c_recv.at[slot], 2 * dst_chip + core)
-
-    def start_part(i, carry):
-        part_copy(chip ^ i, chip).start()
-        return carry
-    with jax.named_scope("gather2"):
-        for j in range(4):
-            advance(j, 2)
         lax.fori_loop(1, CHIPS, start_part, 0, unroll=7)
         own_part = pltpu.make_async_copy(part.at[chip >> 4, aligned(chip & 15, 8)], parts.at[chip], loc.at[1])
         own_part.start()
-        for j in range(4, PAIRS):
-            advance(j, 2)
 
     with jax.named_scope("halo"):
         for kv in range(2):
@@ -307,38 +296,11 @@
         return remote(o_ref.at[aligned(rows_of, 256), aligned(wave, 256)],
                       full_ref.at[:, aligned(cols_of * 4 + wave, 256)], o_send.at[wave], o_recv.at[wave], partner)
 
-    def wait_part(i, carry):
-        part_copy(chip ^ i, chip ^ i).wait()
-        return carry
-
-    def glob_slice(src_chip, src_core):
-        return glob.at[aligned(src_chip % 16, 8), aligned(src_core * 4 + src_chip // 16, 256)]
-
-    def glob_copy(src_chip, src_core):
-        return remote(piece, glob_slice(src_chip, src_core), e_send, e_recv.at[2 * src_chip + src_core], 0)
-
-    def combine():
-        with jax.named_scope("wait_parts"):
-            lax.fori_loop(1, CHIPS, wait_part, 0)
-            own_part.wait()
-        with jax.named_scope("combine"):
-            top = lax.fori_loop(0, CHIPS, lambda i, t: jnp.maximum(t, parts[i, :, 256:384]), jnp.full((8, 128), NEG, jnp.float32), unroll=8)
-
-            def add(i, carry):
-                num, den = carry
-                weight = pltpu.roll(jnp.exp(parts[i, :, 256:384] - top), 124, 1)
-                wide = jnp.concatenate([jnp.broadcast_to(weight[:, t:t + 1], (8, HEAD_DIM)) for t in range(4)], axis=1)
-                return num + wide * parts[i, :, 0:256], den + weight * parts[i, :, 256:384]
-            num, den = lax.fori_loop(0, CHIPS, add, (jnp.zeros((8, 256), jnp.float32), jnp.zeros((8, 128), jnp.float32)), unroll=8)
-            wide = jnp.concatenate([jnp.broadcast_to(den[:, t:t + 1], (8, HEAD_DIM)) for t in range(4)], axis=1)
-            piece[...] = (num / wide).astype(jnp.bfloat16)
-
-            @pl.when(dev != 0)
-            def _():
-                glob_copy(chip, core).start()
-
     def one_wave(wave, carry):
-        pl.when(wave == 3)(combine)
+        @pl.when(wave > 0)
+        def _():
+            with jax.named_scope("out_part"):
+                project_out(wave - 1, False)
         with jax.named_scope("wait_wave"):
             for w in range(4):
                 @pl.when(wave == w)
@@ -379,25 +341,79 @@
                     probs = probs * (1.0 / jnp.sum(probs, axis=0, keepdims=True))
                     out = lax.dot_general(probs.astype(jnp.bfloat16), vals, TN, preferred_element_type=jnp.float32)
                     o_ref[rows, cols] = join_heads(out, BLK).astype(jnp.bfloat16)
+        own_o(wave).start()
         o_copy(wave, 1 - core, core).start()
         return carry
+
+    def own_o(wave):
+        return pltpu.make_async_copy(o_ref.at[aligned(core, 256), aligned(wave, 256)], full_ref.at[:, aligned(4 * core + wave, 256)], loc.at[0])
+
+    def project_out(wave, last):
+        own_o(wave).wait()
+        o_copy(wave, 1 - core, core).wait_send()
+        o_copy(wave, core, 1 - core).wait_recv()
+
+        def tile(t, carry):
+            cols = aligned(t, 256)
+            total = acc[:, cols]
+            for c in range(2):
+                heads = aligned(4 * c + wave, 256)
+                total = total + lax.dot_general(full_ref[:, heads], wo_buf[cols, heads], NT, preferred_element_type=jnp.float32)
+            if last:
+                y_ref[:, cols] = total.astype(jnp.bfloat16)
+            else:
+                acc[:, cols] = total
+            return carry
+        lax.fori_loop(0, PAIRS, tile, 0)
+
+    with jax.named_scope("zero"):
+        acc[...] = jnp.zeros_like(acc)
+        wo_copy.wait()
     lax.fori_loop(0, 4, one_wave, 0)
 
     with jax.named_scope("local"):
-        mine = pltpu.make_async_copy(o_ref.at[aligned(core, 256)], full_ref.at[:, aligned(core, HALF)], loc.at[0])
-        mine.start()
-        for j in range(PAIRS):
+        for j in ALL:
             for stage in range(3):
                 for c in copies(j, stage, False):
                     c.wait_send()
-        mine.wait()
-
-    with jax.named_scope("wait_o"):
-        for wave in range(4):
-            o_copy(wave, 1 - core, core).wait_send()
-            o_copy(wave, core, 1 - core).wait_recv()
-        wo_copy.wait()
-
+
+    def wait_part(i, carry):
+        part_copy(chip ^ i, chip ^ i).wait()
+        return carry
+    with jax.named_scope("wait_parts"):
+        lax.fori_loop(1, CHIPS, wait_part, 0)
+        own_part.wait()
+
+    with jax.named_scope("combine"):
+        top = lax.fori_loop(0, CHIPS, lambda i, t: jnp.maximum(t, parts[i, :, 256:384]), jnp.full((8, 128), NEG, jnp.float32), unroll=8)
+
+        def add(i, carry):
+            num, den = carry
+            weight = pltpu.roll(jnp.exp(parts[i, :, 256:384] - top), 124, 1)
+            wide = jnp.concatenate([jnp.broadcast_to(weight[:, t:t + 1], (8, HEAD_DIM)) for t in range(4)], axis=1)
+            return num + wide * parts[i, :, 0:256], den + weight * parts[i, :, 256:384]
+        num, den = lax.fori_loop(0, CHIPS, add, (jnp.zeros((8, 256), jnp.float32), jnp.zeros((8, 128), jnp.float32)), unroll=8)
+        wide = jnp.concatenate([jnp.broadcast_to(den[:, t:t + 1], (8, HEAD_DIM)) for t in range(4)], axis=1)
+        piece[...] = (num / wide).astype(jnp.bfloat16)
+
+    def glob_slice(src_chip, src_core):
+        return glob.at[aligned(src_chip % 16, 8), aligned(src_core * 4 + src_chip // 16, 256)]
+
+    def glob_copy(src_chip, src_core):
+        return remote(piece, glob_slice(src_chip, src_core), e_send, e_recv.at[2 * src_chip + src_core], 0)
+
+    def project_glob(t, carry):
+        cols = aligned(t, 256)
+        y_ref[0:128, cols] = lax.dot_general(glob[...], wo_buf[cols, :], NT, preferred_element_type=jnp.float32).astype(jnp.bfloat16)
+        return carry
+
+    @pl.when(dev != 0)
+    def _():
+        glob_copy(chip, core).start()
+    with jax.named_scope("out"):
+        project_out(3, True)
+
+    with jax.named_scope("tail"):
         @pl.when(dev != 0)
         def _():
             glob_copy(chip, core).wait_send()
@@ -412,14 +428,7 @@
                 glob_copy(i // 2, i % 2).wait_recv()
                 return carry
             lax.fori_loop(1, 128, wait_glob, 0)
-            full_ref[0:128, :] = glob[...]
-
-    def project_out(t, carry):
-        cols = aligned(t, 256)
-        y_ref[:, cols] = lax.dot_general(full_ref[...], wo_buf[cols, :], NT, preferred_element_type=jnp.float32)
-        return carry
-    with jax.named_scope("out"):
-        lax.fori_loop(0, 8, project_out, 0)
+            lax.fori_loop(0, PAIRS, project_glob, 0)
 
 
 def attend(x, rand_idx, wq, wk, wv, wo):
@@ -429,7 +438,7 @@
     bf16, f32 = jnp.bfloat16, jnp.float32
     return pl.pallas_call(
         kernel,
-        out_shape=jax.ShapeDtypeStruct((256, WIDTH), f32),
+        out_shape=jax.ShapeDtypeStruct((256, WIDTH), bf16),
         in_specs=[vmem, pl.BlockSpec(memory_space=pltpu.SMEM), hbm, hbm, hbm, hbm], out_specs=vmem,
         scratch_shapes=[
             VMEM((1, 128), jnp.int32), VMEM((256, WIDTH), bf16), VMEM((WIDTH, WIDTH), bf16),
@@ -439,9 +448,9 @@
             VMEM((PAIRS, 4, 4, 4, SLOTS, 256), bf16), VMEM((PAIRS, SLOTS, BLK, 256), bf16), VMEM((512, HALF), bf16),
             VMEM((4, 128, 384), f32), VMEM((CHIPS, 8, 384), f32), VMEM((128, WIDTH), bf16), VMEM((8, 256), bf16),
             pltpu.SMEM((2, 1, 128), jnp.int32), pltpu.SMEM((24,), jnp.int32),
-            VMEM((CHIPS, 16, 128), bf16), VMEM((16, BLK, 128), bf16),
+            VMEM((1, 4, 4, 4, SLOTS, 128), bf16), VMEM((SLOTS, BLK, 128), bf16), VMEM((256, WIDTH), f32),
             dma, dma((CHIPS,)), dma((3,)), dma((CHIPS,)), dma((2,)), dma((2, 2)), dma((2, 2)), dma((3,)), dma((3, 4)), dma((2,)),
-            dma((PAIRS, 3, 3)), dma((PAIRS, 3, 3)), dma, dma((CHIPS,)), dma((4,)), dma((4,)), dma, dma((128,)), dma, dma, dma((CHIPS,))],
+            dma((PAIRS + 1, 3, 3)), dma((PAIRS + 1, 3, 3)), dma, dma((CHIPS,)), dma((4,)), dma((4,)), dma, dma((128,)), dma],
         compiler_params=pltpu.CompilerParams(has_side_effects=True, collective_id=0, vmem_limit_bytes=62 * 1024 * 1024), name="attend",
     )(x, rand_idx, wq, wk, wv, wo)
 
@@ -451,6 +460,6 @@
     rep_spec = P(None, None)
 
     def local_fn(tokens, w_query, w_key, w_value, w_out, rand_idx):
-        return attend(tokens, rand_idx, w_query, w_key, w_value, w_out).astype(jnp.bfloat16)
+        return attend(tokens, rand_idx, w_query, w_key, w_value, w_out)
 
     return jax.shard_map(local_fn, mesh=mesh, in_specs=(row_spec, rep_spec, rep_spec, rep_spec, rep_spec, row_spec), out_specs=row_spec, check_vma=False)

time: 102 us -> 99 us (0.971)
  other arithmetic: 2.71 us -> 0 us
  Pallas kernels: 99.2 us -> 96.6 us
  local copies, waits for them, and re-layouts: 0 us -> 2.3 us
    convert_element_type x1 -> x0, other arithmetic: 2.71 us -> none  [local_fn(): attend(tokens, rand_idx, w_query, w_key, w_value, w_out)]
    pallas_call x1, Pallas kernels: 99.2 us -> 96.6 us  [attend(): pl.pallas_call(kernel, out_shape=jax.ShapeDtypeStruct((256, WIDTH), bf16)...]
    unnamed x0 -> x1, local copies, waits for them, and re-layouts: none -> 2.3 us
where the time goes in v8:
time: 99 us; the launch traced here: 98.9 us
  Pallas kernels  96.6 us (98%)
  local copies, waits for them, and re-layouts  2.3 us (2%)
    pallas_call x1, Pallas kernels, attend(): pl.pallas_call(kernel, out_shape=jax.ShapeDtypeStruct((256, WIDTH), bf16)...  96.6 us
    unnamed x1, local copies, waits for them, and re-layouts  2.3 us

profile of v8, /device:TPU:0, one launch (start us, length us, event | category | flops | bytes accessed | tf_op | source)
XLA Modules:
  0.0 98.9 jit_solution(4191627209310405257)
XLA Ops:
  0.0 96.6 %attend.1 = bf16[256,2048]{1,0:T(8,128)(2,1)} custom-call(bf16[256,2048]{1,0:T(8,128)(2,1)} %x_ref.1, s32[4,3]{1,0:T(4,128)} %rand_ref.1, bf16[2048,2048]{1,0:T(8,128)(2,1)} %wq_ref.1, bf16[2048,2048]{1,0:T(8,128)(2,1)} %wk_ref.1, bf16[2048,2048]{1,0:T(8,128)(2,1)} %wv_ref.1, bf16[2048,2048]{1,0:T(8,128)(2,1)} %wo_ref.1), custom_call_target="tpu_custom_call" | custom-call | tf_op jit(solution)/shard_map/attend/pallas_call | solution.py:439
  96.6 2.3 %copy.8 = bf16[256,2048]{1,0:T(8,128)(2,1)} copy(bf16[256,2048]{1,0:T(8,128)(2,1)} %attend.1) | data formatting | bytes 2097152

commit v9 on v8

--- a/solution.py
+++ b/solution.py
@@ -49,9 +49,9 @@
 
 
 def kernel(x_ref, rand_ref, wq_ref, wk_ref, wv_ref, wo_ref, y_ref,
-           idx_ref, full_ref, wo_buf, xs, xc, recv, w_buf, idx_all, sel, other, q_ref, k_ref, v_ref, gath, hot, o_ref, part, parts, glob, piece, near_s, slot_s, gath_q, queries_t, acc,
+           idx_ref, full_ref, wo_buf, xs, xc, recv, w_buf, idx_all, sel, other, q_ref, k_ref, v_ref, gath, hot, o_ref, part, parts, glob, piece, near_s, slot_s, gath_q, queries_t, y_buf, wo_t,
            s_send, s_recv, i_send, i_recv, x_sem, h_send, h_recv, loc, w_sem, p_sem, g_send, g_recv,
-           c_send, c_recv, o_send, o_recv, e_send, e_recv, wo_sem):
+           c_send, c_recv, o_send, o_recv, e_send, e_recv, wo_sem, own_sem, y_sem):
     dev = lax.axis_index("seq")
     chip, core = dev // 2, dev % 2
     partner = dev + 1 - 2 * core
@@ -236,9 +236,18 @@
     with jax.named_scope("gather0"):
         for j in ALL:
             advance(j, 0)
+    def turn(i, carry):
+        a, b = aligned(i >> 3, 256), aligned(i & 7, 256)
+        wo_t[a, b] = wo_buf[b, a].T
+        return carry
+    with jax.named_scope("turn"):
+        wo_copy.wait()
+        lax.fori_loop(0, 32, turn, 0)
     with jax.named_scope("gather1"):
         for j in ALL:
             advance(j, 1)
+    with jax.named_scope("turn2"):
+        lax.fori_loop(32, CHIPS, turn, 0)
     with jax.named_scope("gather2"):
         for j in ALL:
             advance(j, 2)
@@ -297,10 +306,6 @@
                       full_ref.at[:, aligned(cols_of * 4 + wave, 256)], o_send.at[wave], o_recv.at[wave], partner)
 
     def one_wave(wave, carry):
-        @pl.when(wave > 0)
-        def _():
-            with jax.named_scope("out_part"):
-                project_out(wave - 1, False)
         with jax.named_scope("wait_wave"):
             for w in range(4):
                 @pl.when(wave == w)
@@ -346,29 +351,8 @@
         return carry
 
     def own_o(wave):
-        return pltpu.make_async_copy(o_ref.at[aligned(core, 256), aligned(wave, 256)], full_ref.at[:, aligned(4 * core + wave, 256)], loc.at[0])
-
-    def project_out(wave, last):
-        own_o(wave).wait()
-        o_copy(wave, 1 - core, core).wait_send()
-        o_copy(wave, core, 1 - core).wait_recv()
-
-        def tile(t, carry):
-            cols = aligned(t, 256)
-            total = acc[:, cols]
-            for c in range(2):
-                heads = aligned(4 * c + wave, 256)
-                total = total + lax.dot_general(full_ref[:, heads], wo_buf[cols, heads], NT, preferred_element_type=jnp.float32)
-            if last:
-                y_ref[:, cols] = total.astype(jnp.bfloat16)
-            else:
-                acc[:, cols] = total
-            return carry
-        lax.fori_loop(0, PAIRS, tile, 0)
-
-    with jax.named_scope("zero"):
-        acc[...] = jnp.zeros_like(acc)
-        wo_copy.wait()
+        return pltpu.make_async_copy(o_ref.at[aligned(core, 256), aligned(wave, 256)], full_ref.at[:, aligned(4 * core + wave, 256)], own_sem.at[wave])
+
     lax.fori_loop(0, 4, one_wave, 0)
 
     with jax.named_scope("local"):
@@ -402,16 +386,37 @@
     def glob_copy(src_chip, src_core):
         return remote(piece, glob_slice(src_chip, src_core), e_send, e_recv.at[2 * src_chip + src_core], 0)
 
-    def project_glob(t, carry):
-        cols = aligned(t, 256)
-        y_ref[0:128, cols] = lax.dot_general(glob[...], wo_buf[cols, :], NT, preferred_element_type=jnp.float32).astype(jnp.bfloat16)
-        return carry
-
     @pl.when(dev != 0)
     def _():
         glob_copy(chip, core).start()
+
+    def y_copy(half, t):
+        at = (pl.ds(128 * half, 128), aligned(t, 256))
+        return pltpu.make_async_copy(y_buf.at[at], y_ref.at[at], y_sem.at[half, t])
+
+    def project_out(t, carry):
+        cols = aligned(t, 256)
+        y_buf[:, cols] = jnp.dot(full_ref[...], wo_t[:, cols], preferred_element_type=jnp.float32).astype(jnp.bfloat16)
+        y_copy(1, t).start()
+
+        @pl.when(dev != 0)
+        def _():
+            y_copy(0, t).start()
+        return carry
+
+    def project_glob(t, carry):
+        cols = aligned(t, 256)
+        y_buf[0:128, cols] = jnp.dot(glob[...], wo_t[:, cols], preferred_element_type=jnp.float32).astype(jnp.bfloat16)
+        y_copy(0, t).start()
+        return carry
+
+    with jax.named_scope("wait_o"):
+        for wave in range(4):
+            own_o(wave).wait()
+            o_copy(wave, 1 - core, core).wait_send()
+            o_copy(wave, core, 1 - core).wait_recv()
     with jax.named_scope("out"):
-        project_out(3, True)
+        lax.fori_loop(0, PAIRS, project_out, 0)
 
     with jax.named_scope("tail"):
         @pl.when(dev != 0)
@@ -429,6 +434,12 @@
                 return carry
             lax.fori_loop(1, 128, wait_glob, 0)
             lax.fori_loop(0, PAIRS, project_glob, 0)
+
+        def written(t, carry):
+            y_copy(0, t).wait()
+            y_copy(1, t).wait()
+            return carry
+        lax.fori_loop(0, PAIRS, written, 0)
 
 
 def attend(x, rand_idx, wq, wk, wv, wo):
@@ -439,7 +450,7 @@
     return pl.pallas_call(
         kernel,
         out_shape=jax.ShapeDtypeStruct((256, WIDTH), bf16),
-        in_specs=[vmem, pl.BlockSpec(memory_space=pltpu.SMEM), hbm, hbm, hbm, hbm], out_specs=vmem,
+        in_specs=[vmem, pl.BlockSpec(memory_space=pltpu.SMEM), hbm, hbm, hbm, hbm], out_specs=hbm,
         scratch_shapes=[
             VMEM((1, 128), jnp.int32), VMEM((256, WIDTH), bf16), VMEM((WIDTH, WIDTH), bf16),
             VMEM((CHIPS, 4, 16, 128), bf16), VMEM((512, WIDTH), bf16), VMEM((4 * CHIPS, 16, 128), bf16),
@@ -448,9 +459,9 @@
             VMEM((PAIRS, 4, 4, 4, SLOTS, 256), bf16), VMEM((PAIRS, SLOTS, BLK, 256), bf16), VMEM((512, HALF), bf16),
             VMEM((4, 128, 384), f32), VMEM((CHIPS, 8, 384), f32), VMEM((128, WIDTH), bf16), VMEM((8, 256), bf16),
             pltpu.SMEM((2, 1, 128), jnp.int32), pltpu.SMEM((24,), jnp.int32),
-            VMEM((1, 4, 4, 4, SLOTS, 128), bf16), VMEM((SLOTS, BLK, 128), bf16), VMEM((256, WIDTH), f32),
+            VMEM((1, 4, 4, 4, SLOTS, 128), bf16), VMEM((SLOTS, BLK, 128), bf16), VMEM((256, WIDTH), bf16), VMEM((WIDTH, WIDTH), bf16),
             dma, dma((CHIPS,)), dma((3,)), dma((CHIPS,)), dma((2,)), dma((2, 2)), dma((2, 2)), dma((3,)), dma((3, 4)), dma((2,)),
-            dma((PAIRS + 1, 3, 3)), dma((PAIRS + 1, 3, 3)), dma, dma((CHIPS,)), dma((4,)), dma((4,)), dma, dma((128,)), dma],
+            dma((PAIRS + 1, 3, 3)), dma((PAIRS + 1, 3, 3)), dma, dma((CHIPS,)), dma((4,)), dma((4,)), dma, dma((128,)), dma, dma((4,)), dma((2, PAIRS))],
         compiler_params=pltpu.CompilerParams(has_side_effects=True, collective_id=0, vmem_limit_bytes=62 * 1024 * 1024), name="attend",
     )(x, rand_idx, wq, wk, wv, wo)
 

time: 99 us -> 93.5 us (0.944)
  Pallas kernels: 96.6 us -> 91 us
    pallas_call x1, Pallas kernels: 96.6 us -> 91 us  [attend(): pl.pallas_call(kernel, out_shape=jax.ShapeDtypeStruct((256, WIDTH), bf16)...]
where the time goes in v9:
time: 93.5 us; the launch traced here: 93.3 us
  Pallas kernels  91 us (97%)
  local copies, waits for them, and re-layouts  2.3 us (2%)
    pallas_call x1, Pallas kernels, attend(): pl.pallas_call(kernel, out_shape=jax.ShapeDtypeStruct((256, WIDTH), bf16)...  91 us
    unnamed x1, local copies, waits for them, and re-layouts  2.3 us

profile of v9, /device:TPU:0, one launch (start us, length us, event | category | flops | bytes accessed | tf_op | source)
XLA Modules:
  0.0 93.3 jit_solution(15644312788962716035)
XLA Ops:
  0.0 91.0 %attend.1 = bf16[256,2048]{1,0:T(8,128)(2,1)} custom-call(bf16[256,2048]{1,0:T(8,128)(2,1)} %x_ref.1, s32[4,3]{1,0:T(4,128)} %rand_ref.1, bf16[2048,2048]{1,0:T(8,128)(2,1)} %wq_ref.1, bf16[2048,2048]{1,0:T(8,128)(2,1)} %wk_ref.1, bf16[2048,2048]{1,0:T(8,128)(2,1)} %wv_ref.1, bf16[2048,2048]{1,0:T(8,128)(2,1)} %wo_ref.1), custom_call_target="tpu_custom_call" | custom-call | tf_op jit(solution)/shard_map/attend/pallas_call | solution.py:450
  91.0 2.3 %copy.8 = bf16[256,2048]{1,0:T(8,128)(2,1)} copy(bf16[256,2048]{1,0:T(8,128)(2,1)} %attend.1) | data formatting | bytes 2097152

commit v10 on v9

--- a/solution.py
+++ b/solution.py
@@ -49,7 +49,7 @@
 
 
 def kernel(x_ref, rand_ref, wq_ref, wk_ref, wv_ref, wo_ref, y_ref,
-           idx_ref, full_ref, wo_buf, xs, xc, recv, w_buf, idx_all, sel, other, q_ref, k_ref, v_ref, gath, hot, o_ref, part, parts, glob, piece, near_s, slot_s, gath_q, queries_t, y_buf, wo_t,
+           idx_ref, full_ref, wo_buf, xs, xc, recv, w_buf, idx_all, sel, other, q_ref, k_ref, v_ref, gath, hot, o_ref, part, parts, glob, piece, near_s, slot_s, gath_q, queries_t, y_buf,
            s_send, s_recv, i_send, i_recv, x_sem, h_send, h_recv, loc, w_sem, p_sem, g_send, g_recv,
            c_send, c_recv, o_send, o_recv, e_send, e_recv, wo_sem, own_sem, y_sem):
     dev = lax.axis_index("seq")
@@ -177,15 +177,17 @@
                     at = at + jnp.where(h < named, 1, 0)
                 slot_s[3 * b + t] = at
 
+    with jax.named_scope("issue_halos"):
+        for kv in range(2):
+            for side in range(2):
+                halo(kv, side).start()
+
     def wait_row(i, carry):
         row_copy(chip ^ i, chip ^ i).wait()
         return carry
     with jax.named_scope("wait_rows"):
         lax.fori_loop(1, CHIPS, wait_row, 0)
         own_row.wait()
-        for kv in range(2):
-            for side in range(2):
-                halo(kv, side).start()
 
     with jax.named_scope("select"):
         for s in range(SLOTS):
@@ -236,18 +238,9 @@
     with jax.named_scope("gather0"):
         for j in ALL:
             advance(j, 0)
-    def turn(i, carry):
-        a, b = aligned(i >> 3, 256), aligned(i & 7, 256)
-        wo_t[a, b] = wo_buf[b, a].T
-        return carry
-    with jax.named_scope("turn"):
-        wo_copy.wait()
-        lax.fori_loop(0, 32, turn, 0)
     with jax.named_scope("gather1"):
         for j in ALL:
             advance(j, 1)
-    with jax.named_scope("turn2"):
-        lax.fori_loop(32, CHIPS, turn, 0)
     with jax.named_scope("gather2"):
         for j in ALL:
             advance(j, 2)
@@ -279,18 +272,22 @@
                 tops.append(top[:, 128 * h:128 * h + 128])
         stats = jnp.concatenate(sums + tops + [jnp.zeros((120, 128), jnp.float32)], axis=0)
         part[wave, :, 256:384] = stats.T
-        return carry
+
+        def start_part(i, carry):
+            to = 16 * wave + (i ^ (chip & 15))
+
+            @pl.when(to != chip)
+            def _():
+                part_copy(to, chip).start()
+            return carry
+        return lax.fori_loop(0, 16, start_part, carry)
 
     def part_copy(dst_chip, slot):
         return remote(part.at[dst_chip >> 4, aligned(dst_chip & 15, 8)], parts.at[slot], c_send, c_recv.at[slot], 2 * dst_chip + core)
 
-    def start_part(i, carry):
-        part_copy(chip ^ i, chip).start()
-        return carry
     with jax.named_scope("globpart"):
         lax.fori_loop(0, 4, unpack_queries, 0)
         lax.fori_loop(0, 4, glob_part, 0)
-        lax.fori_loop(1, CHIPS, start_part, 0, unroll=7)
         own_part = pltpu.make_async_copy(part.at[chip >> 4, aligned(chip & 15, 8)], parts.at[chip], loc.at[1])
         own_part.start()
 
@@ -396,7 +393,7 @@
 
     def project_out(t, carry):
         cols = aligned(t, 256)
-        y_buf[:, cols] = jnp.dot(full_ref[...], wo_t[:, cols], preferred_element_type=jnp.float32).astype(jnp.bfloat16)
+        y_buf[:, cols] = lax.dot_general(full_ref[...], wo_buf[cols, :], NT, preferred_element_type=jnp.float32).astype(jnp.bfloat16)
         y_copy(1, t).start()
 
         @pl.when(dev != 0)
@@ -406,11 +403,12 @@
 
     def project_glob(t, carry):
         cols = aligned(t, 256)
-        y_buf[0:128, cols] = jnp.dot(glob[...], wo_t[:, cols], preferred_element_type=jnp.float32).astype(jnp.bfloat16)
+        y_buf[0:128, cols] = lax.dot_general(glob[...], wo_buf[cols, :], NT, preferred_element_type=jnp.float32).astype(jnp.bfloat16)
         y_copy(0, t).start()
         return carry
 
     with jax.named_scope("wait_o"):
+        wo_copy.wait()
         for wave in range(4):
             own_o(wave).wait()
             o_copy(wave, 1 - core, core).wait_send()
@@ -459,7 +457,7 @@
             VMEM((PAIRS, 4, 4, 4, SLOTS, 256), bf16), VMEM((PAIRS, SLOTS, BLK, 256), bf16), VMEM((512, HALF), bf16),
             VMEM((4, 128, 384), f32), VMEM((CHIPS, 8, 384), f32), VMEM((128, WIDTH), bf16), VMEM((8, 256), bf16),
             pltpu.SMEM((2, 1, 128), jnp.int32), pltpu.SMEM((24,), jnp.int32),
-            VMEM((1, 4, 4, 4, SLOTS, 128), bf16), VMEM((SLOTS, BLK, 128), bf16), VMEM((256, WIDTH), bf16), VMEM((WIDTH, WIDTH), bf16),
+            VMEM((1, 4, 4, 4, SLOTS, 128), bf16), VMEM((SLOTS, BLK, 128), bf16), VMEM((256, WIDTH), bf16),
             dma, dma((CHIPS,)), dma((3,)), dma((CHIPS,)), dma((2,)), dma((2, 2)), dma((2, 2)), dma((3,)), dma((3, 4)), dma((2,)),
             dma((PAIRS + 1, 3, 3)), dma((PAIRS + 1, 3, 3)), dma, dma((CHIPS,)), dma((4,)), dma((4,)), dma, dma((128,)), dma, dma((4,)), dma((2, PAIRS))],
         compiler_params=pltpu.CompilerParams(has_side_effects=True, collective_id=0, vmem_limit_bytes=62 * 1024 * 1024), name="attend",

time: 93.5 us -> 91 us (0.973)
  Pallas kernels: 91 us -> 88.6 us
    pallas_call x1, Pallas kernels: 91 us -> 88.6 us  [attend(): pl.pallas_call(kernel, out_shape=jax.ShapeDtypeStruct((256, WIDTH), bf16)...]
where the time goes in v10:
time: 91 us; the launch traced here: 90.9 us
  Pallas kernels  88.6 us (97%)
  local copies, waits for them, and re-layouts  2.3 us (3%)
    pallas_call x1, Pallas kernels, attend(): pl.pallas_call(kernel, out_shape=jax.ShapeDtypeStruct((256, WIDTH), bf16)...  88.6 us
    unnamed x1, local copies, waits for them, and re-layouts  2.3 us

profile of v10, /device:TPU:0, one launch (start us, length us, event | category | flops | bytes accessed | tf_op | source)
XLA Modules:
  0.0 90.9 jit_solution(12922366758997911309)
XLA Ops:
  0.0 88.6 %attend.1 = bf16[256,2048]{1,0:T(8,128)(2,1)} custom-call(bf16[256,2048]{1,0:T(8,128)(2,1)} %x_ref.1, s32[4,3]{1,0:T(4,128)} %rand_ref.1, bf16[2048,2048]{1,0:T(8,128)(2,1)} %wq_ref.1, bf16[2048,2048]{1,0:T(8,128)(2,1)} %wk_ref.1, bf16[2048,2048]{1,0:T(8,128)(2,1)} %wv_ref.1, bf16[2048,2048]{1,0:T(8,128)(2,1)} %wo_ref.1), custom_call_target="tpu_custom_call" | custom-call | tf_op jit(solution)/shard_map/attend/pallas_call | solution.py:448
  88.6 2.3 %copy.8 = bf16[256,2048]{1,0:T(8,128)(2,1)} copy(bf16[256,2048]{1,0:T(8,128)(2,1)} %attend.1) | data formatting | bytes 2097152

commit v11 on v10

--- a/solution.py
+++ b/solution.py
@@ -18,24 +18,27 @@
 MESH = pl.DeviceIdType.MESH
 VMEM = pltpu.VMEM
 ORDERS = ((0, 1, 2), (1, 2, 0), (2, 0, 1))
+TILE = 256
+LANES = 128
+NEAR = (1, 3)
 NT = (((1,), (1,)), ((), ()))
 TN = (((0,), (0,)), ((), ()))
 
 
 def permutation():
-    row = lax.broadcasted_iota(jnp.int32, (256, 256), 0)
-    col = lax.broadcasted_iota(jnp.int32, (256, 256), 1)
+    row = lax.broadcasted_iota(jnp.int32, (TILE, TILE), 0)
+    col = lax.broadcasted_iota(jnp.int32, (TILE, TILE), 1)
     return jnp.where(col == (row & 15) * 16 + (row >> 4), 1.0, 0.0).astype(jnp.bfloat16)
 
 
 def split_heads(pair, rows):
-    lane = lax.broadcasted_iota(jnp.int32, (rows, 128), 1)
+    lane = lax.broadcasted_iota(jnp.int32, (rows, LANES), 1)
     zero = jnp.zeros_like(pair)
     return jnp.concatenate([jnp.where(lane < HEAD_DIM, pair, zero), jnp.where(lane < HEAD_DIM, zero, pair)], axis=0)
 
 
 def join_heads(out, rows):
-    lane = lax.broadcasted_iota(jnp.int32, (rows, 128), 1)
+    lane = lax.broadcasted_iota(jnp.int32, (rows, LANES), 1)
     return jnp.where(lane < HEAD_DIM, out[:rows], out[rows:])
 
 
@@ -65,14 +68,14 @@
         pl.semaphore_signal(barrier, inc=1, device_id={"seq": dev ^ i}, device_id_type=MESH)
         return carry
     with jax.named_scope("greet"):
-        lax.fori_loop(1, 128, greet, 0, unroll=8)
+        lax.fori_loop(1, LANES, greet, 0, unroll=8)
 
     def w_copy(i, t):
         w = (wq_ref, wk_ref, wv_ref)[i]
-        return pltpu.make_async_copy(w.at[:, aligned(core * 4 + t, 256)], w_buf.at[i, :, aligned(t, 256)], w_sem.at[i, t])
+        return pltpu.make_async_copy(w.at[:, aligned(core * 4 + t, TILE)], w_buf.at[i, :, aligned(t, TILE)], w_sem.at[i, t])
 
     def x_swap(which):
-        return remote(x_ref, xc.at[aligned(which, 256)], x_sem.at[0], x_sem.at[1], partner)
+        return remote(x_ref, xc.at[aligned(which, TILE)], x_sem.at[0], x_sem.at[1], partner)
 
     def idx_copy(dst_chip, slot):
         return remote(idx_ref, idx_all.at[core, slot], i_send.at[0], i_recv.at[slot], 2 * dst_chip + core)
@@ -95,10 +98,10 @@
         for t in range(4):
             for i in range(3):
                 w_copy(i, t).start()
-        own_x = pltpu.make_async_copy(x_ref, xc.at[aligned(core, 256)], loc.at[1])
+        own_x = pltpu.make_async_copy(x_ref, xc.at[aligned(core, TILE)], loc.at[1])
         own_x.start()
-        named_lane = lax.broadcasted_iota(jnp.int32, (1, 128), 1)
-        line = jnp.full((1, 128), FAR, jnp.int32)
+        named_lane = lax.broadcasted_iota(jnp.int32, (1, LANES), 1)
+        line = jnp.full((1, LANES), FAR, jnp.int32)
         for e in range(12):
             line = jnp.where(named_lane == e, rand_ref[e // 3, e % 3], line)
         idx_ref[...] = line
@@ -107,7 +110,7 @@
     def relayout(step, carry):
         blk, group = step >> 2, step & 3
         rows = x_ref[aligned(step, 16), :]
-        rows = jnp.concatenate([rows[:, 128 * c:128 * c + 128] for c in range(16)], axis=0)
+        rows = jnp.concatenate([rows[:, LANES * c:LANES * c + LANES] for c in range(16)], axis=0)
         moved = jnp.dot(perm, rows, preferred_element_type=jnp.float32).astype(jnp.bfloat16)
         for a in range(16):
             xs[16 * group + a, blk] = moved[16 * a:16 * a + 16]
@@ -138,7 +141,7 @@
         x_swap(1 - core).wait_recv()
 
     def project(t, carry):
-        cols = aligned(t, 256)
+        cols = aligned(t, TILE)
         for i in range(3):
             w_copy(i, t).wait()
         rows = xc[...]
@@ -196,7 +199,7 @@
                 rows = recv[jnp.minimum((h >> 3) * 4 + (h & 3), 4 * CHIPS - 1)]
                 sel[16 * s:16 * s + 16, :] = jnp.where(((h >> 2) & 1) == core, rows, jnp.zeros_like(rows))
             else:
-                sel[16 * s:16 * s + 16, :] = jnp.zeros((16, 128), jnp.bfloat16)
+                sel[16 * s:16 * s + 16, :] = jnp.zeros((16, LANES), jnp.bfloat16)
         swap = remote(sel, other, p_sem.at[0], p_sem.at[1], partner)
         swap.start()
         swap.wait()
@@ -204,11 +207,11 @@
         moved = jnp.dot(perm, sel[...] + other[...], preferred_element_type=jnp.float32).astype(jnp.bfloat16)
         rows = jnp.concatenate([moved[16 * j:16 * j + 16] for j in range(16)], axis=1)
         gq = jnp.dot(rows, w_buf[0], preferred_element_type=jnp.float32)
-        gq = jnp.concatenate([gq[t:t + 1, 128 * j:128 * j + 128] for t in range(2) for j in range(PAIRS)], axis=0)
+        gq = jnp.concatenate([gq[t:t + 1, LANES * j:LANES * j + LANES] for t in range(2) for j in range(PAIRS)], axis=0)
         gath_q[0, coord[2], coord[1], coord[0]] = gq.astype(jnp.bfloat16)
         out = [jnp.dot(rows, w_buf[i], preferred_element_type=jnp.float32) for i in (1, 2)]
         for j in range(PAIRS):
-            cols = slice(128 * j, 128 * j + 128)
+            cols = slice(LANES * j, LANES * j + LANES)
             kv = jnp.concatenate([out[0][:, cols], out[1][:, cols]], axis=1)
             gath[j, coord[2], coord[1], coord[0]] = kv.astype(jnp.bfloat16)
 
@@ -216,7 +219,7 @@
         order = ORDERS[j % 3]
         axis = order[stage]
         out = []
-        for k in (1, 2, 3):
+        for k in NEAR if stage == 2 and j < PAIRS else (1, 2, 3):
             to = lax.rem(coord[axis] + k, 4)
             at = list(coord)
             if receive:
@@ -227,6 +230,28 @@
                               dev + 2 * scale[axis] * (to - coord[axis])))
         return out
 
+    def passed(j, receive):
+        order = ORDERS[j % 3]
+        axis = order[2]
+        out = []
+        for half, k in enumerate(NEAR):
+            at = list(coord)
+            at[axis] = lax.rem(coord[axis] + (2 if receive else 4 - k), 4)
+            ref = gath.at[(j,) + tuple(slice(None) if a in order[:2] else at[a] for a in (2, 1, 0)) + (slice(8 * half, 8 * half + 8),)]
+            to = lax.rem(coord[axis] + k, 4)
+            out.append(remote(ref, ref, g_send.at[j, 3, half], g_recv.at[j, 3, half], dev + 2 * scale[axis] * (to - coord[axis])))
+        return out
+
+    def pass_on(chunks):
+        for j in chunks:
+            for got, nxt in zip(copies(j, 2, True), passed(j, False)):
+                got.wait_recv()
+                nxt.start()
+
+    def arrived(j):
+        for c in passed(j, True):
+            c.wait_recv()
+
     def advance(j, stage):
         if stage:
             for c in copies(j, stage - 1, True):
@@ -242,14 +267,14 @@
         for j in ALL:
             advance(j, 1)
     with jax.named_scope("gather2"):
-        for j in ALL:
+        for j in ALL[:7]:
             advance(j, 2)
 
     with jax.named_scope("wait_queries"):
         advance(PAIRS, 3)
 
     def unpack_queries(z, carry):
-        moved = jnp.dot(perm, gath_q[0, z].reshape(256, 128), preferred_element_type=jnp.float32).astype(jnp.bfloat16)
+        moved = jnp.dot(perm, gath_q[0, z].reshape(TILE, LANES), preferred_element_type=jnp.float32).astype(jnp.bfloat16)
         for s in range(SLOTS):
             queries_t[s, aligned(z, 16), :] = moved[16 * s:16 * s + 16]
         return carry
@@ -258,20 +283,20 @@
         sums, tops = [], []
         for t in range(2):
             j = 2 * wave + t
-            cols = aligned(j, 128)
+            cols = aligned(j, LANES)
             gq = jnp.concatenate([queries_t[j], queries_t[PAIRS + j]], axis=0)
-            queries = split_heads(gq, 128) * jnp.bfloat16(0.125)
+            queries = split_heads(gq, LANES) * jnp.bfloat16(0.125)
             scores = lax.dot_general(k_ref[BLK:9 * BLK, cols], queries, NT, preferred_element_type=jnp.float32)
             top = jnp.max(scores, axis=0, keepdims=True)
             probs = jnp.exp(scores - top)
             total = jnp.sum(probs, axis=0, keepdims=True)
             out = lax.dot_general(probs.astype(jnp.bfloat16), v_ref[BLK:9 * BLK, cols], TN, preferred_element_type=jnp.float32)
-            part[wave, :, 128 * t:128 * t + 128] = join_heads(out, 128)
+            part[wave, :, LANES * t:LANES * t + LANES] = join_heads(out, LANES)
             for h in range(2):
-                sums.append(total[:, 128 * h:128 * h + 128])
-                tops.append(top[:, 128 * h:128 * h + 128])
-        stats = jnp.concatenate(sums + tops + [jnp.zeros((120, 128), jnp.float32)], axis=0)
-        part[wave, :, 256:384] = stats.T
+                sums.append(total[:, LANES * h:LANES * h + LANES])
+                tops.append(top[:, LANES * h:LANES * h + LANES])
+        stats = jnp.concatenate(sums + tops + [jnp.zeros((120, LANES), jnp.float32)], axis=0)
+        part[wave, :, TILE:384] = stats.T
 
         def start_part(i, carry):
             to = 16 * wave + (i ^ (chip & 15))
@@ -280,7 +305,18 @@
             def _():
                 part_copy(to, chip).start()
             return carry
-        return lax.fori_loop(0, 16, start_part, carry)
+        lax.fori_loop(0, 16, start_part, carry)
+
+        @pl.when(wave == 1)
+        def _():
+            pass_on((0, 1, 2))
+            for j in ALL[7:]:
+                advance(j, 2)
+
+        @pl.when(wave == 3)
+        def _():
+            pass_on((3, 4, 5))
+        return carry
 
     def part_copy(dst_chip, slot):
         return remote(part.at[dst_chip >> 4, aligned(dst_chip & 15, 8)], parts.at[slot], c_send, c_recv.at[slot], 2 * dst_chip + core)
@@ -299,20 +335,22 @@
     key = lax.broadcasted_iota(jnp.int32, (3 * BLK, 1), 0)
 
     def o_copy(wave, rows_of, cols_of):
-        return remote(o_ref.at[aligned(rows_of, 256), aligned(wave, 256)],
-                      full_ref.at[:, aligned(cols_of * 4 + wave, 256)], o_send.at[wave], o_recv.at[wave], partner)
+        return remote(o_ref.at[aligned(rows_of, TILE), aligned(wave, TILE)],
+                      full_ref.at[:, aligned(cols_of * 4 + wave, TILE)], o_send.at[wave], o_recv.at[wave], partner)
 
     def one_wave(wave, carry):
         with jax.named_scope("wait_wave"):
             for w in range(4):
                 @pl.when(wave == w)
                 def _():
+                    if w == 1:
+                        pass_on((6, 7))
                     for j in (2 * w, 2 * w + 1):
-                        advance(j, 3)
+                        arrived(j)
 
         def unpack(z, carry):
             for t in range(2):
-                rows = gath[2 * wave + t, z].reshape(256, 256)
+                rows = gath[2 * wave + t, z].reshape(TILE, TILE)
                 moved = jnp.dot(perm, rows, preferred_element_type=jnp.float32).astype(jnp.bfloat16)
                 for s in range(14):
                     hot[2 * wave + t, s, aligned(z, 16), :] = moved[s * 16:s * 16 + 16]
@@ -327,10 +365,10 @@
                 near = slice(b * BLK, b * BLK + 3 * BLK)
                 for t in range(2):
                     j = 2 * wave + t
-                    cols = aligned(j, 128)
+                    cols = aligned(j, LANES)
                     queries = split_heads(q_ref[rows, cols], BLK) * jnp.bfloat16(0.125)
-                    keys = jnp.concatenate([k_ref[near, cols]] + [hot[j, s, :, 0:128] for s in named], axis=0)
-                    vals = jnp.concatenate([v_ref[near, cols]] + [hot[j, s, :, 128:256] for s in named], axis=0)
+                    keys = jnp.concatenate([k_ref[near, cols]] + [hot[j, s, :, 0:LANES] for s in named], axis=0)
+                    vals = jnp.concatenate([v_ref[near, cols]] + [hot[j, s, :, LANES:TILE] for s in named], axis=0)
                     scores = lax.dot_general(keys, queries, NT, preferred_element_type=jnp.float32)
                     if b == 2:
                         bias = jnp.where((key < BLK) & (chip == 0), NEG, 0.0)
@@ -348,7 +386,7 @@
         return carry
 
     def own_o(wave):
-        return pltpu.make_async_copy(o_ref.at[aligned(core, 256), aligned(wave, 256)], full_ref.at[:, aligned(4 * core + wave, 256)], own_sem.at[wave])
+        return pltpu.make_async_copy(o_ref.at[aligned(core, TILE), aligned(wave, TILE)], full_ref.at[:, aligned(4 * core + wave, TILE)], own_sem.at[wave])
 
     lax.fori_loop(0, 4, one_wave, 0)
 
@@ -357,6 +395,9 @@
             for stage in range(3):
                 for c in copies(j, stage, False):
                     c.wait_send()
+            if j < PAIRS:
+                for c in passed(j, False):
+                    c.wait_send()
 
     def wait_part(i, carry):
         part_copy(chip ^ i, chip ^ i).wait()
@@ -366,19 +407,19 @@
         own_part.wait()
 
     with jax.named_scope("combine"):
-        top = lax.fori_loop(0, CHIPS, lambda i, t: jnp.maximum(t, parts[i, :, 256:384]), jnp.full((8, 128), NEG, jnp.float32), unroll=8)
+        top = lax.fori_loop(0, CHIPS, lambda i, t: jnp.maximum(t, parts[i, :, TILE:384]), jnp.full((8, LANES), NEG, jnp.float32), unroll=8)
 
         def add(i, carry):
             num, den = carry
-            weight = pltpu.roll(jnp.exp(parts[i, :, 256:384] - top), 124, 1)
+            weight = pltpu.roll(jnp.exp(parts[i, :, TILE:384] - top), 124, 1)
             wide = jnp.concatenate([jnp.broadcast_to(weight[:, t:t + 1], (8, HEAD_DIM)) for t in range(4)], axis=1)
-            return num + wide * parts[i, :, 0:256], den + weight * parts[i, :, 256:384]
-        num, den = lax.fori_loop(0, CHIPS, add, (jnp.zeros((8, 256), jnp.float32), jnp.zeros((8, 128), jnp.float32)), unroll=8)
+            return num + wide * parts[i, :, 0:TILE], den + weight * parts[i, :, TILE:384]
+        num, den = lax.fori_loop(0, CHIPS, add, (jnp.zeros((8, TILE), jnp.float32), jnp.zeros((8, LANES), jnp.float32)), unroll=8)
         wide = jnp.concatenate([jnp.broadcast_to(den[:, t:t + 1], (8, HEAD_DIM)) for t in range(4)], axis=1)
         piece[...] = (num / wide).astype(jnp.bfloat16)
 
     def glob_slice(src_chip, src_core):
-        return glob.at[aligned(src_chip % 16, 8), aligned(src_core * 4 + src_chip // 16, 256)]
+        return glob.at[aligned(src_chip % 16, 8), aligned(src_core * 4 + src_chip // 16, TILE)]
 
     def glob_copy(src_chip, src_core):
         return remote(piece, glob_slice(src_chip, src_core), e_send, e_recv.at[2 * src_chip + src_core], 0)
@@ -388,11 +429,11 @@
         glob_copy(chip, core).start()
 
     def y_copy(half, t):
-        at = (pl.ds(128 * half, 128), aligned(t, 256))
+        at = (pl.ds(LANES * half, LANES), aligned(t, TILE))
         return pltpu.make_async_copy(y_buf.at[at], y_ref.at[at], y_sem.at[half, t])
 
     def project_out(t, carry):
-        cols = aligned(t, 256)
+        cols = aligned(t, TILE)
         y_buf[:, cols] = lax.dot_general(full_ref[...], wo_buf[cols, :], NT, preferred_element_type=jnp.float32).astype(jnp.bfloat16)
         y_copy(1, t).start()
 
@@ -402,8 +443,8 @@
         return carry
 
     def project_glob(t, carry):
-        cols = aligned(t, 256)
-        y_buf[0:128, cols] = lax.dot_general(glob[...], wo_buf[cols, :], NT, preferred_element_type=jnp.float32).astype(jnp.bfloat16)
+        cols = aligned(t, TILE)
+        y_buf[0:LANES, cols] = lax.dot_general(glob[...], wo_buf[cols, :], NT, preferred_element_type=jnp.float32).astype(jnp.bfloat16)
         y_copy(0, t).start()
         return carry
 
@@ -430,7 +471,7 @@
             def wait_glob(i, carry):
                 glob_copy(i // 2, i % 2).wait_recv()
                 return carry
-            lax.fori_loop(1, 128, wait_glob, 0)
+            lax.fori_loop(1, LANES, wait_glob, 0)
             lax.fori_loop(0, PAIRS, project_glob, 0)
 
         def written(t, carry):
@@ -447,19 +488,19 @@
     bf16, f32 = jnp.bfloat16, jnp.float32
     return pl.pallas_call(
         kernel,
-        out_shape=jax.ShapeDtypeStruct((256, WIDTH), bf16),
+        out_shape=jax.ShapeDtypeStruct((TILE, WIDTH), bf16),
         in_specs=[vmem, pl.BlockSpec(memory_space=pltpu.SMEM), hbm, hbm, hbm, hbm], out_specs=hbm,
         scratch_shapes=[
-            VMEM((1, 128), jnp.int32), VMEM((256, WIDTH), bf16), VMEM((WIDTH, WIDTH), bf16),
-            VMEM((CHIPS, 4, 16, 128), bf16), VMEM((512, WIDTH), bf16), VMEM((4 * CHIPS, 16, 128), bf16),
-            VMEM((3, WIDTH, HALF), bf16), VMEM((2, CHIPS, 1, 128), jnp.int32), VMEM((256, 128), bf16), VMEM((256, 128), bf16),
+            VMEM((1, LANES), jnp.int32), VMEM((TILE, WIDTH), bf16), VMEM((WIDTH, WIDTH), bf16),
+            VMEM((CHIPS, 4, 16, LANES), bf16), VMEM((512, WIDTH), bf16), VMEM((4 * CHIPS, 16, LANES), bf16),
+            VMEM((3, WIDTH, HALF), bf16), VMEM((2, CHIPS, 1, LANES), jnp.int32), VMEM((TILE, LANES), bf16), VMEM((TILE, LANES), bf16),
             VMEM((512, HALF), bf16), VMEM((640, HALF), bf16), VMEM((640, HALF), bf16),
-            VMEM((PAIRS, 4, 4, 4, SLOTS, 256), bf16), VMEM((PAIRS, SLOTS, BLK, 256), bf16), VMEM((512, HALF), bf16),
-            VMEM((4, 128, 384), f32), VMEM((CHIPS, 8, 384), f32), VMEM((128, WIDTH), bf16), VMEM((8, 256), bf16),
-            pltpu.SMEM((2, 1, 128), jnp.int32), pltpu.SMEM((24,), jnp.int32),
-            VMEM((1, 4, 4, 4, SLOTS, 128), bf16), VMEM((SLOTS, BLK, 128), bf16), VMEM((256, WIDTH), bf16),
+            VMEM((PAIRS, 4, 4, 4, SLOTS, TILE), bf16), VMEM((PAIRS, SLOTS, BLK, TILE), bf16), VMEM((512, HALF), bf16),
+            VMEM((4, LANES, 384), f32), VMEM((CHIPS, 8, 384), f32), VMEM((LANES, WIDTH), bf16), VMEM((8, TILE), bf16),
+            pltpu.SMEM((2, 1, LANES), jnp.int32), pltpu.SMEM((24,), jnp.int32),
+            VMEM((1, 4, 4, 4, SLOTS, LANES), bf16), VMEM((SLOTS, BLK, LANES), bf16), VMEM((TILE, WIDTH), bf16),
             dma, dma((CHIPS,)), dma((3,)), dma((CHIPS,)), dma((2,)), dma((2, 2)), dma((2, 2)), dma((3,)), dma((3, 4)), dma((2,)),
-            dma((PAIRS + 1, 3, 3)), dma((PAIRS + 1, 3, 3)), dma, dma((CHIPS,)), dma((4,)), dma((4,)), dma, dma((128,)), dma, dma((4,)), dma((2, PAIRS))],
+            dma((PAIRS + 1, 4, 3)), dma((PAIRS + 1, 4, 3)), dma, dma((CHIPS,)), dma((4,)), dma((4,)), dma, dma((LANES,)), dma, dma((4,)), dma((2, PAIRS))],
         compiler_params=pltpu.CompilerParams(has_side_effects=True, collective_id=0, vmem_limit_bytes=62 * 1024 * 1024), name="attend",
     )(x, rand_idx, wq, wk, wv, wo)
 

time: 91 us -> 94.2 us (1.035)
  Pallas kernels: 88.6 us -> 91.8 us
    pallas_call x1, Pallas kernels: 88.6 us -> 91.8 us  [attend(): pl.pallas_call(kernel, out_shape=jax.ShapeDtypeStruct((TILE, WIDTH), bf16...]
where the time goes in v11:
time: 94.2 us; the launch traced here: 94.1 us
  Pallas kernels  91.8 us (97%)
  local copies, waits for them, and re-layouts  2.3 us (2%)
    pallas_call x1, Pallas kernels, attend(): pl.pallas_call(kernel, out_shape=jax.ShapeDtypeStruct((TILE, WIDTH), bf16...  91.8 us
    unnamed x1, local copies, waits for them, and re-layouts  2.3 us

profile of v11, /device:TPU:0, one launch (start us, length us, event | category | flops | bytes accessed | tf_op | source)
XLA Modules:
  0.0 94.1 jit_solution(15896165196499768102)
XLA Ops:
  0.0 91.8 %attend.1 = bf16[256,2048]{1,0:T(8,128)(2,1)} custom-call(bf16[256,2048]{1,0:T(8,128)(2,1)} %x_ref.1, s32[4,3]{1,0:T(4,128)} %rand_ref.1, bf16[2048,2048]{1,0:T(8,128)(2,1)} %wq_ref.1, bf16[2048,2048]{1,0:T(8,128)(2,1)} %wk_ref.1, bf16[2048,2048]{1,0:T(8,128)(2,1)} %wv_ref.1, bf16[2048,2048]{1,0:T(8,128)(2,1)} %wo_ref.1), custom_call_target="tpu_custom_call" | custom-call | tf_op jit(solution)/shard_map/attend/pallas_call | solution.py:489
  91.8 2.3 %copy.8 = bf16[256,2048]{1,0:T(8,128)(2,1)} copy(bf16[256,2048]{1,0:T(8,128)(2,1)} %attend.1) | data formatting | bytes 2097152

commit v12 on v11

--- a/solution.py
+++ b/solution.py
@@ -20,7 +20,6 @@
 ORDERS = ((0, 1, 2), (1, 2, 0), (2, 0, 1))
 TILE = 256
 LANES = 128
-NEAR = (1, 3)
 NT = (((1,), (1,)), ((), ()))
 TN = (((0,), (0,)), ((), ()))
 
@@ -51,10 +50,10 @@
                                         device_id={"seq": dev}, device_id_type=MESH)
 
 
-def kernel(x_ref, rand_ref, wq_ref, wk_ref, wv_ref, wo_ref, y_ref,
-           idx_ref, full_ref, wo_buf, xs, xc, recv, w_buf, idx_all, sel, other, q_ref, k_ref, v_ref, gath, hot, o_ref, part, parts, glob, piece, near_s, slot_s, gath_q, queries_t, y_buf,
+def kernel(x_ref, rand_ref, wq_ref, wk_ref, wv_ref, full_ref,
+           idx_ref, xs, xc, recv, w_buf, idx_all, sel, other, q_ref, k_ref, v_ref, gath, hot, o_ref, part, parts, glob, piece, near_s, slot_s, gath_q, queries_t,
            s_send, s_recv, i_send, i_recv, x_sem, h_send, h_recv, loc, w_sem, p_sem, g_send, g_recv,
-           c_send, c_recv, o_send, o_recv, e_send, e_recv, wo_sem, own_sem, y_sem):
+           c_send, c_recv, o_send, o_recv, e_send, e_recv, own_sem):
     dev = lax.axis_index("seq")
     chip, core = dev // 2, dev % 2
     partner = dev + 1 - 2 * core
@@ -92,7 +91,6 @@
         return remote(ref.at[pl.ds((8 - 7 * side) * BLK, BLK)], ref.at[pl.ds(9 * side * BLK, BLK)],
                       h_send.at[kv, side], h_recv.at[kv, side], 2 * to + core)
 
-    wo_copy = pltpu.make_async_copy(wo_ref, wo_buf, wo_sem)
 
     with jax.named_scope("issue"):
         for t in range(4):
@@ -136,7 +134,6 @@
 
     with jax.named_scope("wait_x"):
         own_x.wait()
-        wo_copy.start()
         x_swap(core).wait_send()
         x_swap(1 - core).wait_recv()
 
@@ -219,7 +216,7 @@
         order = ORDERS[j % 3]
         axis = order[stage]
         out = []
-        for k in NEAR if stage == 2 and j < PAIRS else (1, 2, 3):
+        for k in (1, 2, 3):
             to = lax.rem(coord[axis] + k, 4)
             at = list(coord)
             if receive:
@@ -230,28 +227,6 @@
                               dev + 2 * scale[axis] * (to - coord[axis])))
         return out
 
-    def passed(j, receive):
-        order = ORDERS[j % 3]
-        axis = order[2]
-        out = []
-        for half, k in enumerate(NEAR):
-            at = list(coord)
-            at[axis] = lax.rem(coord[axis] + (2 if receive else 4 - k), 4)
-            ref = gath.at[(j,) + tuple(slice(None) if a in order[:2] else at[a] for a in (2, 1, 0)) + (slice(8 * half, 8 * half + 8),)]
-            to = lax.rem(coord[axis] + k, 4)
-            out.append(remote(ref, ref, g_send.at[j, 3, half], g_recv.at[j, 3, half], dev + 2 * scale[axis] * (to - coord[axis])))
-        return out
-
-    def pass_on(chunks):
-        for j in chunks:
-            for got, nxt in zip(copies(j, 2, True), passed(j, False)):
-                got.wait_recv()
-                nxt.start()
-
-    def arrived(j):
-        for c in passed(j, True):
-            c.wait_recv()
-
     def advance(j, stage):
         if stage:
             for c in copies(j, stage - 1, True):
@@ -267,7 +242,7 @@
         for j in ALL:
             advance(j, 1)
     with jax.named_scope("gather2"):
-        for j in ALL[:7]:
+        for j in ALL:
             advance(j, 2)
 
     with jax.named_scope("wait_queries"):
@@ -279,10 +254,11 @@
             queries_t[s, aligned(z, 16), :] = moved[16 * s:16 * s + 16]
         return carry
 
-    def glob_part(wave, carry):
+    def glob_part(step, carry):
         sums, tops = [], []
-        for t in range(2):
-            j = 2 * wave + t
+        for t in range(4):
+            j = 4 * step + t
+            wave = 2 * step + t // 2
             cols = aligned(j, LANES)
             gq = jnp.concatenate([queries_t[j], queries_t[PAIRS + j]], axis=0)
             queries = split_heads(gq, LANES) * jnp.bfloat16(0.125)
@@ -291,39 +267,29 @@
             probs = jnp.exp(scores - top)
             total = jnp.sum(probs, axis=0, keepdims=True)
             out = lax.dot_general(probs.astype(jnp.bfloat16), v_ref[BLK:9 * BLK, cols], TN, preferred_element_type=jnp.float32)
-            part[wave, :, LANES * t:LANES * t + LANES] = join_heads(out, LANES)
-            for h in range(2):
-                sums.append(total[:, LANES * h:LANES * h + LANES])
-                tops.append(top[:, LANES * h:LANES * h + LANES])
-        stats = jnp.concatenate(sums + tops + [jnp.zeros((120, LANES), jnp.float32)], axis=0)
-        part[wave, :, TILE:384] = stats.T
+            part[wave, :, LANES * (t % 2):LANES * (t % 2) + LANES] = join_heads(out, LANES)
+            sums += [total[:, 0:LANES], total[:, LANES:TILE]]
+            tops += [top[:, 0:LANES], top[:, LANES:TILE]]
+        pad = [jnp.zeros((120, LANES), jnp.float32)]
+        for u in range(2):
+            stats = jnp.concatenate(sums[4 * u:4 * u + 4] + tops[4 * u:4 * u + 4] + pad, axis=0)
+            part[2 * step + u, :, TILE:384] = stats.T
 
         def start_part(i, carry):
-            to = 16 * wave + (i ^ (chip & 15))
+            to = 32 * step + (i ^ (chip & 31))
 
             @pl.when(to != chip)
             def _():
                 part_copy(to, chip).start()
             return carry
-        lax.fori_loop(0, 16, start_part, carry)
-
-        @pl.when(wave == 1)
-        def _():
-            pass_on((0, 1, 2))
-            for j in ALL[7:]:
-                advance(j, 2)
-
-        @pl.when(wave == 3)
-        def _():
-            pass_on((3, 4, 5))
-        return carry
+        return lax.fori_loop(0, 32, start_part, carry)
 
     def part_copy(dst_chip, slot):
         return remote(part.at[dst_chip >> 4, aligned(dst_chip & 15, 8)], parts.at[slot], c_send, c_recv.at[slot], 2 * dst_chip + core)
 
     with jax.named_scope("globpart"):
         lax.fori_loop(0, 4, unpack_queries, 0)
-        lax.fori_loop(0, 4, glob_part, 0)
+        lax.fori_loop(0, 2, glob_part, 0)
         own_part = pltpu.make_async_copy(part.at[chip >> 4, aligned(chip & 15, 8)], parts.at[chip], loc.at[1])
         own_part.start()
 
@@ -343,20 +309,19 @@
             for w in range(4):
                 @pl.when(wave == w)
                 def _():
-                    if w == 1:
-                        pass_on((6, 7))
                     for j in (2 * w, 2 * w + 1):
-                        arrived(j)
+                        advance(j, 3)
 
         def unpack(z, carry):
             for t in range(2):
                 rows = gath[2 * wave + t, z].reshape(TILE, TILE)
                 moved = jnp.dot(perm, rows, preferred_element_type=jnp.float32).astype(jnp.bfloat16)
                 for s in range(14):
-                    hot[2 * wave + t, s, aligned(z, 16), :] = moved[s * 16:s * 16 + 16]
+                    hot[2 * wave + t, s, 16 * z:16 * z + 16, :] = moved[s * 16:s * 16 + 16]
             return carry
         with jax.named_scope("unpack"):
-            lax.fori_loop(0, 4, unpack, 0)
+            for z in range(4):
+                unpack(z, 0)
 
         with jax.named_scope("blocks"):
             for b in range(8):
@@ -395,9 +360,6 @@
             for stage in range(3):
                 for c in copies(j, stage, False):
                     c.wait_send()
-            if j < PAIRS:
-                for c in passed(j, False):
-                    c.wait_send()
 
     def wait_part(i, carry):
         part_copy(chip ^ i, chip ^ i).wait()
@@ -428,35 +390,11 @@
     def _():
         glob_copy(chip, core).start()
 
-    def y_copy(half, t):
-        at = (pl.ds(LANES * half, LANES), aligned(t, TILE))
-        return pltpu.make_async_copy(y_buf.at[at], y_ref.at[at], y_sem.at[half, t])
-
-    def project_out(t, carry):
-        cols = aligned(t, TILE)
-        y_buf[:, cols] = lax.dot_general(full_ref[...], wo_buf[cols, :], NT, preferred_element_type=jnp.float32).astype(jnp.bfloat16)
-        y_copy(1, t).start()
-
-        @pl.when(dev != 0)
-        def _():
-            y_copy(0, t).start()
-        return carry
-
-    def project_glob(t, carry):
-        cols = aligned(t, TILE)
-        y_buf[0:LANES, cols] = lax.dot_general(glob[...], wo_buf[cols, :], NT, preferred_element_type=jnp.float32).astype(jnp.bfloat16)
-        y_copy(0, t).start()
-        return carry
-
     with jax.named_scope("wait_o"):
-        wo_copy.wait()
         for wave in range(4):
             own_o(wave).wait()
             o_copy(wave, 1 - core, core).wait_send()
             o_copy(wave, core, 1 - core).wait_recv()
-    with jax.named_scope("out"):
-        lax.fori_loop(0, PAIRS, project_out, 0)
-
     with jax.named_scope("tail"):
         @pl.when(dev != 0)
         def _():
@@ -472,16 +410,26 @@
                 glob_copy(i // 2, i % 2).wait_recv()
                 return carry
             lax.fori_loop(1, LANES, wait_glob, 0)
-            lax.fori_loop(0, PAIRS, project_glob, 0)
-
-        def written(t, carry):
-            y_copy(0, t).wait()
-            y_copy(1, t).wait()
-            return carry
-        lax.fori_loop(0, PAIRS, written, 0)
-
-
-def attend(x, rand_idx, wq, wk, wv, wo):
+            full_ref[0:LANES, :] = glob[...]
+
+
+def out_kernel(rows_ref, w_ref, y_ref):
+    y_ref[...] = lax.dot_general(rows_ref[...], w_ref[...], NT, preferred_element_type=jnp.float32).astype(jnp.bfloat16)
+
+
+def project_out(rows, wo):
+    tile = TILE
+    return pl.pallas_call(
+        out_kernel, grid=(WIDTH // tile,),
+        in_specs=[pl.BlockSpec(rows.shape, lambda j: (0, 0)), pl.BlockSpec((tile, WIDTH), lambda j: (j, 0))],
+        out_specs=pl.BlockSpec((rows.shape[0], tile), lambda j: (0, j)),
+        out_shape=jax.ShapeDtypeStruct(rows.shape, jnp.bfloat16), name="project_out",
+        compiler_params=pltpu.CompilerParams(vmem_limit_bytes=16 << 20),
+        cost_estimate=pl.CostEstimate(flops=2 * rows.shape[0] * WIDTH * WIDTH, bytes_accessed=10 << 20, transcendentals=0),
+    )(rows, wo)
+
+
+def attend(x, rand_idx, wq, wk, wv):
     vmem = pl.BlockSpec(memory_space=VMEM)
     hbm = pl.BlockSpec(memory_space=pl.ANY)
     dma = pltpu.SemaphoreType.DMA
@@ -489,20 +437,20 @@
     return pl.pallas_call(
         kernel,
         out_shape=jax.ShapeDtypeStruct((TILE, WIDTH), bf16),
-        in_specs=[vmem, pl.BlockSpec(memory_space=pltpu.SMEM), hbm, hbm, hbm, hbm], out_specs=hbm,
+        in_specs=[vmem, pl.BlockSpec(memory_space=pltpu.SMEM), hbm, hbm, hbm], out_specs=vmem,
         scratch_shapes=[
-            VMEM((1, LANES), jnp.int32), VMEM((TILE, WIDTH), bf16), VMEM((WIDTH, WIDTH), bf16),
+            VMEM((1, LANES), jnp.int32),
             VMEM((CHIPS, 4, 16, LANES), bf16), VMEM((512, WIDTH), bf16), VMEM((4 * CHIPS, 16, LANES), bf16),
             VMEM((3, WIDTH, HALF), bf16), VMEM((2, CHIPS, 1, LANES), jnp.int32), VMEM((TILE, LANES), bf16), VMEM((TILE, LANES), bf16),
             VMEM((512, HALF), bf16), VMEM((640, HALF), bf16), VMEM((640, HALF), bf16),
             VMEM((PAIRS, 4, 4, 4, SLOTS, TILE), bf16), VMEM((PAIRS, SLOTS, BLK, TILE), bf16), VMEM((512, HALF), bf16),
             VMEM((4, LANES, 384), f32), VMEM((CHIPS, 8, 384), f32), VMEM((LANES, WIDTH), bf16), VMEM((8, TILE), bf16),
             pltpu.SMEM((2, 1, LANES), jnp.int32), pltpu.SMEM((24,), jnp.int32),
-            VMEM((1, 4, 4, 4, SLOTS, LANES), bf16), VMEM((SLOTS, BLK, LANES), bf16), VMEM((TILE, WIDTH), bf16),
+            VMEM((1, 4, 4, 4, SLOTS, LANES), bf16), VMEM((SLOTS, BLK, LANES), bf16),
             dma, dma((CHIPS,)), dma((3,)), dma((CHIPS,)), dma((2,)), dma((2, 2)), dma((2, 2)), dma((3,)), dma((3, 4)), dma((2,)),
-            dma((PAIRS + 1, 4, 3)), dma((PAIRS + 1, 4, 3)), dma, dma((CHIPS,)), dma((4,)), dma((4,)), dma, dma((LANES,)), dma, dma((4,)), dma((2, PAIRS))],
-        compiler_params=pltpu.CompilerParams(has_side_effects=True, collective_id=0, vmem_limit_bytes=62 * 1024 * 1024), name="attend",
-    )(x, rand_idx, wq, wk, wv, wo)
+            dma((PAIRS + 1, 3, 3)), dma((PAIRS + 1, 3, 3)), dma, dma((CHIPS,)), dma((4,)), dma((4,)), dma, dma((LANES,)), dma((4,))],
+        compiler_params=pltpu.CompilerParams(has_side_effects=True, collective_id=0, vmem_limit_bytes=44 << 20), name="attend",
+    )(x, rand_idx, wq, wk, wv)
 
 
 def solution(mesh):
@@ -510,6 +458,6 @@
     rep_spec = P(None, None)
 
     def local_fn(tokens, w_query, w_key, w_value, w_out, rand_idx):
-        return attend(tokens, rand_idx, w_query, w_key, w_value, w_out)
+        return project_out(attend(tokens, rand_idx, w_query, w_key, w_value), w_out)
 
     return jax.shard_map(local_fn, mesh=mesh, in_specs=(row_spec, rep_spec, rep_spec, rep_spec, rep_spec, row_spec), out_specs=row_spec, check_vma=False)

time: 94.2 us -> 90.2 us (0.958)
  Pallas kernels: 91.8 us -> 87.8 us
    pallas_call x1, Pallas kernels: 91.8 us -> 82.8 us  [attend(): pl.pallas_call(kernel, out_shape=jax.ShapeDtypeStruct((TILE, WIDTH), bf16...]
    pallas_call x0 -> x1, Pallas kernels: none -> 5.03 us  [project_out(): pl.pallas_call(out_kernel, grid=(WIDTH // tile,), in_specs=[pl.BlockSpec(...]
    unnamed x1 -> x6, local copies, waits for them, and re-layouts: 2.3 us -> 2.28 us
where the time goes in v12:
time: 90.2 us; the launch traced here: 90.1 us
  Pallas kernels  87.8 us (97%)
  local copies, waits for them, and re-layouts  2.28 us (3%)
    pallas_call x1, Pallas kernels, attend(): pl.pallas_call(kernel, out_shape=jax.ShapeDtypeStruct((TILE, WIDTH), bf16...  82.8 us
    pallas_call x1, Pallas kernels, project_out(): pl.pallas_call(out_kernel, grid=(WIDTH // tile,), in_specs=[pl.BlockSpec(...  5.03 us
    unnamed x6, local copies, waits for them, and re-layouts  2.28 us

profile of v12, /device:TPU:0, one launch (start us, length us, event | category | flops | bytes accessed | tf_op | source)
XLA Modules:
  0.0 90.1 jit_solution(7714889431546372499)
XLA Ops:
  0.0 0.0 copy-start
  0.0 0.0 copy-start.1
  0.0 1.4 %copy-done.1 = bf16[256,2048]{1,0:T(8,128)(2,1)S(1)} copy-done((bf16[256,2048]{1,0:T(8,128)(2,1)S(1)}, bf16[256,2048]{1,0:T(8,128)(2,1)}, u32[]{:S(2)}) %copy-start.1) | copy-done | bytes 1048600
  1.4 0.0 copy-start.2
  1.4 0.9 %copy-done.2 = s32[4,3]{1,0:T(4,128)S(1)} copy-done((s32[4,3]{1,0:T(4,128)S(1)}, s32[4,3]{1,0:T(4,128)}, u32[]{:S(2)}) %copy-start.2) | copy-done | bytes 72
  2.3 82.8 %attend.1.rows_ref = bf16[256,2048]{1,0:T(8,128)(2,1)S(1)} custom-call(bf16[256,2048]{1,0:T(8,128)(2,1)S(1)} %copy-done.1, s32[4,3]{1,0:T(4,128)S(1)} %copy-done.2, bf16[2048,2048]{1,0:T(8,128)(2,1)} %wq_ref.1, bf16[2048,2048]{1,0:T(8,128)(2,1)} %wk_ref.1, bf16[2048,2048]{1,0:T(8,128)(2,1)} %wv_ref.1), custom_call_target="tpu_custom_call" | custom-call | tf_op jit(solution)/shard_map/attend/pallas_call | solution.py:437
  85.1 0.0 copy-done
  85.1 5.0 %project_out.1 = bf16[256,2048]{1,0:T(8,128)(2,1)} custom-call(bf16[256,2048]{1,0:T(8,128)(2,1)S(1)} %attend.1.rows_ref, bf16[2048,2048]{1,0:T(8,128)(2,1)S(1)} %copy-done), custom_call_target="tpu_custom_call" | custom-call | flops 2147483648 | bytes 10485760 | tf_op jit(solution)/shard_map/project_out/pallas_call | solution.py:422
Async XLA Ops:
  0.0 85.1 %copy-start = (bf16[2048,2048]{1,0:T(8,128)(2,1)S(1)}, bf16[2048,2048]{1,0:T(8,128)(2,1)}, u32[]{:S(2)}) copy-start(bf16[2048,2048]{1,0:T(8,128)(2,1)} %w_ref.1) | copy-start | bytes 25165828
  0.0 1.4 %copy-start.1 = (bf16[256,2048]{1,0:T(8,128)(2,1)S(1)}, bf16[256,2048]{1,0:T(8,128)(2,1)}, u32[]{:S(2)}) copy-start(bf16[256,2048]{1,0:T(8,128)(2,1)} %x_ref.1) | copy-start | bytes 3145732
  1.4 0.9 %copy-start.2 = (s32[4,3]{1,0:T(4,128)S(1)}, s32[4,3]{1,0:T(4,128)}, u32[]{:S(2)}) copy-start(s32[4,3]{1,0:T(4,128)} %rand_ref.1) | copy-start | bytes 148

commit v13 on v12

--- a/solution.py
+++ b/solution.py
@@ -12,7 +12,7 @@
 HALF = 1024
 CHIPS = 64
 PAIRS = 8
-ALL = (PAIRS,) + tuple(range(PAIRS))
+ALL = tuple(range(PAIRS)) + (PAIRS,)
 NEG = -1e30
 FAR = 1 << 20
 MESH = pl.DeviceIdType.MESH
@@ -203,9 +203,6 @@
     with jax.named_scope("publish"):
         moved = jnp.dot(perm, sel[...] + other[...], preferred_element_type=jnp.float32).astype(jnp.bfloat16)
         rows = jnp.concatenate([moved[16 * j:16 * j + 16] for j in range(16)], axis=1)
-        gq = jnp.dot(rows, w_buf[0], preferred_element_type=jnp.float32)
-        gq = jnp.concatenate([gq[t:t + 1, LANES * j:LANES * j + LANES] for t in range(2) for j in range(PAIRS)], axis=0)
-        gath_q[0, coord[2], coord[1], coord[0]] = gq.astype(jnp.bfloat16)
         out = [jnp.dot(rows, w_buf[i], preferred_element_type=jnp.float32) for i in (1, 2)]
         for j in range(PAIRS):
             cols = slice(LANES * j, LANES * j + LANES)
@@ -236,8 +233,13 @@
                 c.start()
 
     with jax.named_scope("gather0"):
-        for j in ALL:
+        for j in range(PAIRS):
             advance(j, 0)
+    with jax.named_scope("publish_queries"):
+        gq = jnp.dot(rows, w_buf[0], preferred_element_type=jnp.float32)
+        gq = jnp.concatenate([gq[t:t + 1, LANES * j:LANES * j + LANES] for t in range(2) for j in range(PAIRS)], axis=0)
+        gath_q[0, coord[2], coord[1], coord[0]] = gq.astype(jnp.bfloat16)
+        advance(PAIRS, 0)
     with jax.named_scope("gather1"):
         for j in ALL:
             advance(j, 1)
@@ -449,7 +451,7 @@
             VMEM((1, 4, 4, 4, SLOTS, LANES), bf16), VMEM((SLOTS, BLK, LANES), bf16),
             dma, dma((CHIPS,)), dma((3,)), dma((CHIPS,)), dma((2,)), dma((2, 2)), dma((2, 2)), dma((3,)), dma((3, 4)), dma((2,)),
             dma((PAIRS + 1, 3, 3)), dma((PAIRS + 1, 3, 3)), dma, dma((CHIPS,)), dma((4,)), dma((4,)), dma, dma((LANES,)), dma((4,))],
-        compiler_params=pltpu.CompilerParams(has_side_effects=True, collective_id=0, vmem_limit_bytes=44 << 20), name="attend",
+        compiler_params=pltpu.CompilerParams(has_side_effects=True, collective_id=0, vmem_limit_bytes=62 << 20), name="attend",
     )(x, rand_idx, wq, wk, wv)
 
 

time: 90.2 us -> 94.3 us (1.045)
  local copies, waits for them, and re-layouts: 2.28 us -> 4.6 us
  Pallas kernels: 87.8 us -> 89.5 us
    unnamed x6 -> x4, local copies, waits for them, and re-layouts: 2.28 us -> 4.6 us
    pallas_call x1, Pallas kernels: 82.8 us -> 84.5 us  [attend(): pl.pallas_call(kernel, out_shape=jax.ShapeDtypeStruct((TILE, WIDTH), bf16...]
where the time goes in v13:
time: 94.3 us; the launch traced here: 94.1 us
  Pallas kernels  89.5 us (95%)
  local copies, waits for them, and re-layouts  4.6 us (5%)
    pallas_call x1, Pallas kernels, attend(): pl.pallas_call(kernel, out_shape=jax.ShapeDtypeStruct((TILE, WIDTH), bf16...  84.5 us
    pallas_call x1, Pallas kernels, project_out(): pl.pallas_call(out_kernel, grid=(WIDTH // tile,), in_specs=[pl.BlockSpec(...  5 us
    unnamed x4, local copies, waits for them, and re-layouts  4.6 us

profile of v13, /device:TPU:0, one launch (start us, length us, event | category | flops | bytes accessed | tf_op | source)
XLA Modules:
  0.0 94.1 jit_solution(13572366734564948643)
XLA Ops:
  0.0 84.5 %attend.1.rows_ref = bf16[256,2048]{1,0:T(8,128)(2,1)} custom-call(bf16[256,2048]{1,0:T(8,128)(2,1)} %x_ref.1, s32[4,3]{1,0:T(4,128)} %rand_ref.1, bf16[2048,2048]{1,0:T(8,128)(2,1)} %wq_ref.1, bf16[2048,2048]{1,0:T(8,128)(2,1)} %wk_ref.1, bf16[2048,2048]{1,0:T(8,128)(2,1)} %wv_ref.1), custom_call_target="tpu_custom_call" | custom-call | tf_op jit(solution)/shard_map/attend/pallas_call | solution.py:439
  84.5 0.0 copy-start
  84.5 3.4 %copy-done = bf16[2048,2048]{1,0:T(8,128)(2,1)S(1)} copy-done((bf16[2048,2048]{1,0:T(8,128)(2,1)S(1)}, bf16[2048,2048]{1,0:T(8,128)(2,1)}, u32[]{:S(2)}) %copy-start) | copy-done | bytes 8388632
  87.9 0.0 copy-start.1
  87.9 1.2 %copy-done.1 = bf16[256,2048]{1,0:T(8,128)(2,1)S(1)} copy-done((bf16[256,2048]{1,0:T(8,128)(2,1)S(1)}, bf16[256,2048]{1,0:T(8,128)(2,1)}, u32[]{:S(2)}) %copy-start.1) | copy-done | bytes 1048600
  89.1 5.0 %project_out.1 = bf16[256,2048]{1,0:T(8,128)(2,1)} custom-call(bf16[256,2048]{1,0:T(8,128)(2,1)S(1)} %copy-done.1, bf16[2048,2048]{1,0:T(8,128)(2,1)S(1)} %copy-done), custom_call_target="tpu_custom_call" | custom-call | flops 2147483648 | bytes 10485760 | tf_op jit(solution)/shard_map/project_out/pallas_call | solution.py:424
Async XLA Ops:
  84.5 3.4 %copy-start = (bf16[2048,2048]{1,0:T(8,128)(2,1)S(1)}, bf16[2048,2048]{1,0:T(8,128)(2,1)}, u32[]{:S(2)}) copy-start(bf16[2048,2048]{1,0:T(8,128)(2,1)} %w_ref.1) | copy-start | bytes 25165828
  87.9 1.2 %copy-start.1 = (bf16[256,2048]{1,0:T(8,128)(2,1)S(1)}, bf16[256,2048]{1,0:T(8,128)(2,1)}, u32[]{:S(2)}) copy-start(bf16[256,2048]{1,0:T(8,128)(2,1)} %attend.1.rows_ref) | copy-start | bytes 3145732

commit v14 on v13

--- a/solution.py
+++ b/solution.py
@@ -12,7 +12,7 @@
 HALF = 1024
 CHIPS = 64
 PAIRS = 8
-ALL = tuple(range(PAIRS)) + (PAIRS,)
+ALL = (PAIRS,) + tuple(range(PAIRS))
 NEG = -1e30
 FAR = 1 << 20
 MESH = pl.DeviceIdType.MESH
@@ -426,7 +426,7 @@
         in_specs=[pl.BlockSpec(rows.shape, lambda j: (0, 0)), pl.BlockSpec((tile, WIDTH), lambda j: (j, 0))],
         out_specs=pl.BlockSpec((rows.shape[0], tile), lambda j: (0, j)),
         out_shape=jax.ShapeDtypeStruct(rows.shape, jnp.bfloat16), name="project_out",
-        compiler_params=pltpu.CompilerParams(vmem_limit_bytes=16 << 20),
+        compiler_params=pltpu.CompilerParams(vmem_limit_bytes=62 << 20),
         cost_estimate=pl.CostEstimate(flops=2 * rows.shape[0] * WIDTH * WIDTH, bytes_accessed=10 << 20, transcendentals=0),
     )(rows, wo)
 

time: 94.3 us -> 93.4 us (level)
  local copies, waits for them, and re-layouts: 4.6 us -> 0 us
  Pallas kernels: 89.5 us -> 93.1 us
    unnamed x4 -> x0, local copies, waits for them, and re-layouts: 4.6 us -> none
    pallas_call x1, Pallas kernels: 5 us -> 8.77 us  [project_out(): pl.pallas_call(out_kernel, grid=(WIDTH // tile,), in_specs=[pl.BlockSpec(...]
where the time goes in v14:
time: 93.4 us; the launch traced here: 93.1 us
  Pallas kernels  93.1 us (100%)
    pallas_call x1, Pallas kernels, attend(): pl.pallas_call(kernel, out_shape=jax.ShapeDtypeStruct((TILE, WIDTH), bf16...  84.4 us
    pallas_call x1, Pallas kernels, project_out(): pl.pallas_call(out_kernel, grid=(WIDTH // tile,), in_specs=[pl.BlockSpec(...  8.77 us

profile of v14, /device:TPU:0, one launch (start us, length us, event | category | flops | bytes accessed | tf_op | source)
XLA Modules:
  0.0 93.1 jit_solution(6048875282289746908)
XLA Ops:
  0.0 84.4 %attend.1.rows_ref = bf16[256,2048]{1,0:T(8,128)(2,1)} custom-call(bf16[256,2048]{1,0:T(8,128)(2,1)} %x_ref.1, s32[4,3]{1,0:T(4,128)} %rand_ref.1, bf16[2048,2048]{1,0:T(8,128)(2,1)} %wq_ref.1, bf16[2048,2048]{1,0:T(8,128)(2,1)} %wk_ref.1, bf16[2048,2048]{1,0:T(8,128)(2,1)} %wv_ref.1), custom_call_target="tpu_custom_call" | custom-call | tf_op jit(solution)/shard_map/attend/pallas_call | solution.py:439
  84.4 8.8 %project_out.1 = bf16[256,2048]{1,0:T(8,128)(2,1)} custom-call(bf16[256,2048]{1,0:T(8,128)(2,1)} %attend.1.rows_ref, bf16[2048,2048]{1,0:T(8,128)(2,1)} %w_ref.1), custom_call_target="tpu_custom_call" | custom-call | flops 2147483648 | bytes 10485760 | tf_op jit(solution)/shard_map/project_out/pallas_call | solution.py:424

commit v15 on v14

--- a/solution.py
+++ b/solution.py
@@ -426,7 +426,7 @@
         in_specs=[pl.BlockSpec(rows.shape, lambda j: (0, 0)), pl.BlockSpec((tile, WIDTH), lambda j: (j, 0))],
         out_specs=pl.BlockSpec((rows.shape[0], tile), lambda j: (0, j)),
         out_shape=jax.ShapeDtypeStruct(rows.shape, jnp.bfloat16), name="project_out",
-        compiler_params=pltpu.CompilerParams(vmem_limit_bytes=62 << 20),
+        compiler_params=pltpu.CompilerParams(vmem_limit_bytes=16 << 20),
         cost_estimate=pl.CostEstimate(flops=2 * rows.shape[0] * WIDTH * WIDTH, bytes_accessed=10 << 20, transcendentals=0),
     )(rows, wo)
 
@@ -451,7 +451,7 @@
             VMEM((1, 4, 4, 4, SLOTS, LANES), bf16), VMEM((SLOTS, BLK, LANES), bf16),
             dma, dma((CHIPS,)), dma((3,)), dma((CHIPS,)), dma((2,)), dma((2, 2)), dma((2, 2)), dma((3,)), dma((3, 4)), dma((2,)),
             dma((PAIRS + 1, 3, 3)), dma((PAIRS + 1, 3, 3)), dma, dma((CHIPS,)), dma((4,)), dma((4,)), dma, dma((LANES,)), dma((4,))],
-        compiler_params=pltpu.CompilerParams(has_side_effects=True, collective_id=0, vmem_limit_bytes=62 << 20), name="attend",
+        compiler_params=pltpu.CompilerParams(has_side_effects=True, collective_id=0, vmem_limit_bytes=44 << 20), name="attend",
     )(x, rand_idx, wq, wk, wv)
 
 

time: 93.4 us -> 90.2 us (0.966)
  Pallas kernels: 93.1 us -> 87.8 us
  local copies, waits for them, and re-layouts: 0 us -> 2.28 us
    pallas_call x1, Pallas kernels: 8.77 us -> 5.03 us  [project_out(): pl.pallas_call(out_kernel, grid=(WIDTH // tile,), in_specs=[pl.BlockSpec(...]
    unnamed x0 -> x6, local copies, waits for them, and re-layouts: none -> 2.28 us
    pallas_call x1, Pallas kernels: 84.4 us -> 82.7 us  [attend(): pl.pallas_call(kernel, out_shape=jax.ShapeDtypeStruct((TILE, WIDTH), bf16...]
where the time goes in v15:
time: 90.2 us; the launch traced here: 90.1 us
  Pallas kernels  87.8 us (97%)
  local copies, waits for them, and re-layouts  2.28 us (3%)
    pallas_call x1, Pallas kernels, attend(): pl.pallas_call(kernel, out_shape=jax.ShapeDtypeStruct((TILE, WIDTH), bf16...  82.7 us
    pallas_call x1, Pallas kernels, project_out(): pl.pallas_call(out_kernel, grid=(WIDTH // tile,), in_specs=[pl.BlockSpec(...  5.03 us
    unnamed x6, local copies, waits for them, and re-layouts  2.28 us

profile of v15, /device:TPU:0, one launch (start us, length us, event | category | flops | bytes accessed | tf_op | source)
XLA Modules:
  0.0 90.1 jit_solution(3361052350958174195)
XLA Ops:
  0.0 0.0 copy-start
  0.0 0.0 copy-start.1
  0.0 1.4 %copy-done.1 = bf16[256,2048]{1,0:T(8,128)(2,1)S(1)} copy-done((bf16[256,2048]{1,0:T(8,128)(2,1)S(1)}, bf16[256,2048]{1,0:T(8,128)(2,1)}, u32[]{:S(2)}) %copy-start.1) | copy-done | bytes 1048600
  1.4 0.0 copy-start.2
  1.4 0.9 %copy-done.2 = s32[4,3]{1,0:T(4,128)S(1)} copy-done((s32[4,3]{1,0:T(4,128)S(1)}, s32[4,3]{1,0:T(4,128)}, u32[]{:S(2)}) %copy-start.2) | copy-done | bytes 72
  2.3 82.7 %attend.1.rows_ref = bf16[256,2048]{1,0:T(8,128)(2,1)S(1)} custom-call(bf16[256,2048]{1,0:T(8,128)(2,1)S(1)} %copy-done.1, s32[4,3]{1,0:T(4,128)S(1)} %copy-done.2, bf16[2048,2048]{1,0:T(8,128)(2,1)} %wq_ref.1, bf16[2048,2048]{1,0:T(8,128)(2,1)} %wk_ref.1, bf16[2048,2048]{1,0:T(8,128)(2,1)} %wv_ref.1), custom_call_target="tpu_custom_call" | custom-call | tf_op jit(solution)/shard_map/attend/pallas_call | solution.py:439
  85.0 0.0 copy-done
  85.0 5.0 %project_out.1 = bf16[256,2048]{1,0:T(8,128)(2,1)} custom-call(bf16[256,2048]{1,0:T(8,128)(2,1)S(1)} %attend.1.rows_ref, bf16[2048,2048]{1,0:T(8,128)(2,1)S(1)} %copy-done), custom_call_target="tpu_custom_call" | custom-call | flops 2147483648 | bytes 10485760 | tf_op jit(solution)/shard_map/project_out/pallas_call | solution.py:424
Async XLA Ops:
  0.0 85.0 %copy-start = (bf16[2048,2048]{1,0:T(8,128)(2,1)S(1)}, bf16[2048,2048]{1,0:T(8,128)(2,1)}, u32[]{:S(2)}) copy-start(bf16[2048,2048]{1,0:T(8,128)(2,1)} %w_ref.1) | copy-start | bytes 25165828
  0.0 1.4 %copy-start.1 = (bf16[256,2048]{1,0:T(8,128)(2,1)S(1)}, bf16[256,2048]{1,0:T(8,128)(2,1)}, u32[]{:S(2)}) copy-start(bf16[256,2048]{1,0:T(8,128)(2,1)} %x_ref.1) | copy-start | bytes 3145732
  1.4 0.9 %copy-start.2 = (s32[4,3]{1,0:T(4,128)S(1)}, s32[4,3]{1,0:T(4,128)}, u32[]{:S(2)}) copy-start(s32[4,3]{1,0:T(4,128)} %rand_ref.1) | copy-start | bytes 148
